TPU v7x, 32 devices: a whole 2x2x4 slice. The times are simulated.
32 devices in a mesh: dp: 8 (over y, x, core), tensor: 4 (over z).
Axes of the slice: x: 2, y: 2, z: 4, core: 2. Of those that a mesh axis runs over, the one named last changes fastest.
Arguments:
- hidden_in: bfloat16 [8192, 2048], P(('dp', 'tensor')), may hold values from -6 to 6
- attn_gain: float32 [2048], replicated, may hold values from 0.5 to 1.5
- query_weight: bfloat16 [2048, 2048], P(None, 'tensor'), may hold values from -0.125 to 0.125
- key_weight: bfloat16 [2048, 2048], P(None, 'tensor'), may hold values from -0.125 to 0.125
- value_weight: bfloat16 [2048, 2048], P(None, 'tensor'), may hold values from -0.125 to 0.125
- output_weight: bfloat16 [2048, 2048], P('tensor'), may hold values from -0.75 to 0.75
- mlp_gain: float32 [2048], replicated, may hold values from 0.5 to 1.5
- gate_weight: bfloat16 [2048, 8192], P(None, 'tensor'), may hold values from -0.125 to 0.125
- up_weight: bfloat16 [2048, 8192], P(None, 'tensor'), may hold values from -0.125 to 0.125
- down_weight: bfloat16 [8192, 2048], P('tensor'), may hold values from -0.0625 to 0.0625
- segment_ids: int32 [8192], P('dp'), may hold values from 0 to 31, as said below
- positions: int32 [8192], P('dp'), may hold values from 0 to 1023, as said below
- out_cotangent: bfloat16 [8192, 2048], P(('dp', 'tensor')), may hold values from -6 to 6
Outputs:
- block_out: bfloat16 [8192, 2048], P(('dp', 'tensor'))
- input_grad: bfloat16 [8192, 2048], P(('dp', 'tensor'))
- attn_gain_grad: float32 [2048], P(('dp', 'tensor'))
- query_grad: float32 [2048, 2048], P('dp', 'tensor')
- key_grad: float32 [2048, 2048], P('dp', 'tensor')
- value_grad: float32 [2048, 2048], P('dp', 'tensor')
- output_grad: float32 [2048, 2048], P('tensor', 'dp')
- mlp_gain_grad: float32 [2048], P(('dp', 'tensor'))
- gate_grad: float32 [2048, 8192], P('dp', 'tensor')
- up_grad: float32 [2048, 8192], P('dp', 'tensor')
- down_grad: float32 [8192, 2048], P('tensor', 'dp')
Inputs may be any that keep to these rules, and one draw needn't show every extreme that they name: `segment_ids`: each aligned run of 1024 tokens is one packed sequence of one to four whole documents of 100 to 1024 tokens; ids never fall within it, and different sequences have different ids. `positions`: a token's offset from the first token of its document.
All inputs are finite; a program needn't handle non-finite values.
Results may differ from a plain program's by a relative error of at most 0.014.
Values may be sent and summed in bfloat16 or wider, within the bound.
A program may use at most 320 MiB of HBM per device.

v0:
```python
import jax
import jax.numpy as jnp
from jax import lax
from jax.sharding import PartitionSpec as P

HEAD_DIM = 64
LENGTH = 1024


EPS = 1e-05
THETA = 130000.0
NEG = -1e30


def rope_tables(positions):
    half = HEAD_DIM // 2
    freqs = THETA ** (-(jnp.arange(half, dtype=jnp.float32) * 2.0 / HEAD_DIM))
    angles = positions.astype(jnp.float32)[:, None] * freqs[None, :]
    return (jnp.cos(angles)[:, None, :], jnp.sin(angles)[:, None, :])


def rotate(values, cosine, sine):
    half = values.shape[-1] // 2
    first = values[..., :half]
    second = values[..., half:]
    return jnp.concatenate(
        [first * cosine - second * sine, second * cosine + first * sine], axis=-1
    )


def unrotate(values, cosine, sine):
    half = values.shape[-1] // 2
    first = values[..., :half]
    second = values[..., half:]
    return jnp.concatenate(
        [first * cosine + second * sine, second * cosine - first * sine], axis=-1
    )


def visible(segments):
    order = jnp.arange(segments.shape[0])
    return (segments[:, None] == segments[None, :]) & (order[None, :] <= order[:, None])


def contract_rows(left, right):
    return lax.dot_general(
        left, right, (((0,), (0,)), ((), ())), preferred_element_type=jnp.float32
    )


def contract_cols(left, right):
    return lax.dot_general(
        left, right, (((1,), (1,)), ((), ())), preferred_element_type=jnp.float32
    )


def norm_stats(values):
    inverse = lax.rsqrt(jnp.mean(values * values, axis=-1, keepdims=True) + EPS)
    return (values * inverse, inverse)


def norm_back(grad_normed, scaled, inverse, gain):
    upstream = grad_normed * gain
    grad_in = inverse * (upstream - scaled * jnp.mean(upstream * scaled, axis=-1, keepdims=True))
    return (grad_in, jnp.sum(grad_normed * scaled, axis=0))


def local(
    hidden_in,
    attn_gain,
    query_weight,
    key_weight,
    value_weight,
    output_weight,
    mlp_gain,
    gate_weight,
    up_weight,
    down_weight,
    segment_ids,
    positions,
    out_cotangent,
):
    rows_all = segment_ids.shape[0]
    seqs = rows_all // LENGTH
    heads_here = query_weight.shape[1] // HEAD_DIM
    scale = HEAD_DIM ** (-0.5)
    cosine, sine = rope_tables(positions)
    seg_blocks = segment_ids.reshape(seqs, LENGTH)

    def split_heads(values):
        return values.reshape(seqs, LENGTH, heads_here, HEAD_DIM)

    resid = hidden_in.astype(jnp.float32)
    scaled_one, inverse_one = norm_stats(resid)
    normed_one = (scaled_one * attn_gain).astype(jnp.bfloat16)
    full_one = lax.all_gather(normed_one, "tensor", axis=0, tiled=True)

    def project(weight):
        return jnp.dot(full_one, weight, preferred_element_type=jnp.float32).reshape(
            rows_all, heads_here, HEAD_DIM
        )

    queries = rotate(project(query_weight), cosine, sine).astype(jnp.bfloat16)
    keys = rotate(project(key_weight), cosine, sine).astype(jnp.bfloat16)
    values = project(value_weight).astype(jnp.bfloat16)

    def attend(block):
        query_block, key_block, value_block, segments = block
        scores = (
            jnp.einsum("qhd,khd->hqk", query_block, key_block, preferred_element_type=jnp.float32)
            * scale
        )
        scores = jnp.where(visible(segments)[None], scores, NEG)
        top = jnp.max(scores, axis=2, keepdims=True)
        expo = jnp.exp(scores - top)
        totals = jnp.sum(expo, axis=2, keepdims=True)
        weights = (expo / totals).astype(jnp.bfloat16)
        context_block = jnp.einsum(
            "hqk,khd->qhd", weights, value_block, preferred_element_type=jnp.float32
        )
        return (context_block.astype(jnp.bfloat16), (top + jnp.log(totals))[:, :, 0])

    context, log_totals = lax.map(
        attend, (split_heads(queries), split_heads(keys), split_heads(values), seg_blocks)
    )
    context = context.reshape(rows_all, heads_here * HEAD_DIM)
    mid = resid + lax.psum_scatter(
        jnp.dot(context, output_weight, preferred_element_type=jnp.float32),
        "tensor",
        scatter_dimension=0,
        tiled=True,
    )
    scaled_two, inverse_two = norm_stats(mid)
    normed_two = (scaled_two * mlp_gain).astype(jnp.bfloat16)
    full_two = lax.all_gather(normed_two, "tensor", axis=0, tiled=True)
    gate = jnp.dot(full_two, gate_weight, preferred_element_type=jnp.float32)
    upper = jnp.dot(full_two, up_weight, preferred_element_type=jnp.float32)
    sigmoid_gate = 1.0 / (1.0 + jnp.exp(-gate))
    hidden = (gate * sigmoid_gate * upper).astype(jnp.bfloat16)
    block_out = (
        mid
        + lax.psum_scatter(
            jnp.dot(hidden, down_weight, preferred_element_type=jnp.float32),
            "tensor",
            scatter_dimension=0,
            tiled=True,
        )
    ).astype(jnp.bfloat16)
    norm_one_all, norm_two_all = (full_one, full_two)
    grad_out = out_cotangent.astype(jnp.float32)
    full_grad = lax.all_gather(out_cotangent, "tensor", axis=0, tiled=True)
    grad_hidden = contract_cols(full_grad, down_weight)
    down_part = contract_rows(hidden, full_grad)
    slope = sigmoid_gate * (1.0 + gate * (1.0 - sigmoid_gate))
    grad_gate = (grad_hidden * upper * slope).astype(jnp.bfloat16)
    grad_upper = (grad_hidden * gate * sigmoid_gate).astype(jnp.bfloat16)
    gate_part = contract_rows(norm_two_all, grad_gate)
    up_part = contract_rows(norm_two_all, grad_upper)
    grad_normed_two = lax.psum_scatter(
        contract_cols(grad_gate, gate_weight) + contract_cols(grad_upper, up_weight),
        "tensor",
        scatter_dimension=0,
        tiled=True,
    )
    grad_mid_norm, gain_two_part = norm_back(grad_normed_two, scaled_two, inverse_two, mlp_gain)
    grad_mid = grad_out + grad_mid_norm
    full_branch = lax.all_gather(grad_mid.astype(jnp.bfloat16), "tensor", axis=0, tiled=True)
    output_part = contract_rows(context, full_branch)
    grad_context = contract_cols(full_branch, output_weight).astype(jnp.bfloat16)

    def attend_back(block):
        query_block, key_block, value_block, grad_block, log_block, segments = block
        scores = (
            jnp.einsum("qhd,khd->hqk", query_block, key_block, preferred_element_type=jnp.float32)
            * scale
        )
        scores = jnp.where(visible(segments)[None], scores, NEG)
        probs = jnp.exp(scores - log_block[:, :, None])
        value_part = jnp.einsum(
            "hqk,qhd->khd",
            probs.astype(jnp.bfloat16),
            grad_block,
            preferred_element_type=jnp.float32,
        )
        prob_grad = jnp.einsum(
            "qhd,khd->hqk", grad_block, value_block, preferred_element_type=jnp.float32
        )
        score_grad = (
            probs * (prob_grad - jnp.sum(probs * prob_grad, axis=2, keepdims=True))
        ).astype(jnp.bfloat16)
        query_part = (
            jnp.einsum("hqk,khd->qhd", score_grad, key_block, preferred_element_type=jnp.float32)
            * scale
        )
        key_part = (
            jnp.einsum("hqk,qhd->khd", score_grad, query_block, preferred_element_type=jnp.float32)
            * scale
        )
        return (query_part, key_part, value_part)

    grad_query, grad_key, grad_value = lax.map(
        attend_back,
        (
            split_heads(queries),
            split_heads(keys),
            split_heads(values),
            split_heads(grad_context),
            log_totals,
            seg_blocks,
        ),
    )
    merged = (rows_all, heads_here * HEAD_DIM)
    grad_query = (
        unrotate(grad_query.reshape(rows_all, heads_here, HEAD_DIM), cosine, sine)
        .astype(jnp.bfloat16)
        .reshape(merged)
    )
    grad_key = (
        unrotate(grad_key.reshape(rows_all, heads_here, HEAD_DIM), cosine, sine)
        .astype(jnp.bfloat16)
        .reshape(merged)
    )
    grad_value = grad_value.astype(jnp.bfloat16).reshape(merged)
    query_part_w = contract_rows(norm_one_all, grad_query)
    key_part_w = contract_rows(norm_one_all, grad_key)
    value_part_w = contract_rows(norm_one_all, grad_value)
    total_term = contract_cols(grad_query, query_weight)
    total_term = total_term + contract_cols(grad_key, key_weight)
    grad_normed_one = lax.psum_scatter(
        total_term + contract_cols(grad_value, value_weight),
        "tensor",
        scatter_dimension=0,
        tiled=True,
    )
    grad_in_norm, gain_one_part = norm_back(grad_normed_one, scaled_one, inverse_one, attn_gain)
    input_grad = (grad_mid + grad_in_norm).astype(jnp.bfloat16)
    query_sum, key_sum, value_sum, output_sum, gate_sum, up_sum, down_sum = (
        lax.psum_scatter(query_part_w, "dp", scatter_dimension=0, tiled=True),
        lax.psum_scatter(key_part_w, "dp", scatter_dimension=0, tiled=True),
        lax.psum_scatter(value_part_w, "dp", scatter_dimension=0, tiled=True),
        lax.psum_scatter(output_part, "dp", scatter_dimension=1, tiled=True),
        lax.psum_scatter(gate_part, "dp", scatter_dimension=0, tiled=True),
        lax.psum_scatter(up_part, "dp", scatter_dimension=0, tiled=True),
        lax.psum_scatter(down_part, "dp", scatter_dimension=1, tiled=True),
    )
    gain_one_sum, gain_two_sum = (
        lax.psum_scatter(gain_one_part, ("dp", "tensor"), scatter_dimension=0, tiled=True),
        lax.psum_scatter(gain_two_part, ("dp", "tensor"), scatter_dimension=0, tiled=True),
    )
    return (
        block_out,
        input_grad,
        gain_one_sum,
        query_sum,
        key_sum,
        value_sum,
        output_sum,
        gain_two_sum,
        gate_sum,
        up_sum,
        down_sum,
    )


def solution(mesh):
    in_specs = (
        P(("dp", "tensor"), None),
        P(),
        P(None, "tensor"),
        P(None, "tensor"),
        P(None, "tensor"),
        P("tensor", None),
        P(),
        P(None, "tensor"),
        P(None, "tensor"),
        P("tensor", None),
        P("dp"),
        P("dp"),
        P(("dp", "tensor"), None),
    )
    out_specs = (
        P(("dp", "tensor"), None),
        P(("dp", "tensor"), None),
        P(("dp", "tensor")),
        P("dp", "tensor"),
        P("dp", "tensor"),
        P("dp", "tensor"),
        P("tensor", "dp"),
        P(("dp", "tensor")),
        P("dp", "tensor"),
        P("dp", "tensor"),
        P("tensor", "dp"),
    )
    return jax.shard_map(local, mesh=mesh, in_specs=in_specs, out_specs=out_specs, check_vma=False)
```

profile of v0, /device:TPU:0, one launch (start us, length us, event | category | flops | bytes accessed | tf_op | source)
XLA Modules:
  0.0 1725.2 jit_solution(2969948165057329048)
XLA Ops:
  13.3 82.4 %all-gather.5.cloned.1.call-done = bf16[1024,2048]{1,0:T(8,128)(2,1)} async-done(((bf16[256,2048]{1,0:T(8,128)(2,1)}), bf16[1024,2048]{1,0:T(8,128)(2,1)}) %all-gather.5.cloned.1.call-update) | async-done | bytes 4194320 | tf_op jit(solution)/shard_map/all_gather | solution.py:96
  104.3 13.9 fusion.27
  118.2 13.2 fusion
  133.9 14.0 fusion.22
  154.6 143.2 %reduce-scatter.12.cloned.1.call-done = f32[256,2048]{1,0:T(8,128)} async-done(((f32[1024,2048]{1,0:T(8,128)}), f32[256,2048]{1,0:T(8,128)}) %reduce-scatter.12.cloned.1.call-update) | async-done | bytes 2097168 | tf_op jit(solution)/shard_map/reduce_scatter | solution.py:127
  303.0 80.9 %all-gather.7.cloned.1.call-done = bf16[1024,2048]{1,0:T(8,128)(2,1)} async-done(((bf16[256,2048]{1,0:T(8,128)(2,1)}), bf16[1024,2048]{1,0:T(8,128)(2,1)}) %all-gather.7.cloned.1.call-update) | async-done | bytes 4194320 | tf_op jit(solution)/shard_map/all_gather | solution.py:135
  383.8 15.9 fusion.32
  399.7 13.3 fusion.31
  413.1 51.4 %all-gather.9.cloned.1.call-done = bf16[1024,2048]{1,0:T(8,128)(2,1)} async-done(((bf16[256,2048]{1,0:T(8,128)(2,1)}), bf16[1024,2048]{1,0:T(8,128)(2,1)}) %all-gather.9.cloned.1.call-update) | async-done | bytes 4194320 | tf_op jit(solution)/shard_map/all_gather | solution.py:151
  464.5 21.7 %multiply_convert_fusion.1 = (bf16[1024,2048]{1,0:T(8,128)(2,1)}, bf16[1024,2048]{1,0:T(8,128)(2,1)}, bf16[1024,2048]{1,0:T(8,128)(2,1)}) fusion(f32[1024,2048]{1,0:T(8,128)} %fusion.31, f32[1024,2048]{1,0:T(8,128)} %fusion.32, bf16[1024,2048]{1,0:T(8,128)(2,1)} %all-gather.9.cloned.1.call-done, bf16[2048,2048]{1,0:T(8,128)(2,1)} %param.22), kind=kOutput, calls=%fused_computation.12 | convolution fusion | flops 8623489024 | bytes 41943040 | tf_op jit(solution)/shard_map/dot_general | solution.py:52
  486.3 12.9 fusion.34
  499.1 13.6 convolution_add_fusion
  512.8 143.2 %reduce-scatter.16.cloned.1.call-done = f32[256,2048]{1,0:T(8,128)} async-done(((f32[1024,2048]{1,0:T(8,128)}), f32[256,2048]{1,0:T(8,128)}) %reduce-scatter.16.cloned.1.call-update) | async-done | bytes 2097168 | tf_op jit(solution)/shard_map/reduce_scatter | solution.py:159
  661.4 81.4 %all-gather.11.cloned.1.call-done = bf16[1024,2048]{1,0:T(8,128)(2,1)} async-done(((bf16[256,2048]{1,0:T(8,128)(2,1)}), bf16[1024,2048]{1,0:T(8,128)(2,1)}) %all-gather.11.cloned.1.call-update) | async-done | bytes 4194320 | tf_op jit(solution)/shard_map/all_gather | solution.py:167
  747.4 14.4 fusion.19
  761.8 22.0 %multiply_reduce_fusion = (f32[8,1024]{1,0:T(8,128)S(1)}, f32[8,1024,1024]{1,2,0:T(8,128)}) fusion(f32[8,1024,1024]{1,2,0:T(8,128)} %get-tuple-element.90, f32[8,1024]{1,0:T(8,128)S(1)} %log_add_fusion, bf16[1024,8,64]{0,2,1:T(8,128)(2,1)S(1)} %bitcast.65, bf16[1024,8,64]{0,2,1:T(8,128)(2,1)S(1)} %bitcast.71), kind=kOutput, calls=%fused_computation.1 | convolution fusion | flops 1098899456 | bytes 69271552 | tf_op jit(solution)/shard_map/while/body/eval_jaxpr/qhd,khd->hqk/dot_general | solution.py:185
  783.8 28.5 %multiply_convert_fusion = bf16[8,1024,1024]{1,2,0:T(8,128)(2,1)} fusion(f32[8,1024,1024]{1,2,0:T(8,128)} %get-tuple-element.92, f32[8,1024,1024]{1,2,0:T(8,128)} %get-tuple-element.90, f32[8,1024]{1,0:T(8,128)S(1)} %get-tuple-element.91, f32[8,1024]{1,0:T(8,128)S(1)} %log_add_fusion), kind=kLoop, calls=%fused_computation | loop fusion | flops 33554432 | bytes 83951616 | tf_op jit(solution)/shard_map/while/body/eval_jaxpr/convert_element_type | solution.py:190
  812.3 11.4 multiply_bitcast_fusion
  845.1 14.6 fusion.33
  859.7 15.3 fusion.43
  875.1 15.6 fusion.42
  890.8 15.3 fusion.41
  933.7 54.5 %reduce-scatter.18.cloned.1.call-done = f32[256,2048]{1,0:T(8,128)} async-done(((f32[1024,2048]{1,0:T(8,128)}), f32[256,2048]{1,0:T(8,128)}) %reduce-scatter.18.cloned.1.call-update) | async-done | bytes 2097168 | tf_op jit(solution)/shard_map/reduce_scatter | solution.py:229
  990.5 46.3 %all-reduce.2 = (f32[2048]{0:T(1024)S(1)}, f32[2048]{0:T(1024)S(1)}) all-reduce(f32[2048]{0:T(1024)S(1)} %get-tuple-element.54, f32[2048]{0:T(1024)S(1)} %copy-done.26), channel_id=6, replica_groups=mesh['dp'=8,'tensor'=4] {'dp','tensor'}, use_global_device_ids=true, to_apply=%region_12.13.clone | all-reduce | flops 4096 | bytes 32768
  1038.0 98.8 %reduce-scatter.14.cloned.1.call-done = f32[256,2048]{1,0:T(8,128)} async-done(((f32[1024,2048]{1,0:T(8,128)}), f32[256,2048]{1,0:T(8,128)}) %reduce-scatter.14.cloned.1.call-update) | async-done | bytes 2097168 | tf_op jit(solution)/shard_map/reduce_scatter | solution.py:142
  1143.1 114.7 %reduce-scatter.32.cloned.1.call-done = f32[2048,256]{1,0:T(8,128)} async-done(((f32[2048,2048]{1,0:T(8,128)}), f32[2048,256]{1,0:T(8,128)}) %reduce-scatter.32.cloned.1.call-update) | async-done | bytes 2097168 | tf_op jit(solution)/shard_map/reduce_scatter | solution.py:244
  1257.7 120.2 %reduce-scatter.30.cloned.1.call-done = f32[256,2048]{1,0:T(8,128)} async-done(((f32[2048,2048]{1,0:T(8,128)}), f32[256,2048]{1,0:T(8,128)}) %reduce-scatter.30.cloned.1.call-update) | async-done | bytes 2097168 | tf_op jit(solution)/shard_map/reduce_scatter | solution.py:243
  1378.0 120.4 %reduce-scatter.28.cloned.1.call-done = f32[256,2048]{1,0:T(8,128)} async-done(((f32[2048,2048]{1,0:T(8,128)}), f32[256,2048]{1,0:T(8,128)}) %reduce-scatter.28.cloned.1.call-update) | async-done | bytes 2097168 | tf_op jit(solution)/shard_map/reduce_scatter | solution.py:242
  1498.3 54.9 %reduce-scatter.26.cloned.1.call-done = f32[512,256]{1,0:T(8,128)} async-done(((f32[512,2048]{1,0:T(8,128)}), f32[512,256]{1,0:T(8,128)}) %reduce-scatter.26.cloned.1.call-update) | async-done | bytes 524304 | tf_op jit(solution)/shard_map/reduce_scatter | solution.py:241
  1553.2 55.1 %reduce-scatter.24.cloned.1.call-done = f32[256,512]{1,0:T(8,128)} async-done(((f32[2048,512]{1,0:T(8,128)}), f32[256,512]{1,0:T(8,128)}) %reduce-scatter.24.cloned.1.call-update) | async-done | bytes 524304 | tf_op jit(solution)/shard_map/reduce_scatter | solution.py:240
  1608.3 55.0 %reduce-scatter.20.cloned.1.call-done = f32[256,512]{1,0:T(8,128)} async-done(((f32[2048,512]{1,0:T(8,128)}), f32[256,512]{1,0:T(8,128)}) %reduce-scatter.20.cloned.1.call-update) | async-done | bytes 524304 | tf_op jit(solution)/shard_map/reduce_scatter | solution.py:238
  1663.3 55.0 %reduce-scatter.22.cloned.1.call-done = f32[256,512]{1,0:T(8,128)} async-done(((f32[2048,512]{1,0:T(8,128)}), f32[256,512]{1,0:T(8,128)}) %reduce-scatter.22.cloned.1.call-update) | async-done | bytes 524304 | tf_op jit(solution)/shard_map/reduce_scatter | solution.py:239
  (149 shorter events, 97.3 us)
Async XLA Ops:
  7.2 141.7 %copy-start = (bf16[512,2048]{1,0:T(8,128)(2,1)S(1)}, bf16[512,2048]{1,0:T(8,128)(2,1)}, u32[]{:S(2)}) copy-start(bf16[512,2048]{1,0:T(8,128)(2,1)} %param.18) | copy-start | bytes 6291460
  7.2 88.4 %all-gather.5.cloned.1.call-start = ((), (), s32[]{:S(2)}) async-start(), calls=%async_computation.11 | async-start | bytes 5242880 | tf_op jit(solution)/shard_map/all_gather | solution.py:96
  12.0 285.8 %reduce-scatter.12.cloned.1.call-start = ((), (), s32[]{:S(2)}) async-start(), calls=%async_computation.12 | async-start | bytes 10485760 | tf_op jit(solution)/shard_map/reduce_scatter | solution.py:127
  12.7 90.8 %copy-start.17 = (f32[1024,32]{0,1:T(8,128)}, f32[1024,32]{0,1:T(8,128)S(1)}, u32[]{:S(2)}) copy-start(f32[1024,32]{0,1:T(8,128)S(1)} %get-tuple-element.87) | copy-start | bytes 393220
  12.7 90.8 %copy-start.19 = (f32[1024,32]{0,1:T(8,128)}, f32[1024,32]{0,1:T(8,128)S(1)}, u32[]{:S(2)}) copy-start(f32[1024,32]{0,1:T(8,128)S(1)} %get-tuple-element.88) | copy-start | bytes 393220
  154.5 143.3 %copy-start.4 = (bf16[256,2048]{1,0:T(8,128)(2,1)S(1)}, bf16[256,2048]{1,0:T(8,128)(2,1)}, u32[]{:S(2)}) copy-start(bf16[256,2048]{1,0:T(8,128)(2,1)} %param.13) | copy-start | bytes 3145732
  154.5 146.6 %copy-start.23 = (f32[2048]{0:T(1024)S(1)}, f32[2048]{0:T(1024)}, u32[]{:S(2)}) copy-start(f32[2048]{0:T(1024)} %param.19) | copy-start | bytes 24580
  154.5 229.3 %all-gather.7.cloned.1.call-start = ((), (), s32[]{:S(2)}) async-start(), calls=%async_computation.13 | async-start | bytes 5242880 | tf_op jit(solution)/shard_map/all_gather | solution.py:135
  299.8 359.8 %copy-start.27 = (f32[256]{0:T(256)}, f32[256]{0:T(256)S(1)}, u32[]{:S(2)}) copy-start(f32[256]{0:T(256)S(1)} %add_rsqrt_fusion) | copy-start | bytes 3076
  302.3 162.2 %all-gather.9.cloned.1.call-start = ((), (), s32[]{:S(2)}) async-start(), calls=%async_computation.15 | async-start | bytes 5242880 | tf_op jit(solution)/shard_map/all_gather | solution.py:151
  302.9 353.1 %reduce-scatter.16.cloned.1.call-start = ((), (), s32[]{:S(2)}) async-start(), calls=%async_computation.16 | async-start | bytes 10485760 | tf_op jit(solution)/shard_map/reduce_scatter | solution.py:159
  383.8 15.9 copy-start.36
  512.8 146.8 %copy-start.7 = (bf16[256,2048]{1,0:T(8,128)(2,1)S(1)}, bf16[256,2048]{1,0:T(8,128)(2,1)}, u32[]{:S(2)}) copy-start(bf16[256,2048]{1,0:T(8,128)(2,1)} %param.25) | copy-start | bytes 3145732
  512.8 230.0 %all-gather.11.cloned.1.call-start = ((), (), s32[]{:S(2)}) async-start(), calls=%async_computation.17 | async-start | bytes 5242880 | tf_op jit(solution)/shard_map/all_gather | solution.py:167
  661.3 327.0 %reduce-scatter.18.cloned.1.call-start = ((), (), s32[]{:S(2)}) async-start(), calls=%async_computation.18 | async-start | bytes 10485760 | tf_op jit(solution)/shard_map/reduce_scatter | solution.py:229
  747.4 14.4 copy-start.22
  845.0 291.8 %reduce-scatter.14.cloned.1.call-start = ((), (), s32[]{:S(2)}) async-start(), calls=%async_computation.14 | async-start | bytes 10485760 | tf_op jit(solution)/shard_map/reduce_scatter | solution.py:142
  859.7 398.1 %reduce-scatter.32.cloned.1.call-start = ((), (), s32[]{:S(2)}) async-start(), calls=%async_computation.25 | async-start | bytes 18874368 | tf_op jit(solution)/shard_map/reduce_scatter | solution.py:244
  875.1 502.9 %reduce-scatter.30.cloned.1.call-start = ((), (), s32[]{:S(2)}) async-start(), calls=%async_computation.24 | async-start | bytes 18874368 | tf_op jit(solution)/shard_map/reduce_scatter | solution.py:243
  890.7 607.6 %reduce-scatter.28.cloned.1.call-start = ((), (), s32[]{:S(2)}) async-start(), calls=%async_computation.23 | async-start | bytes 18874368 | tf_op jit(solution)/shard_map/reduce_scatter | solution.py:242
  906.1 647.1 %reduce-scatter.26.cloned.1.call-start = ((), (), s32[]{:S(2)}) async-start(), calls=%async_computation.22 | async-start | bytes 4718592 | tf_op jit(solution)/shard_map/reduce_scatter | solution.py:241
  913.0 695.3 %reduce-scatter.24.cloned.1.call-start = ((), (), s32[]{:S(2)}) async-start(), calls=%async_computation.21 | async-start | bytes 4718592 | tf_op jit(solution)/shard_map/reduce_scatter | solution.py:240
  920.1 743.2 %reduce-scatter.20.cloned.1.call-start = ((), (), s32[]{:S(2)}) async-start(), calls=%async_computation.19 | async-start | bytes 4718592 | tf_op jit(solution)/shard_map/reduce_scatter | solution.py:238
  927.0 791.3 %reduce-scatter.22.cloned.1.call-start = ((), (), s32[]{:S(2)}) async-start(), calls=%async_computation.20 | async-start | bytes 4718592 | tf_op jit(solution)/shard_map/reduce_scatter | solution.py:239
  933.7 54.6 %copy-start.5 = (bf16[256,2048]{1,0:T(8,128)(2,1)S(1)}, bf16[256,2048]{1,0:T(8,128)(2,1)}, u32[]{:S(2)}) copy-start(bf16[256,2048]{1,0:T(8,128)(2,1)} %param.13) | copy-start | bytes 3145732
  933.7 54.6 %copy-start.25 = (f32[2048]{0:T(1024)S(1)}, f32[2048]{0:T(1024)}, u32[]{:S(2)}) copy-start(f32[2048]{0:T(1024)} %param.14) | copy-start | bytes 24580
  933.7 54.6 %copy-start.31 = (f32[256]{0:T(256)S(1)}, f32[256]{0:T(256)}, u32[]{:S(2)}) copy-start(f32[256]{0:T(256)} %copy-done.30) | copy-start | bytes 3076
  933.7 56.9 %copy-start.26 = (f32[2048]{0:T(1024)S(1)}, f32[2048]{0:T(1024)}, u32[]{:S(2)}) copy-start(f32[2048]{0:T(1024)} %get-tuple-element.52) | copy-start | bytes 24580
  933.7 203.2 %copy-start.24 = (f32[2048]{0:T(1024)S(1)}, f32[2048]{0:T(1024)}, u32[]{:S(2)}) copy-start(f32[2048]{0:T(1024)} %param.19) | copy-start | bytes 24580
  933.7 203.2 %copy-start.28 = (f32[256]{0:T(256)S(1)}, f32[256]{0:T(256)}, u32[]{:S(2)}) copy-start(f32[256]{0:T(256)} %copy-done.27) | copy-start | bytes 3076
  933.7 203.2 %copy-start.33 = (f32[256]{0:T(256)S(1)}, f32[256]{0:T(256)}, u32[]{:S(2)}) copy-start(f32[256]{0:T(256)} %copy-done.32) | copy-start | bytes 3076
  1038.0 680.2 %copy-start.1 = (bf16[512,2048]{1,0:T(8,128)(2,1)S(1)}, bf16[512,2048]{1,0:T(8,128)(2,1)}, u32[]{:S(2)}) copy-start(bf16[512,2048]{1,0:T(8,128)(2,1)} %param.18) | copy-start | bytes 6291460
  (25 other events, 178.0 us)
Sparse Core Ops, SparseCore 0:
  12.1 83.4 all-gather.4
  154.7 143.0 reduce-scatter.11
  302.5 81.3 all-gather.6
  385.3 79.2 all-gather.8
  512.9 143.0 reduce-scatter.15
  661.4 81.3 all-gather.10
  845.1 143.0 reduce-scatter.17
  990.6 146.1 reduce-scatter.13
  1141.0 116.7 reduce-scatter.31
  1261.7 116.1 reduce-scatter.29
  1382.1 116.1 reduce-scatter.27
  1502.1 51.0 reduce-scatter.25
  1557.2 51.1 reduce-scatter.23
  1612.1 51.1 reduce-scatter.19
  1667.1 51.1 reduce-scatter.21
where the time goes:
time: 1730 us
  waiting for transfers between devices  1310 us (76%)
  matrix products  281 us (16%)
  other arithmetic  65.4 us (4%)
  blocking collectives  46.3 us (3%)
    reduce_scatter x1, waiting for transfers between devices, local(): lax.psum_scatter(contract_cols(grad_gate, gate_weight) + contract_cols(gr...  143 us
    reduce_scatter x1, waiting for transfers between devices, local(): lax.psum_scatter(jnp.dot(context, output_weight, preferred_element_type=j...  143 us
    reduce_scatter x1, waiting for transfers between devices, local(): lax.psum_scatter(gate_part, 'dp', scatter_dimension=0, tiled=True)  120 us
    reduce_scatter x1, waiting for transfers between devices, local(): lax.psum_scatter(up_part, 'dp', scatter_dimension=0, tiled=True)  120 us
    reduce_scatter x1, waiting for transfers between devices, local(): lax.psum_scatter(down_part, 'dp', scatter_dimension=1, tiled=True)  115 us
    reduce_scatter x1, waiting for transfers between devices, local(): lax.psum_scatter(jnp.dot(hidden, down_weight, preferred_element_type=jnp....  98.8 us
    all_gather x1, waiting for transfers between devices, local(): full_one = lax.all_gather(normed_one, 'tensor', axis=0, tiled=True)  82.4 us
    all_gather x1, waiting for transfers between devices, local(): lax.all_gather(grad_mid.astype(jnp.bfloat16), 'tensor', axis=0, tiled=True)  81.4 us
  transfers between devices with their start and end apart: 15, of which 15 were waited for; matrix products, arithmetic and copies ran while one was open for 7% of the time, Pallas kernels for 0%

commit v1 on v0

v1 whole, which is shorter than its diff:
```python
import functools

import jax
import jax.numpy as jnp
from jax import lax
from jax.experimental import pallas as pl
from jax.experimental.pallas import tpu as pltpu
from jax.sharding import PartitionSpec as P

HEAD_DIM = 64
LENGTH = 1024
EPS = 1e-05
THETA = 130000.0
NEG = -1e30
BF = jnp.bfloat16
F32 = jnp.float32
MESH = pl.DeviceIdType.MESH
HBM = pl.BlockSpec(memory_space=pl.ANY)
VM = pl.BlockSpec(memory_space=pltpu.VMEM)
DMA = pltpu.SemaphoreType.DMA
ZAXIS = "tensor"
VMEM_MAX = 66_000_000


def dot_nn(left, right):
    return jnp.dot(left, right, preferred_element_type=F32)


def dot_nt(left, right):
    return lax.dot_general(left, right, (((1,), (1,)), ((), ())), preferred_element_type=F32)


def dot_tn(left, right):
    return lax.dot_general(left, right, (((0,), (0,)), ((), ())), preferred_element_type=F32)


def norm_stats(values):
    inverse = lax.rsqrt(jnp.mean(values * values, axis=-1, keepdims=True) + EPS)
    return (values * inverse, inverse)


def norm_back(grad_normed, scaled, inverse, gain):
    upstream = grad_normed * gain
    grad_in = inverse * (upstream - scaled * jnp.mean(upstream * scaled, axis=-1, keepdims=True))
    return (grad_in, jnp.sum(grad_normed * scaled, axis=0))


def inside(value, size):
    return (value >= 0) & (value < size)


def greet_line(t, n, partner=None):
    barrier = pltpu.get_barrier_semaphore()
    if partner is not None:
        pl.semaphore_signal(barrier, inc=1, device_id={"dp": partner}, device_id_type=MESH)

    @pl.when(t < n - 1)
    def _():
        pl.semaphore_signal(barrier, inc=1, device_id={ZAXIS: t + 1}, device_id_type=MESH)

    @pl.when(t > 0)
    def _():
        pl.semaphore_signal(barrier, inc=1, device_id={ZAXIS: t - 1}, device_id_type=MESH)

    others = 0 if partner is None else 1
    pl.semaphore_wait(barrier, others + (t > 0).astype(jnp.int32) + (t < n - 1).astype(jnp.int32))


class LineGather:
    def __init__(self, t, n, rows, buf, send_sem, recv_sem):
        self.t, self.n, self.rows = t, n, rows
        self.buf, self.send_sem, self.recv_sem = buf, send_sem, recv_sem

    def slot(self, shard):
        shard = jnp.clip(shard, 0, self.n - 1)
        return self.buf.at[pl.ds(pl.multiple_of(shard * self.rows, self.rows), self.rows)]

    def sent(self, s, d):
        return self.t - s + 2 * s * d

    def got(self, s, d):
        return self.t - 1 - s + 2 * d * (1 + s)

    def send_ok(self, s, d):
        return (s < self.n - 1) & inside(self.sent(s, d), self.n) & inside(self.t + 1 - 2 * d, self.n)

    def recv_ok(self, s, d):
        return (s < self.n - 1) & inside(self.got(s, d), self.n)

    def _copy(self, shard, s, d, peer):
        s = jnp.minimum(s, self.n - 2)
        return pltpu.make_async_remote_copy(
            src_ref=self.slot(shard),
            dst_ref=self.slot(shard),
            send_sem=self.send_sem.at[d, s],
            recv_sem=self.recv_sem.at[d, s],
            device_id={ZAXIS: jnp.clip(peer, 0, self.n - 1)},
            device_id_type=MESH,
        )

    def start(self, s, d):
        @pl.when(self.send_ok(s, d))
        def _():
            self._copy(self.sent(s, d), s, d, self.t + 1 - 2 * d).start()

    def take(self, s, d):
        @pl.when(self.recv_ok(s, d))
        def _():
            self._copy(self.got(s, d), s, d, self.t + 1 - 2 * d).wait_recv()
            self.start(s + 1, d)

    def finish(self):
        for s in range(self.n - 1):
            for d in range(2):

                @pl.when(self.send_ok(s, d))
                def _():
                    self._copy(self.sent(s, d), s, d, self.t + 1 - 2 * d).wait_send()


class LineScatter:
    def __init__(self, t, n, part, recv, send_sem, recv_sem):
        self.t, self.n, self.part, self.recv = t, n, part, recv
        self.send_sem, self.recv_sem = send_sem, recv_sem

    def owner(self, s, d):
        return s if d == 1 else self.n - 1 - s

    def slot(self, s, d):
        s = jnp.clip(s, 0, self.n - 1)
        return self.n - s if d == 1 else s

    def _copy(self, src, s, d):
        return pltpu.make_async_remote_copy(
            src_ref=src,
            dst_ref=self.recv.at[self.slot(s, d)],
            send_sem=self.send_sem.at[d, jnp.clip(s, 0, self.n - 2)],
            recv_sem=self.recv_sem.at[d, jnp.clip(s, 0, self.n - 2)],
            device_id={ZAXIS: jnp.clip(self.t + 1 - 2 * d, 0, self.n - 1)},
            device_id_type=MESH,
        )

    def first(self, s, d):
        self._copy(self.part.at[self.owner(s, d)], s, d).start()

    def step(self, tau):
        t, n = self.t, self.n
        for d in range(2):
            s = tau - t if d == 0 else tau - (n - 1 - t)
            has = (t > 0) if d == 0 else (t < n - 1)

            @pl.when(has & (s >= 0))
            def _():
                at = self.slot(s, d)
                self._copy(self.recv.at[at], s, d).wait_recv()
                owner = self.owner(s, d)

                @pl.when(owner != t)
                def _():
                    both = self.recv[at].astype(F32) + self.part[owner].astype(F32)
                    self.recv[at] = both.astype(BF)
                    self._copy(self.recv.at[at], s, d).start()

    def emit(self, out, sem):
        t, n = self.t, self.n
        own = pltpu.make_async_copy(self.part.at[t], out.at[0], sem.at[0])
        left = pltpu.make_async_copy(self.recv.at[self.slot(n - 1 - t, 0)], out.at[1], sem.at[1])
        right = pltpu.make_async_copy(self.recv.at[self.slot(t, 1)], out.at[2], sem.at[2])
        own.start()

        @pl.when(t > 0)
        def _():
            left.start()

        @pl.when(t < n - 1)
        def _():
            right.start()

        own.wait()

        @pl.when(t > 0)
        def _():
            left.wait()

        @pl.when(t < n - 1)
        def _():
            right.wait()

    def finish(self):
        t, n = self.t, self.n
        for s in range(n - 1):
            for d in range(2):
                sends = (n - 1 - s > t) if d == 0 else (s < t)

                @pl.when(sends)
                def _():
                    self._copy(self.recv.at[self.slot(s, d)], s, d).wait_send()


def line_total(parts, n):
    t = lax.axis_index(ZAXIS)
    own, left, right = (parts[i].astype(F32) for i in range(3))
    return own + jnp.where(t > 0, left, 0.0) + jnp.where(t < n - 1, right, 0.0)


def qkv_kernel(n, n1_ref, wq, wk, wv, cos_ref, sin_ref, full_ref, qkv_ref, buf, own_sem, out_sem, send_sem, recv_sem):
    t = lax.axis_index(ZAXIS)
    rows = n1_ref.shape[0]
    width = wq.shape[1]
    half = HEAD_DIM // 2
    line = LineGather(t, n, rows, buf, send_sem, recv_sem)
    own = pltpu.make_async_copy(n1_ref, line.slot(t), own_sem)
    own.start()
    greet_line(t, n)
    own.wait()
    line.start(0, 0)
    line.start(0, 1)

    def keep(shard):
        place = pl.ds(pl.multiple_of(shard * rows, rows), rows)
        return pltpu.make_async_copy(buf.at[place], full_ref.at[place], out_sem.at[shard])

    def project(shard):
        place = pl.ds(pl.multiple_of(shard * rows, rows), rows)
        normed = buf[place, :]
        cosine, sine = cos_ref[:, place], sin_ref[:, place]
        for index, weight in enumerate((wq, wk, wv)):
            turned = dot_nn(normed, weight[...]).T
            base = index * width
            if index == 2:
                qkv_ref[base : base + width, place] = turned.astype(BF)
                continue
            factor = HEAD_DIM ** (-0.5) if index == 0 else 1.0
            for low in range(0, width, HEAD_DIM):
                first, second = turned[low : low + half], turned[low + half : low + HEAD_DIM]
                qkv_ref[base + low : base + low + half, place] = (
                    (first * cosine - second * sine) * factor
                ).astype(BF)
                qkv_ref[base + low + half : base + low + HEAD_DIM, place] = (
                    (second * cosine + first * sine) * factor
                ).astype(BF)

    def event(e, carry):
        es = jnp.maximum(e - 1, 0)
        s, d = es // 2, es % 2
        shard = jnp.where(e == 0, t, line.got(s, d))

        @pl.when(inside(shard, n))
        def _():
            @pl.when(e > 0)
            def _():
                line.take(s, d)

            keep(shard).start()
            project(shard)

        return carry

    lax.fori_loop(0, 2 * n - 1, event, 0)
    line.finish()
    for shard in range(n):
        keep(shard).wait()


def gather_qkv(n, n1, wq, wk, wv, cosine, sine):
    rows, depth = n1.shape
    width = wq.shape[1]
    return pl.pallas_call(
        functools.partial(qkv_kernel, n),
        out_shape=[
            jax.ShapeDtypeStruct((n * rows, depth), BF),
            jax.ShapeDtypeStruct((3 * width, n * rows), BF),
        ],
        in_specs=[VM] * 6,
        out_specs=[HBM, VM],
        scratch_shapes=[
            pltpu.VMEM((n * rows, depth), BF),
            DMA,
            DMA((n,)),
            DMA((2, n - 1)),
            DMA((2, n - 1)),
        ],
        compiler_params=pltpu.CompilerParams(collective_id=0, has_side_effects=True, vmem_limit_bytes=VMEM_MAX),
        name="gather_qkv",
    )(n1, wq, wk, wv, cosine, sine)


def masked(scores, seg_col, seg_row, start):
    scores = jnp.where(seg_col == seg_row, scores, NEG)
    corner = scores[start:]
    key_at = lax.broadcasted_iota(jnp.int32, corner.shape, 0)
    query_at = lax.broadcasted_iota(jnp.int32, corner.shape, 1)
    corner = jnp.where(key_at <= query_at, corner, NEG)
    return jnp.concatenate([scores[:start], corner], axis=0) if start else corner


def attend_kernel(block, q_ref, k_ref, v_ref, seg_row, seg_col, ctx_ref, lse_ref):
    keys, values = k_ref[...], v_ref[...]
    column = seg_col[...]
    for start in range(0, q_ref.shape[1], block):
        end = start + block
        scores = masked(dot_tn(keys[:, :end], q_ref[:, start:end]), column[:end], seg_row[:, start:end], start)
        top = jnp.max(scores, axis=0, keepdims=True)
        expo = jnp.exp(scores - top)
        total = jnp.sum(expo, axis=0, keepdims=True)
        weights = (expo * (1.0 / total)).astype(BF)
        ctx_ref[:, start:end] = dot_nn(values[:, :end], weights).astype(BF)
        lse_ref[0, :, start:end] = top + jnp.log(total)


def attend(qkv, seg_row, seg_col):
    heads, length = qkv.shape[0] // (3 * HEAD_DIM), qkv.shape[1]
    part = lambda o: pl.BlockSpec((HEAD_DIM, length), lambda h: (h + o * heads, 0))
    whole = lambda *shape: pl.BlockSpec(shape, lambda h: (0,) * len(shape))
    return pl.pallas_call(
        functools.partial(attend_kernel, 512),
        grid=(heads,),
        in_specs=[part(0), part(1), part(2), whole(1, length), whole(length, 1)],
        out_specs=[part(0), pl.BlockSpec((1, 1, length), lambda h: (h, 0, 0))],
        out_shape=[
            jax.ShapeDtypeStruct((heads * HEAD_DIM, length), BF),
            jax.ShapeDtypeStruct((heads, 1, length), F32),
        ],
        compiler_params=pltpu.CompilerParams(vmem_limit_bytes=48 << 20),
        name="attend",
    )(qkv, qkv, qkv, seg_row, seg_col)


def turn_back(values, cosine, sine):
    half = HEAD_DIM // 2
    first, second = values[:half], values[half:]
    return jnp.concatenate([first * cosine + second * sine, second * cosine - first * sine], axis=0)


def attend_back_kernel(
    block, q_ref, k_ref, v_ref, g_ref, lse_ref, seg_row, seg_col, cos_ref, sin_ref, dq_ref, dk_ref, dv_ref, dk_sum, dv_sum
):
    keys, values = k_ref[...], v_ref[...]
    column = seg_col[...]
    for start in range(0, q_ref.shape[1], block):
        end = start + block
        here = slice(start, end)
        queries, grads = q_ref[:, here], g_ref[:, here]
        scores = masked(dot_tn(keys[:, :end], queries), column[:end], seg_row[:, here], start)
        probs = jnp.exp(scores - lse_ref[0, :, here])
        prob_grad = dot_tn(values[:, :end], grads)
        inner = jnp.sum(probs * prob_grad, axis=0, keepdims=True)
        score_grad = (probs * (prob_grad - inner)).astype(BF)
        dq = dot_nn(keys[:, :end], score_grad) * HEAD_DIM ** (-0.5)
        dq_ref[:, here] = turn_back(dq, cos_ref[:, here], sin_ref[:, here]).astype(BF)
        dv = dot_nt(grads, probs.astype(BF))
        dk = dot_nt(queries, score_grad)
        if start:
            dv_sum[:, :start] += dv[:, :start]
            dk_sum[:, :start] += dk[:, :start]
        dv_sum[:, here] = dv[:, start:]
        dk_sum[:, here] = dk[:, start:]
    dk_ref[...] = turn_back(dk_sum[...], cos_ref[...], sin_ref[...]).astype(BF)
    dv_ref[...] = dv_sum[...].astype(BF)


def attend_back(qkv, grads, lse, seg_row, seg_col, cosine, sine):
    heads, length = qkv.shape[0] // (3 * HEAD_DIM), qkv.shape[1]
    part = lambda o: pl.BlockSpec((HEAD_DIM, length), lambda h: (h + o * heads, 0))
    whole = lambda *shape: pl.BlockSpec(shape, lambda h: (0,) * len(shape))
    return pl.pallas_call(
        functools.partial(attend_back_kernel, 256),
        grid=(heads,),
        in_specs=[
            part(0),
            part(1),
            part(2),
            part(0),
            pl.BlockSpec((1, 1, length), lambda h: (h, 0, 0)),
            whole(1, length),
            whole(length, 1),
            whole(HEAD_DIM // 2, length),
            whole(HEAD_DIM // 2, length),
        ],
        out_specs=[part(0)] * 3,
        out_shape=[jax.ShapeDtypeStruct((heads * HEAD_DIM, length), BF)] * 3,
        scratch_shapes=[pltpu.VMEM((HEAD_DIM, length), F32)] * 2,
        compiler_params=pltpu.CompilerParams(vmem_limit_bytes=48 << 20),
        name="attend_back",
    )(qkv, qkv, qkv, grads, lse, seg_row, seg_col, cosine, sine)


def swap_kernel(n, forward, x_ref, o_ref, own_sem, send_sem, recv_sem):
    t = lax.axis_index(ZAXIS)
    rows = x_ref.shape[0] if forward else x_ref.shape[0] // n
    cols = x_ref.shape[1] // n if forward else x_ref.shape[1]
    row = lambda i: pl.ds(pl.multiple_of(i * rows, rows), rows)
    col = lambda i: pl.ds(pl.multiple_of(i * cols, cols), cols)
    source = lambda i: x_ref.at[:, col(i)] if forward else x_ref.at[row(i), :]
    target = o_ref.at[row(t), :] if forward else o_ref.at[:, col(t)]
    barrier = pltpu.get_barrier_semaphore()
    for s in range(1, n):
        pl.semaphore_signal(barrier, inc=1, device_id={ZAXIS: lax.rem(t + s, n)}, device_id_type=MESH)
    pl.semaphore_wait(barrier, n - 1)
    copies = []
    for s in range(1, n):
        peer = lax.rem(t + s, n)
        copies.append(
            pltpu.make_async_remote_copy(
                src_ref=source(peer),
                dst_ref=target,
                send_sem=send_sem.at[s - 1],
                recv_sem=recv_sem.at[s - 1],
                device_id={ZAXIS: peer},
                device_id_type=MESH,
            )
        )
        copies[-1].start()
    own = pltpu.make_async_copy(source(t), target, own_sem)
    own.start()
    for copy in copies:
        copy.wait()
    own.wait()


def swap(n, x, forward):
    rows, cols = x.shape
    shape = (rows * n, cols // n) if forward else (rows // n, cols * n)
    return pl.pallas_call(
        functools.partial(swap_kernel, n, forward),
        out_shape=jax.ShapeDtypeStruct(shape, x.dtype),
        in_specs=[VM],
        out_specs=VM,
        scratch_shapes=[DMA, DMA((n - 1,)), DMA((n - 1,))],
        compiler_params=pltpu.CompilerParams(
            collective_id=1 if forward else 2, has_side_effects=True, vmem_limit_bytes=32 << 20
        ),
        name="swap_out" if forward else "swap_back",
    )(x)


def mlp_kernel(
    m,
    n,
    n2_ref,
    cot_ref,
    wg_ref,
    wu_ref,
    wd_ref,
    out_ref,
    dn2_ref,
    grads_ref,
    n2,
    cot,
    wg,
    wu,
    wd,
    hid,
    dgate,
    dup,
    obuf,
    part,
    recv,
    turned,
    spare,
    load_sem,
    out_sem,
    grad_sem,
    ag_send,
    ag_recv,
    rs_send,
    rs_recv,
    core_send,
    core_recv,
    sum_sem,
    ready,
):
    t = lax.axis_index(ZAXIS)
    index = lax.axis_index("dp")
    core = index % 2
    partner = index + 1 - 2 * core
    rows, depth = n2_ref.shape
    units = wg.shape[1]
    strip = depth // m
    wide = min(512, units)
    line = LineGather(t, n, rows, n2, ag_send, ag_recv)
    ring = LineScatter(t, n, part, recv, rs_send, rs_recv)
    loads = [
        pltpu.make_async_copy(n2_ref, line.slot(t), load_sem.at[0]),
        pltpu.make_async_copy(wg_ref, wg, load_sem.at[1]),
        pltpu.make_async_copy(wu_ref, wu, load_sem.at[2]),
        pltpu.make_async_copy(cot_ref, cot, load_sem.at[3]),
        pltpu.make_async_copy(wd_ref, wd, load_sem.at[4]),
    ]
    for load in loads:
        load.start()
    greet_line(t, n, partner)
    loads[0].wait()
    line.start(0, 0)
    line.start(0, 1)
    for load in loads[1:]:
        load.wait()

    def place(shard):
        return pl.ds(pl.multiple_of(shard * rows, rows), rows)

    def flush(shard):
        return pltpu.make_async_copy(obuf, out_ref.at[place(shard)], out_sem)

    def up_half(shard):
        at = place(shard)

        def body(i, carry):
            cols = pl.ds(pl.multiple_of(i * wide, wide), wide)
            gate = dot_nn(n2[at, :], wg[:, cols])
            upper = dot_nn(n2[at, :], wu[:, cols])
            dh = dot_nt(cot[at, :], wd[cols, :])
            sg = 1.0 / (1.0 + jnp.exp(-gate))
            gs = gate * sg
            hid[at, cols] = (gs * upper).astype(BF)
            dup[at, cols] = (dh * gs).astype(BF)
            dgate[at, cols] = (dh * upper * (sg * (1.0 + gate * (1.0 - sg)))).astype(BF)
            return carry

        lax.fori_loop(0, units // wide, body, 0)

    def down_half(shard, first):
        at = place(shard)

        @pl.when(jnp.logical_not(first))
        def _():
            flush(shard).wait()

        def body(i, carry):
            cols = pl.ds(pl.multiple_of(i * 512, 512), 512)
            obuf[:, cols] = dot_nn(hid[at, :], wd[:, cols]).astype(BF)
            part[shard, :, cols] = (dot_nt(dgate[at, :], wg[cols, :]) + dot_nt(dup[at, :], wu[cols, :])).astype(BF)
            return carry

        lax.fori_loop(0, depth // 512, body, 0)
        flush(shard).start()

    def event(e, carry):
        es = jnp.maximum(e - 1, 0)
        s, d = es // 2, es % 2
        shard = jnp.where(e == 0, t, line.got(s, d))
        two = inside(line.got(s, 0), n) & inside(line.got(s, 1), n)
        valid = inside(shard, n)

        @pl.when(valid)
        def _():
            up_half(shard)

        @pl.when((e > 0) & (d == 1) & two)
        def _():
            line.take(s + 1, 0)
            line.take(s + 1, 1)

        @pl.when(valid)
        def _():
            down_half(shard, e == 0)

        @pl.when(e == 0)
        def _():
            line.take(0, 0)
            line.take(0, 1)

        @pl.when((e > 0) & (d == 1) & jnp.logical_not(two))
        def _():
            line.take(s + 1, 0)
            line.take(s + 1, 1)

        return carry

    lax.fori_loop(0, 2 * n - 1, event, 0)

    for s in range(n - 1):

        @pl.when(t == 0)
        def _():
            ring.first(s, 0)

        @pl.when(t == n - 1)
        def _():
            ring.first(s, 1)

    pl.semaphore_signal(ready, inc=1, device_id={"dp": partner}, device_id_type=MESH)
    pl.semaphore_wait(ready, 1)
    pairs = m // 2

    def held(store, k):
        return store.at[pl.ds(pl.multiple_of(k * strip, strip), strip)]

    def cross(which, store, k):
        return pltpu.make_async_remote_copy(
            src_ref=held(store, k),
            dst_ref=held(store, pairs + k),
            send_sem=core_send.at[which, k],
            recv_sem=core_recv.at[which, k],
            device_id={"dp": partner},
            device_id_type=MESH,
        )

    def put(which, store, k, part_half):
        size = strip // 2
        source = pl.ds(pl.multiple_of((pairs + k) * strip + part_half * size, size), size)
        return pltpu.make_async_copy(
            store.at[source], grads_ref.at[k, part_half, which], grad_sem.at[which, k, part_half]
        )

    def weight_grad(left, rights, mine):
        def outer(k, carry):
            q = 2 * k + (core if mine else 1 - core)
            turned[...] = left[:, pl.ds(pl.multiple_of(q * strip, strip), strip)].T
            slot = pairs + k if mine else k
            at = pl.ds(pl.multiple_of(slot * strip, strip), strip)
            if mine:
                for which, right, store in rights:
                    cross(which, store, k).wait_recv()

            def inner(j, c):
                cols = pl.ds(pl.multiple_of(j * wide, wide), wide)
                for which, right, store in rights:
                    value = dot_nn(turned[...], right[:, cols])
                    if mine:
                        value = value + store[at, cols].astype(F32)
                    store[at, cols] = value.astype(BF)
                return c

            lax.fori_loop(0, units // wide, inner, 0)
            for which, right, store in rights:
                if mine:
                    put(which, store, k, 0).start()
                    put(which, store, k, 1).start()
                else:
                    cross(which, store, k).start()
            return carry

        return outer

    down_store = wd if wd.shape == (depth, units) else spare
    both = ((0, dgate, wg), (1, dup, wu))
    down = ((2, hid, down_store),)
    lax.fori_loop(0, pairs, weight_grad(n2, both, False), 0)
    lax.fori_loop(0, pairs, weight_grad(n2, both, True), 0)
    for tau in range(1, n):
        ring.step(tau)
        if tau < 3:
            lax.fori_loop(0, pairs, weight_grad(cot, down, tau == 2), 0)
    ring.emit(dn2_ref, sum_sem)
    line.finish()
    ring.finish()
    flush(0).wait()

    def settle(k, carry):
        for which, store in ((0, wg), (1, wu), (2, down_store)):
            cross(which, store, k).wait_send()
            put(which, store, k, 0).wait()
            put(which, store, k, 1).wait()
        return carry

    lax.fori_loop(0, pairs, settle, 0)


def mlp(m, n, n2, cot, wg, wu, wd):
    rows, depth = n2.shape
    units = wg.shape[1]
    spare = (16, 128) if wd.shape == (depth, units) else (depth, units)
    return pl.pallas_call(
        functools.partial(mlp_kernel, m, n),
        out_shape=[
            jax.ShapeDtypeStruct((n * rows, depth), BF),
            jax.ShapeDtypeStruct((3, rows, depth), BF),
            jax.ShapeDtypeStruct((m // 2, 2, 3, depth // m // 2, units), BF),
        ],
        in_specs=[HBM] * 5,
        out_specs=[HBM, HBM, HBM],
        scratch_shapes=[
            pltpu.VMEM((n * rows, depth), BF),
            pltpu.VMEM((n * rows, depth), BF),
            pltpu.VMEM((depth, units), BF),
            pltpu.VMEM((depth, units), BF),
            pltpu.VMEM((units, depth), BF),
            pltpu.VMEM((n * rows, units), BF),
            pltpu.VMEM((n * rows, units), BF),
            pltpu.VMEM((n * rows, units), BF),
            pltpu.VMEM((rows, depth), BF),
            pltpu.VMEM((n, rows, depth), BF),
            pltpu.VMEM((n + 1, rows, depth), BF),
            pltpu.VMEM((depth // m, n * rows), BF),
            pltpu.VMEM(spare, BF),
            DMA((5,)),
            DMA,
            DMA((3, m // 2, 2)),
            DMA((2, n - 1)),
            DMA((2, n - 1)),
            DMA((2, n - 1)),
            DMA((2, n - 1)),
            DMA((3, m // 2)),
            DMA((3, m // 2)),
            DMA((3,)),
            pltpu.SemaphoreType.REGULAR,
        ],
        compiler_params=pltpu.CompilerParams(collective_id=3, has_side_effects=True, vmem_limit_bytes=VMEM_MAX),
        name="mlp",
    )(n2, cot, wg, wu, wd)


def input_kernel(n, dq_ref, dk_ref, dv_ref, wq, wk, wv, dn1_ref, part, recv, send_sem, recv_sem, sum_sem):
    t = lax.axis_index(ZAXIS)
    rows = dn1_ref.shape[1]
    ring = LineScatter(t, n, part, recv, send_sem, recv_sem)
    greet_line(t, n)

    def body(k, carry):
        owner = jnp.where(t == n - 1, k, n - 1 - k)
        cols = pl.ds(pl.multiple_of(owner * rows, rows), rows)
        total = dot_nt(dq_ref[:, cols].T, wq[...])
        total = total + dot_nt(dk_ref[:, cols].T, wk[...])
        total = total + dot_nt(dv_ref[:, cols].T, wv[...])
        part[owner] = total.astype(BF)

        @pl.when((t == 0) & (k < n - 1))
        def _():
            ring.first(k, 0)

        @pl.when((t == n - 1) & (k < n - 1))
        def _():
            ring.first(k, 1)

        return carry

    lax.fori_loop(0, n, body, 0)
    for tau in range(1, n):
        ring.step(tau)
    ring.emit(dn1_ref, sum_sem)
    ring.finish()


def input_back(n, dq, dk, dv, wq, wk, wv):
    depth = wq.shape[0]
    rows = dq.shape[1] // n
    return pl.pallas_call(
        functools.partial(input_kernel, n),
        out_shape=jax.ShapeDtypeStruct((3, rows, depth), BF),
        in_specs=[VM] * 6,
        out_specs=HBM,
        scratch_shapes=[
            pltpu.VMEM((n, rows, depth), BF),
            pltpu.VMEM((n + 1, rows, depth), BF),
            DMA((2, n - 1)),
            DMA((2, n - 1)),
            DMA((3,)),
        ],
        compiler_params=pltpu.CompilerParams(collective_id=4, has_side_effects=True, vmem_limit_bytes=VMEM_MAX),
        name="input_back",
    )(dq, dk, dv, wq, wk, wv)


def halve(values, axis_name, size, axis, bit):
    me = lax.axis_index(axis_name)
    mine = (me >> bit) & 1
    keep = lax.dynamic_index_in_dim(values, mine, axis, keepdims=False)
    give = lax.dynamic_index_in_dim(values, 1 - mine, axis, keepdims=False)
    got = lax.ppermute(give, axis_name, [(i, i ^ (1 << bit)) for i in range(size)])
    return keep, got


def add_to(dtype, pair):
    keep, got = pair
    return (keep.astype(F32) + got.astype(F32)).astype(dtype)


def split_bits(values, size):
    bits = size.bit_length() - 1
    return values.reshape((2,) * bits + (values.shape[0] // size,) + values.shape[1:])


def fold(values, m, left, bit, kind):
    axis = left.index(bit)
    return add_to(kind, halve(values, "dp", m, axis, bit)), [b for b in left if b != bit]


class ChipReduce:
    def __init__(self, halves, m, last=F32):
        bits = list(range(m.bit_length() - 2, 0, -1))
        self.m, self.last = m, last
        self.orders = [bits[::-1], bits]
        self.left = [bits, bits]
        self.halves = [h.reshape((2,) * len(bits) + h.shape[1:]) for h in halves]

    def step(self):
        for side in range(2):
            bit = self.orders[side][0]
            self.orders[side] = self.orders[side][1:]
            kind = BF if self.orders[side] else self.last
            self.halves[side], self.left[side] = fold(self.halves[side], self.m, self.left[side], bit, kind)
        return self.halves

    def rest(self):
        while self.orders[0]:
            self.step()
        return self.halves


def core_reduce(values, m):
    rows, cols = values.shape
    parts = values.reshape(m // 2, 2, 2, rows // m // 2, cols)
    core_sum = add_to(BF, halve(parts, "dp", m, 1, 0))
    return [core_sum[:, 0], core_sum[:, 1]]


def reduce_vector(values, m, n):
    parts = split_bits(values.reshape(m, n, -1), m)
    for bit in range(m.bit_length() - 1):
        left = m.bit_length() - 1 - bit
        parts = add_to(F32, halve(parts, "dp", m, left - 1, bit))
    parts = split_bits(parts[0], n)
    for bit in range(n.bit_length() - 1):
        left = n.bit_length() - 1 - bit
        parts = add_to(F32, halve(parts, ZAXIS, n, left - 1, bit))
    return parts[0]


def after(value, *others):
    return lax.optimization_barrier((value,) + others)[0]


def local(
    m,
    n,
    hidden_in,
    attn_gain,
    query_weight,
    key_weight,
    value_weight,
    output_weight,
    mlp_gain,
    gate_weight,
    up_weight,
    down_weight,
    segment_ids,
    positions,
    out_cotangent,
):
    length = segment_ids.shape[0]
    rows, depth = hidden_in.shape
    half = HEAD_DIM // 2
    freqs = THETA ** (-(jnp.arange(half, dtype=F32) * 2.0 / HEAD_DIM))
    angles = freqs[:, None] * positions.astype(F32)[None, :]
    cosine, sine = jnp.cos(angles), jnp.sin(angles)
    seg_row, seg_col = segment_ids[None, :], segment_ids[:, None]

    piece = output_weight.shape[0] // m
    strip = lax.dynamic_slice_in_dim(output_weight, lax.axis_index("dp") * piece, piece, 0)
    out_full = lax.all_gather(strip, (ZAXIS, "dp"), axis=0, tiled=True)

    resid = hidden_in.astype(F32)
    scaled_one, inverse_one = norm_stats(resid)
    normed_one = (scaled_one * attn_gain).astype(BF)
    full_one, qkv = gather_qkv(n, normed_one, query_weight, key_weight, value_weight, cosine, sine)
    full_grad = lax.all_gather(after(out_cotangent, qkv), ZAXIS, axis=0, tiled=True)
    context, lse = attend(qkv, seg_row, seg_col)
    context_all = swap(n, context, True)
    mid = resid + dot_tn(context_all, out_full)
    scaled_two, inverse_two = norm_stats(mid)
    normed_two = (scaled_two * mlp_gain).astype(BF)

    out_part, grad_two_parts, mlp_grads = mlp(m, n, normed_two, full_grad, gate_weight, up_weight, down_weight)
    mlp_reduce = ChipReduce([mlp_grads[:, 0], mlp_grads[:, 1]], m)
    mlp_first = mlp_reduce.step()
    block_out = (
        mid + lax.psum_scatter(out_part, ZAXIS, scatter_dimension=0, tiled=True).astype(F32)
    ).astype(BF)
    grad_normed_two = line_total(grad_two_parts, n)
    grad_mid_norm, gain_two_part = norm_back(grad_normed_two, scaled_two, inverse_two, mlp_gain)
    grad_mid = out_cotangent.astype(F32) + grad_mid_norm
    branch = grad_mid.astype(BF)
    units = gate_weight.shape[1]
    gain_two_sum = reduce_vector(gain_two_part, m, n)

    grad_context = swap(n, dot_nt(out_full, branch).astype(BF), False)
    output_part = lax.dot_general(branch, context_all, (((0,), (1,)), ((), ())), preferred_element_type=F32)
    output_reduce = ChipReduce(core_reduce(output_part.astype(BF), m), m, BF)

    dq, dk, dv = attend_back(qkv, grad_context, lse, seg_row, seg_col, cosine, sine)
    merged = jnp.concatenate([dq, dk, dv], axis=0)
    qkv_part = lax.dot_general(full_one, merged, (((0,), (1,)), ((), ())), preferred_element_type=F32).astype(BF)
    qkv_reduce = ChipReduce(core_reduce(qkv_part, m), m)
    dq, *firsts = lax.optimization_barrier([dq] + mlp_first + qkv_reduce.halves + output_reduce.halves)
    mlp_reduce.halves, qkv_reduce.halves, output_reduce.halves = firsts[:2], firsts[2:4], firsts[4:]
    mlp_sum = jnp.stack(mlp_reduce.rest(), axis=1).reshape(3, depth // m, units)
    grad_normed_one = line_total(input_back(n, dq, dk, dv, query_weight, key_weight, value_weight), n)
    output_rows = jnp.concatenate(output_reduce.rest(), axis=0)
    output_sum = lax.psum_scatter(output_rows, ZAXIS, scatter_dimension=1, tiled=True).astype(F32).T
    qkv_sum = jnp.concatenate(qkv_reduce.rest(), axis=0)
    grad_in_norm, gain_one_part = norm_back(grad_normed_one, scaled_one, inverse_one, attn_gain)
    input_grad = (grad_mid + grad_in_norm).astype(BF)
    gain_one_sum = reduce_vector(gain_one_part, m, n)
    width = query_weight.shape[1]
    return (
        block_out,
        input_grad,
        gain_one_sum,
        qkv_sum[:, :width],
        qkv_sum[:, width : 2 * width],
        qkv_sum[:, 2 * width :],
        output_sum,
        gain_two_sum,
        mlp_sum[0],
        mlp_sum[1],
        mlp_sum[2].T,
    )


def solution(mesh):
    m, n = mesh.shape["dp"], mesh.shape["tensor"]
    in_specs = (
        P(("dp", "tensor"), None),
        P(),
        P(None, "tensor"),
        P(None, "tensor"),
        P(None, "tensor"),
        P("tensor", None),
        P(),
        P(None, "tensor"),
        P(None, "tensor"),
        P("tensor", None),
        P("dp"),
        P("dp"),
        P(("dp", "tensor"), None),
    )
    out_specs = (
        P(("dp", "tensor"), None),
        P(("dp", "tensor"), None),
        P(("dp", "tensor")),
        P("dp", "tensor"),
        P("dp", "tensor"),
        P("dp", "tensor"),
        P("tensor", "dp"),
        P(("dp", "tensor")),
        P("dp", "tensor"),
        P("dp", "tensor"),
        P("tensor", "dp"),
    )
    return jax.shard_map(
        functools.partial(local, m, n), mesh=mesh, in_specs=in_specs, out_specs=out_specs, check_vma=False
    )
```

time: 1730 us -> 839 us (0.48)
  waiting for transfers between devices: 1310 us -> 212 us
  Pallas kernels: 0 us -> 448 us
  matrix products: 281 us -> 28.6 us
  blocking collectives: 46.3 us -> 0 us
  local copies, waits for them, and re-layouts: 4.93 us -> 45.4 us
  starting transfers between devices: 0.87 us -> 28.7 us
    reduce_scatter x11 -> x2, waiting for transfers between devices: 1010 us -> 75.8 us  [the longest x1 60.6 us: local(): lax.psum_scatter(out_part, ZAXIS, scatter_dimension=0, tiled=True)]
    pallas_call x0 -> x7, Pallas kernels: none -> 448 us  [the longest x1 156 us: mlp(): pl.pallas_call(functools.partial(mlp_kernel, m, n), out_shape=[jax.ShapeD...]
    all_gather x4 -> x2, waiting for transfers between devices: 296 us -> 42.2 us  [the longest x1 42.1 us: local(): lax.all_gather(after(out_cotangent, qkv), ZAXIS, axis=0, tiled=True)]
    dot_general x27 -> x4, matrix products: 281 us -> 28.6 us  [the longest x1 13.3 us: local(): lax.dot_general(full_one, merged, (((0,), (1,)), ((), ())), preferred_ele...]
    ppermute x0 -> x24, waiting for transfers between devices: none -> 93.9 us  [halve(): lax.ppermute(give, axis_name, [(i, i ^ 1 << bit) for i in range(size)])]
    unnamed x1 -> x0, blocking collectives: 46.3 us -> none
    ppermute x0 -> x24, starting transfers between devices: none -> 28.5 us  [halve(): lax.ppermute(give, axis_name, [(i, i ^ 1 << bit) for i in range(size)])]
    convert_element_type x6 -> x14, other arithmetic: 40.1 us -> 26.4 us  [the longest x10 19.5 us: add_to(): return (keep.astype(F32) + got.astype(F32)).astype(dtype)]
  transfers between devices with their start and end apart: 15 -> 28, of which waited for: 15 -> 15; matrix products, arithmetic and copies ran while one was open for 7% -> 12% of each run, Pallas kernels for 0% -> 26%
where the time goes in v1:
time: 839 us; the launch traced here: 830 us
  Pallas kernels  448 us (53%)
  waiting for transfers between devices  212 us (25%)
  other arithmetic  52.7 us (6%)
  local copies, waits for them, and re-layouts  45.4 us (5%)
  starting transfers between devices  28.7 us (3%)
  matrix products  28.6 us (3%)
  between operations  14.6 us (2%)
    pallas_call x1, Pallas kernels, mlp(): pl.pallas_call(functools.partial(mlp_kernel, m, n), out_shape=[jax.ShapeD...  156 us
    pallas_call x1, Pallas kernels, gather_qkv(): pl.pallas_call(functools.partial(qkv_kernel, n), out_shape=[jax.ShapeDtyp...  119 us
    ppermute x24, waiting for transfers between devices, halve(): lax.ppermute(give, axis_name, [(i, i ^ 1 << bit) for i in range(size)])  93.9 us
    pallas_call x1, Pallas kernels, input_back(): pl.pallas_call(functools.partial(input_kernel, n), out_shape=jax.ShapeDty...  79.1 us
    reduce_scatter x1, waiting for transfers between devices, local(): lax.psum_scatter(out_part, ZAXIS, scatter_dimension=0, tiled=True)  60.6 us
    pallas_call x2, Pallas kernels, swap(): pl.pallas_call(functools.partial(swap_kernel, n, forward), out_shape=jax....  58.6 us
    all_gather x1, waiting for transfers between devices, local(): lax.all_gather(after(out_cotangent, qkv), ZAXIS, axis=0, tiled=True)  42.1 us
    ppermute x24, starting transfers between devices, halve(): lax.ppermute(give, axis_name, [(i, i ^ 1 << bit) for i in range(size)])  28.5 us
  transfers between devices with their start and end apart: 28, of which 15 were waited for; matrix products, arithmetic and copies ran while one was open for 12% of the time, Pallas kernels for 26%

profile of v1, /device:TPU:0, one launch (start us, length us, event | category | flops | bytes accessed | tf_op | source)
XLA Modules:
  0.0 829.8 jit_solution(15429774313614637687)
XLA Ops:
  13.8 118.8 %gather_qkv.1 = (bf16[1024,2048]{1,0:T(8,128)(2,1)}, bf16[1536,1024]{1,0:T(8,128)(2,1)}) custom-call(bf16[256,2048]{1,0:T(8,128)(2,1)} %fusion.15.n1_ref, bf16[2048,512]{1,0:T(8,128)(2,1)} %wq.3, bf16[2048,512]{1,0:T(8,128)(2,1)} %wk.3, bf16[2048,512]{1,0:T(8,128)(2,1)} %wv.3, f32[32,1024]{1,0:T(8,128)} %get-tuple-element.92.cos_ref, ...), custom_call_target="tpu_custom_call" | custom-call | tf_op jit(solution)/shard_map/gather_qkv/pallas_call | solution.py:268
  134.8 13.2 %attend.1 = (bf16[512,1024]{1,0:T(8,128)(2,1)S(1)}, f32[8,1,1024]{2,1,0:T(1,128)S(1)}) custom-call(bf16[1536,1024]{1,0:T(8,128)(2,1)S(1)} %copy-done, bf16[1536,1024]{1,0:T(8,128)(2,1)S(1)} %copy-done, bf16[1536,1024]{1,0:T(8,128)(2,1)S(1)} %copy-done, s32[1,1024]{1,0:T(1,128)S(1)} %bitcast.182, s32[1024,1]{1,0:T(8,128)S(1)} %copy.36.seg_col), custom_call_target="tpu_custom_call" | custom-call | tf_op jit(solution)/shard_map/attend/pallas_call | solution.py:315
  148.1 36.8 %swap_out.1 = bf16[2048,256]{1,0:T(8,128)(2,1)S(1)} custom-call(bf16[512,1024]{1,0:T(8,128)(2,1)S(1)} %get-tuple-element.30.x_ref), custom_call_target="tpu_custom_call" | custom-call | tf_op jit(solution)/shard_map/swap_out/pallas_call | solution.py:424
  185.0 6.4 multiply_reduce_fusion.1
  194.0 42.1 %all-gather.5.cloned.1.call-done.cot_ref = bf16[1024,2048]{1,0:T(8,128)(2,1)} async-done(((bf16[256,2048]{1,0:T(8,128)(2,1)}), bf16[1024,2048]{1,0:T(8,128)(2,1)}) %all-gather.5.cloned.1.call-update) | async-done | bytes 4194320 | tf_op jit(solution)/shard_map/all_gather | solution.py:857
  236.1 155.9 %mlp.1 = (bf16[1024,2048]{1,0:T(8,128)(2,1)}, bf16[3,256,2048]{2,1,0:T(8,128)(2,1)}, bf16[4,2,3,128,2048]{4,3,2,1,0:T(8,128)(2,1)}) custom-call(bf16[256,2048]{1,0:T(8,128)(2,1)} %multiply_convert_fusion.n2_ref, bf16[1024,2048]{1,0:T(8,128)(2,1)} %all-gather.5.cloned.1.call-done.cot_ref, bf16[2048,2048]{1,0:T(8,128)(2,1)} %wg_ref.1, ...), custom_call_target="tpu_custom_call" | custom-call | tf_op jit(solution)/shard_map/mlp/pallas_call | solution.py:664
  392.1 5.7 fusion.63
  407.8 60.6 %reduce-scatter.3.cloned.1.call-done = bf16[256,2048]{1,0:T(8,128)(2,1)} async-done(((bf16[1024,2048]{1,0:T(8,128)(2,1)}), bf16[256,2048]{1,0:T(8,128)(2,1)}) %reduce-scatter.3.cloned.1.call-update) | async-done | bytes 1048592 | tf_op jit(solution)/shard_map/reduce_scatter | solution.py:868
  468.4 4.9 multiply_add_fusion
  473.3 6.5 convolution_convert_fusion.2.x_ref
  479.8 21.7 %swap_back.1.g_ref = bf16[512,1024]{1,0:T(8,128)(2,1)S(1)} custom-call(bf16[2048,256]{1,0:T(8,128)(2,1)S(1)} %convolution_convert_fusion.2.x_ref), custom_call_target="tpu_custom_call" | custom-call | tf_op jit(solution)/shard_map/swap_back/pallas_call | solution.py:424
  501.6 22.2 %attend_back.1 = (bf16[512,1024]{1,0:T(8,128)(2,1)S(1)}, bf16[512,1024]{1,0:T(8,128)(2,1)S(1)}, bf16[512,1024]{1,0:T(8,128)(2,1)S(1)}) custom-call(bf16[1536,1024]{1,0:T(8,128)(2,1)} %get-tuple-element.29.q_ref.k_ref.v_ref, bf16[1536,1024]{1,0:T(8,128)(2,1)} %get-tuple-element.29.q_ref.k_ref.v_ref, bf16[1536,1024]{1,0:T(8,128)(2,1)} %get-tuple-element.29.q_ref.k_ref.v_ref, ...), custom_call_target="tpu_custom_call" | custom-call | tf_op jit(solution)/shard_map/attend_back/pallas_call | solution.py:366
  523.8 13.3 %convolution_convert_fusion.1 = bf16[2048,1536]{1,0:T(8,128)(2,1)S(1)} fusion(bf16[1024,2048]{1,0:T(8,128)(2,1)} %get-tuple-element.37, bf16[512,1024]{1,0:T(8,128)(2,1)S(1)} %get-tuple-element.39.dv_ref, bf16[512,1024]{1,0:T(8,128)(2,1)S(1)} %get-tuple-element.38.dk_ref, bf16[512,1024]{1,0:T(8,128)(2,1)S(1)} %get-tuple-element.40.dq_ref), kind=kOutput, calls=%fused_computation.3 | convolution fusion | flops 6455033856 | bytes 13631488 | tf_op jit(solution)/shard_map/dot_general | solution.py:883
  543.7 4.1 constant_dynamic-slice_fusion.21
  547.8 4.9 copy.57
  553.4 7.0 collective-permute-done.17
  567.6 6.2 fusion.3
  573.8 5.0 fusion.2
  578.8 2.8 fusion.1
  584.9 4.1 fusion
  591.3 79.1 %input_back.1 = bf16[3,256,2048]{2,1,0:T(8,128)(2,1)} custom-call(bf16[512,1024]{1,0:T(8,128)(2,1)} %copy-done.5, bf16[512,1024]{1,0:T(8,128)(2,1)} %copy-done.6, bf16[512,1024]{1,0:T(8,128)(2,1)} %copy-done.7, bf16[2048,512]{1,0:T(8,128)(2,1)} %wq.3, bf16[2048,512]{1,0:T(8,128)(2,1)} %wk.3, bf16[2048,512]{1,0:T(8,128)(2,1)} %wv.3), custom_call_target="tpu_custom_call" | custom-call | tf_op jit(solution)/shard_map/input_back/pallas_call | solution.py:738
  670.4 3.4 fusion.21
  673.9 3.7 fusion.20
  686.4 16.0 %collective-permute-done.5 = f32[2,1,4,64]{3,2,1,0:T(4,128)S(1)} collective-permute-done((f32[2,1,4,64]{3,2,1,0:T(4,128)S(1)}, f32[2,1,4,64]{3,2,1,0:T(4,128)S(1)}, u32[]{:S(2)}, u32[]{:S(2)}) %collective-permute-start.5) | collective-permute-done | bytes 2080 | tf_op jit(solution)/shard_map/ppermute | solution.py:760
  704.2 17.3 %collective-permute-done.6 = f32[1,4,64]{2,1,0:T(4,128)S(1)} collective-permute-done((f32[1,4,64]{2,1,0:T(4,128)S(1)}, f32[1,4,64]{2,1,0:T(4,128)S(1)}, u32[]{:S(2)}, u32[]{:S(2)}) %collective-permute-start.6) | collective-permute-done | bytes 1056 | tf_op jit(solution)/shard_map/ppermute | solution.py:760
  728.7 2.5 collective-permute-start.8
  733.2 2.5 collective-permute-start.21
  746.2 37.3 %collective-permute-done.12 = bf16[128,1536]{1,0:T(8,128)(2,1)S(1)} collective-permute-done((bf16[128,1536]{1,0:T(8,128)(2,1)S(1)}, bf16[128,1536]{1,0:T(8,128)(2,1)S(1)}, u32[]{:S(2)}, u32[]{:S(2)}) %collective-permute-start.12) | collective-permute-done | bytes 393248 | tf_op jit(solution)/shard_map/ppermute | solution.py:760
  785.9 3.2 collective-permute-done.16
  789.2 3.4 collective-permute-done.14
  801.5 2.4 pad_maximum_fusion
  805.8 15.2 %reduce-scatter.5.cloned.1.call-done = bf16[256,512]{1,0:T(8,128)(2,1)} async-done(((bf16[256,2048]{1,0:T(8,128)(2,1)}), bf16[256,512]{1,0:T(8,128)(2,1)}) %reduce-scatter.5.cloned.1.call-update) | async-done | bytes 262160 | tf_op jit(solution)/shard_map/reduce_scatter | solution.py:890
  (182 shorter events, 86.9 us)
Async XLA Ops:
  7.2 177.8 %all-gather.3.cloned.1.call-start = ((), (), s32[]{:S(2)}) async-start(), calls=%async_computation.2 | async-start | bytes 8650752 | tf_op jit(solution)/shard_map/all_gather | solution.py:851
  9.0 227.1 %all-gather.5.cloned.1.call-start = ((), (), s32[]{:S(2)}) async-start(), calls=%async_computation.3 | async-start | bytes 5242880 | tf_op jit(solution)/shard_map/all_gather | solution.py:857
  13.8 118.9 %copy-start.8 = (s32[1024]{0:T(1024)S(1)}, s32[1024]{0:T(1024)}, u32[]{:S(2)}) copy-start(s32[1024]{0:T(1024)} %param.23) | copy-start | bytes 12292
  132.7 335.7 %reduce-scatter.3.cloned.1.call-start = ((), (), s32[]{:S(2)}) async-start(), calls=%async_computation.4 | async-start | bytes 5242880 | tf_op jit(solution)/shard_map/reduce_scatter | solution.py:868
  392.0 429.0 %reduce-scatter.5.cloned.1.call-start = ((), (), s32[]{:S(2)}) async-start(), calls=%async_computation.5 | async-start | bytes 1310720 | tf_op jit(solution)/shard_map/reduce_scatter | solution.py:890
  400.1 167.5 %collective-permute-start = (bf16[2,3,128,2048]{3,2,1,0:T(8,128)(2,1)}, bf16[2,3,128,2048]{3,2,1,0:T(8,128)(2,1)}, u32[]{:S(2)}, u32[]{:S(2)}) collective-permute-start(bf16[2,3,128,2048]{3,2,1,0:T(8,128)(2,1)} %dynamic-slice_bitcast_fusion.1), channel_id=1, source_target_pairs={{0,8},{4,12},{8,0},{12,4},{16,24},{20,28},{24,16},{28,20},{1,9},{5... | collective-permute-start | bytes 9437192 | tf_op jit(solution)/shard_map/ppermute | solution.py:760
  405.2 168.6 %collective-permute-start.1 = (bf16[2,3,128,2048]{3,2,1,0:T(8,128)(2,1)}, bf16[2,3,128,2048]{3,2,1,0:T(8,128)(2,1)}, u32[]{:S(2)}, u32[]{:S(2)}) collective-permute-start(bf16[2,3,128,2048]{3,2,1,0:T(8,128)(2,1)} %dynamic-slice_bitcast_fusion), channel_id=1, source_target_pairs={{0,16},{4,20},{8,24},{12,28},{16,0},{20,4},{24,8},{28,12},{1,17},{... | collective-permute-start | bytes 9437192 | tf_op jit(solution)/shard_map/ppermute | solution.py:760
  473.3 68.0 %copy-start.16 = (f32[256,2048]{1,0:T(8,128)}, f32[256,2048]{1,0:T(8,128)S(1)}, u32[]{:S(2)}) copy-start(f32[256,2048]{1,0:T(8,128)S(1)} %get-tuple-element.86) | copy-start | bytes 6291460
  541.3 37.6 %collective-permute-start.2 = (bf16[4,2,128,1536]{3,2,0,1:T(8,128)(2,1)}, bf16[4,2,128,1536]{3,2,0,1:T(8,128)(2,1)}, u32[]{:S(2)}, u32[]{:S(2)}) collective-permute-start(bf16[4,2,128,1536]{3,2,0,1:T(8,128)(2,1)} %bitcast.180), channel_id=1, source_target_pairs={{0,4},{4,0},{8,12},{12,8},{16,20},{20,16},{24,28},{28,24},{1,5},{5... | collective-permute-start | bytes 9437192 | tf_op jit(solution)/shard_map/ppermute | solution.py:760
  552.7 30.9 %collective-permute-start.3 = (bf16[4,2,128,2048]{3,2,0,1:T(8,128)(2,1)}, bf16[4,2,128,2048]{3,2,0,1:T(8,128)(2,1)}, u32[]{:S(2)}, u32[]{:S(2)}) collective-permute-start(bf16[4,2,128,2048]{3,2,0,1:T(8,128)(2,1)} %bitcast.179), channel_id=1, source_target_pairs={{0,4},{4,0},{8,12},{12,8},{16,20},{20,16},{24,28},{28,24},{1,5},{5... | collective-permute-start | bytes 12582920 | tf_op jit(solution)/shard_map/ppermute | solution.py:760
  553.3 7.0 collective-permute-start.17
  560.4 3.6 collective-permute-start.18
  564.0 3.6 collective-permute-start.19
  677.7 6.4 collective-permute-start.4
  679.1 60.6 %collective-permute-start.11 = (bf16[2,128,1536]{2,1,0:T(8,128)(2,1)S(1)}, bf16[2,128,1536]{2,1,0:T(8,128)(2,1)S(1)}, u32[]{:S(2)}, u32[]{:S(2)}) collective-permute-start(bf16[2,128,1536]{2,1,0:T(8,128)(2,1)S(1)} %dynamic-slice_bitcast_fusion.6), channel_id=1, source_target_pairs={{0,16},{4,20},{8,24},{12,28},{16,0},{20,4},{24,8},{28,12},{1,17},{... | collective-permute-start | bytes 2359304 | tf_op jit(solution)/shard_map/ppermute | solution.py:760
  681.8 59.5 %collective-permute-start.9 = (bf16[2,128,1536]{2,1,0:T(8,128)(2,1)S(1)}, bf16[2,128,1536]{2,1,0:T(8,128)(2,1)S(1)}, u32[]{:S(2)}, u32[]{:S(2)}) collective-permute-start(bf16[2,128,1536]{2,1,0:T(8,128)(2,1)S(1)} %dynamic-slice_bitcast_fusion.7), channel_id=1, source_target_pairs={{0,8},{4,12},{8,0},{12,4},{16,24},{20,28},{24,16},{28,20},{1,9},{5... | collective-permute-start | bytes 2359304 | tf_op jit(solution)/shard_map/ppermute | solution.py:760
  683.5 58.8 %collective-permute-start.15 = (bf16[2,128,2048]{2,1,0:T(8,128)(2,1)S(1)}, bf16[2,128,2048]{2,1,0:T(8,128)(2,1)S(1)}, u32[]{:S(2)}, u32[]{:S(2)}) collective-permute-start(bf16[2,128,2048]{2,1,0:T(8,128)(2,1)S(1)} %dynamic-slice_bitcast_fusion.4), channel_id=1, source_target_pairs={{0,16},{4,20},{8,24},{12,28},{16,0},{20,4},{24,8},{28,12},{1,17},{... | collective-permute-start | bytes 3145736 | tf_op jit(solution)/shard_map/ppermute | solution.py:760
  684.1 18.3 %collective-permute-start.5 = (f32[2,1,4,64]{3,2,1,0:T(4,128)S(1)}, f32[2,1,4,64]{3,2,1,0:T(4,128)S(1)}, u32[]{:S(2)}, u32[]{:S(2)}) collective-permute-start(f32[2,1,4,64]{3,2,1,0:T(4,128)S(1)} %fusion.44), channel_id=1, source_target_pairs={{0,8},{4,12},{8,0},{12,4},{16,24},{20,28},{24,16},{28,20},{1,9},{5... | collective-permute-start | bytes 6152 | tf_op jit(solution)/shard_map/ppermute | solution.py:760
  684.8 38.5 %copy-start.18 = (bf16[2,3,128,2048]{3,2,1,0:T(8,128)(2,1)S(1)}, bf16[2,3,128,2048]{3,2,1,0:T(8,128)(2,1)}, u32[]{:S(2)}) copy-start(bf16[2,3,128,2048]{3,2,1,0:T(8,128)(2,1)} %fusion.3) | copy-start | bytes 9437188
  684.9 59.3 %collective-permute-start.13 = (bf16[2,128,2048]{2,1,0:T(8,128)(2,1)S(1)}, bf16[2,128,2048]{2,1,0:T(8,128)(2,1)S(1)}, u32[]{:S(2)}, u32[]{:S(2)}) collective-permute-start(bf16[2,128,2048]{2,1,0:T(8,128)(2,1)S(1)} %dynamic-slice_bitcast_fusion.5), channel_id=1, source_target_pairs={{0,8},{4,12},{8,0},{12,4},{16,24},{20,28},{24,16},{28,20},{1,9},{5... | collective-permute-start | bytes 3145736 | tf_op jit(solution)/shard_map/ppermute | solution.py:760
  702.4 19.1 %collective-permute-start.6 = (f32[1,4,64]{2,1,0:T(4,128)S(1)}, f32[1,4,64]{2,1,0:T(4,128)S(1)}, u32[]{:S(2)}, u32[]{:S(2)}) collective-permute-start(f32[1,4,64]{2,1,0:T(4,128)S(1)} %fusion.50), channel_id=1, source_target_pairs={{0,16},{4,20},{8,24},{12,28},{16,0},{20,4},{24,8},{28,12},{1,17},{... | collective-permute-start | bytes 3080 | tf_op jit(solution)/shard_map/ppermute | solution.py:760
  704.2 36.9 %copy-start.27 = (bf16[4,1,128,1536]{3,2,0,1:T(8,128)(2,1)S(1)}, bf16[4,1,128,1536]{3,2,0,1:T(8,128)(2,1)}, u32[]{:S(2)}) copy-start(bf16[4,1,128,1536]{3,2,0,1:T(8,128)(2,1)} %get-tuple-element.84) | copy-start | bytes 4718596
  721.5 3.6 collective-permute-start.7
  725.1 3.6 collective-permute-start.20
  728.7 4.5 collective-permute-start.8
  733.2 4.5 collective-permute-start.21
  737.7 59.9 %collective-permute-start.23 = (bf16[3,128,2048]{2,1,0:T(8,128)(2,1)}, bf16[3,128,2048]{2,1,0:T(8,128)(2,1)}, u32[]{:S(2)}, u32[]{:S(2)}) collective-permute-start(bf16[3,128,2048]{2,1,0:T(8,128)(2,1)} %dynamic-slice_bitcast_fusion.2), channel_id=1, source_target_pairs={{0,8},{4,12},{8,0},{12,4},{16,24},{20,28},{24,16},{28,20},{1,9},{5... | collective-permute-start | bytes 4718600 | tf_op jit(solution)/shard_map/ppermute | solution.py:760
  739.6 59.9 %collective-permute-start.22 = (bf16[3,128,2048]{2,1,0:T(8,128)(2,1)}, bf16[3,128,2048]{2,1,0:T(8,128)(2,1)}, u32[]{:S(2)}, u32[]{:S(2)}) collective-permute-start(bf16[3,128,2048]{2,1,0:T(8,128)(2,1)} %dynamic-slice_bitcast_fusion.3), channel_id=1, source_target_pairs={{0,16},{4,20},{8,24},{12,28},{16,0},{20,4},{24,8},{28,12},{1,17},{... | collective-permute-start | bytes 4718600 | tf_op jit(solution)/shard_map/ppermute | solution.py:760
  741.4 42.1 %collective-permute-start.12 = (bf16[128,1536]{1,0:T(8,128)(2,1)S(1)}, bf16[128,1536]{1,0:T(8,128)(2,1)S(1)}, u32[]{:S(2)}, u32[]{:S(2)}) collective-permute-start(bf16[128,1536]{1,0:T(8,128)(2,1)S(1)} %dynamic-slice_bitcast_fusion.10), channel_id=1, source_target_pairs={{0,8},{4,12},{8,0},{12,4},{16,24},{20,28},{24,16},{28,20},{1,9},{5... | collective-permute-start | bytes 1179656 | tf_op jit(solution)/shard_map/ppermute | solution.py:760
  743.1 50.8 %collective-permute-start.10 = (bf16[128,1536]{1,0:T(8,128)(2,1)S(1)}, bf16[128,1536]{1,0:T(8,128)(2,1)}, u32[]{:S(2)}, u32[]{:S(2)}) collective-permute-start(bf16[128,1536]{1,0:T(8,128)(2,1)S(1)} %dynamic-slice_bitcast_fusion.11), channel_id=1, source_target_pairs={{0,16},{4,20},{8,24},{12,28},{16,0},{20,4},{24,8},{28,12},{1,17},{... | collective-permute-start | bytes 1179656 | tf_op jit(solution)/shard_map/ppermute | solution.py:760
  744.2 44.9 %collective-permute-start.16 = (bf16[128,2048]{1,0:T(8,128)(2,1)S(1)}, bf16[128,2048]{1,0:T(8,128)(2,1)S(1)}, u32[]{:S(2)}, u32[]{:S(2)}) collective-permute-start(bf16[128,2048]{1,0:T(8,128)(2,1)S(1)} %dynamic-slice_bitcast_fusion.8), channel_id=1, source_target_pairs={{0,8},{4,12},{8,0},{12,4},{16,24},{20,28},{24,16},{28,20},{1,9},{5... | collective-permute-start | bytes 1572872 | tf_op jit(solution)/shard_map/ppermute | solution.py:760
  783.5 9.2 %collective-permute-start.14 = (bf16[128,2048]{1,0:T(8,128)(2,1)S(1)}, bf16[128,2048]{1,0:T(8,128)(2,1)S(1)}, u32[]{:S(2)}, u32[]{:S(2)}) collective-permute-start(bf16[128,2048]{1,0:T(8,128)(2,1)S(1)} %dynamic-slice_bitcast_fusion.9), channel_id=1, source_target_pairs={{0,16},{4,20},{8,24},{12,28},{16,0},{20,4},{24,8},{28,12},{1,17},{... | collective-permute-start | bytes 1572872 | tf_op jit(solution)/shard_map/ppermute | solution.py:760
  (29 other events, 240.1 us)
Sparse Core Ops, SparseCore 0:
  11.4 95.0 all-gather.2
  132.8 103.2 all-gather.4
  392.1 76.1 reduce-scatter.2
  794.0 26.9 reduce-scatter.4

commit v2 on v1

--- a/solution.py
+++ b/solution.py
@@ -45,13 +45,17 @@
     return (grad_in, jnp.sum(grad_normed * scaled, axis=0))
 
 
+def cost(us):
+    return pl.CostEstimate(flops=int(us * 1e9), bytes_accessed=1 << 20, transcendentals=0)
+
+
 def inside(value, size):
     return (value >= 0) & (value < size)
 
 
-def greet_line(t, n, partner=None):
+def greet_line(t, n, partners=()):
     barrier = pltpu.get_barrier_semaphore()
-    if partner is not None:
+    for partner in partners:
         pl.semaphore_signal(barrier, inc=1, device_id={"dp": partner}, device_id_type=MESH)
 
     @pl.when(t < n - 1)
@@ -62,18 +66,20 @@
     def _():
         pl.semaphore_signal(barrier, inc=1, device_id={ZAXIS: t - 1}, device_id_type=MESH)
 
-    others = 0 if partner is None else 1
-    pl.semaphore_wait(barrier, others + (t > 0).astype(jnp.int32) + (t < n - 1).astype(jnp.int32))
+    pl.semaphore_wait(barrier, len(partners) + (t > 0).astype(jnp.int32) + (t < n - 1).astype(jnp.int32))
+
+
+def flip(index, bit):
+    return index + (1 << bit) * (1 - 2 * ((index // (1 << bit)) % 2))
 
 
 class LineGather:
-    def __init__(self, t, n, rows, buf, send_sem, recv_sem):
-        self.t, self.n, self.rows = t, n, rows
-        self.buf, self.send_sem, self.recv_sem = buf, send_sem, recv_sem
+    def __init__(self, t, n, place, send_sem, recv_sem):
+        self.t, self.n, self.place = t, n, place
+        self.send_sem, self.recv_sem = send_sem, recv_sem
 
     def slot(self, shard):
-        shard = jnp.clip(shard, 0, self.n - 1)
-        return self.buf.at[pl.ds(pl.multiple_of(shard * self.rows, self.rows), self.rows)]
+        return self.place(jnp.clip(shard, 0, self.n - 1))
 
     def sent(self, s, d):
         return self.t - s + 2 * s * d
@@ -118,6 +124,10 @@
                     self._copy(self.sent(s, d), s, d, self.t + 1 - 2 * d).wait_send()
 
 
+def rows_of(buf, rows):
+    return lambda shard: buf.at[pl.ds(pl.multiple_of(shard * rows, rows), rows)]
+
+
 class LineScatter:
     def __init__(self, t, n, part, recv, send_sem, recv_sem):
         self.t, self.n, self.part, self.recv = t, n, part, recv
@@ -203,16 +213,93 @@
     return own + jnp.where(t > 0, left, 0.0) + jnp.where(t < n - 1, right, 0.0)
 
 
-def qkv_kernel(n, n1_ref, wq, wk, wv, cos_ref, sin_ref, full_ref, qkv_ref, buf, own_sem, out_sem, send_sem, recv_sem):
+class SpreadRows:
+    def __init__(self, m, index, ref, send_sem, recv_sem):
+        self.m, self.index, self.ref = m, index, ref
+        self.send_sem, self.recv_sem = send_sem, recv_sem
+        self.bits = m.bit_length() - 1
+        chip_bits = list(range(1, self.bits))
+        self.orders = [chip_bits + [0], chip_bits[::-1] + [0]]
+        self.steps = self.bits
+
+    def copies(self, step, back):
+        half = self.ref.shape[2] // 2
+        for side in range(2):
+            order = self.orders[side]
+            partner = flip(self.index, order[step])
+            for held in range(1 << step):
+                which = partner if back else self.index
+                for i in range(step):
+                    if held >> i & 1:
+                        which = flip(which, order[i])
+                block = self.ref.at[:, which, side * half : (side + 1) * half]
+                at = (1 << step) - 1 + held
+                yield pltpu.make_async_remote_copy(
+                    src_ref=block,
+                    dst_ref=block,
+                    send_sem=self.send_sem.at[side, at],
+                    recv_sem=self.recv_sem.at[side, at],
+                    device_id={"dp": partner},
+                    device_id_type=MESH,
+                )
+
+    def start(self, step):
+        for copy in self.copies(step, False):
+            copy.start()
+
+    def arrive(self, step):
+        for copy in self.copies(step, True):
+            copy.wait_recv()
+
+    def sent(self):
+        for step in range(self.steps):
+            for copy in self.copies(step, False):
+                copy.wait_send()
+
+
+def qkv_kernel(
+    m,
+    n,
+    n1_ref,
+    wq,
+    wk,
+    wv,
+    cos_ref,
+    sin_ref,
+    strip_ref,
+    full_ref,
+    qkv_ref,
+    wo_ref,
+    buf,
+    own_sem,
+    out_sem,
+    send_sem,
+    recv_sem,
+    wo_send,
+    wo_recv,
+    dp_send,
+    dp_recv,
+):
     t = lax.axis_index(ZAXIS)
+    index = lax.axis_index("dp")
     rows = n1_ref.shape[0]
     width = wq.shape[1]
     half = HEAD_DIM // 2
-    line = LineGather(t, n, rows, buf, send_sem, recv_sem)
-    own = pltpu.make_async_copy(n1_ref, line.slot(t), own_sem)
+    line = LineGather(t, n, rows_of(buf, rows), send_sem, recv_sem)
+    strips = LineGather(t, n, lambda z: wo_ref.at[z, index], wo_send, wo_recv)
+    spread = SpreadRows(m, index, wo_ref, dp_send, dp_recv)
+    own = pltpu.make_async_copy(n1_ref, line.slot(t), own_sem.at[0])
+    own_strip = pltpu.make_async_copy(strip_ref, strips.slot(t), own_sem.at[1])
     own.start()
-    greet_line(t, n)
+    own_strip.start()
+    greet_line(t, n, [flip(index, bit) for bit in range(spread.bits)])
     own.wait()
+    own_strip.wait()
+    strips.start(0, 0)
+    strips.start(0, 1)
+    for s in range(n - 2):
+        strips.take(s, 0)
+        strips.take(s, 1)
     line.start(0, 0)
     line.start(0, 1)
 
@@ -254,35 +341,57 @@
             keep(shard).start()
             project(shard)
 
+        @pl.when(e == 0)
+        def _():
+            strips.take(n - 2, 0)
+            strips.take(n - 2, 1)
+            spread.start(0)
+
+        for step in range(1, spread.steps):
+
+            @pl.when(e == min(2 * step, 2 * n - 2))
+            def _():
+                spread.arrive(step - 1)
+                spread.start(step)
+
         return carry
 
     lax.fori_loop(0, 2 * n - 1, event, 0)
+    spread.arrive(spread.steps - 1)
+    spread.sent()
     line.finish()
+    strips.finish()
     for shard in range(n):
         keep(shard).wait()
 
 
-def gather_qkv(n, n1, wq, wk, wv, cosine, sine):
+def gather_qkv(m, n, n1, wq, wk, wv, cosine, sine, strip):
     rows, depth = n1.shape
     width = wq.shape[1]
     return pl.pallas_call(
-        functools.partial(qkv_kernel, n),
+        functools.partial(qkv_kernel, m, n),
         out_shape=[
             jax.ShapeDtypeStruct((n * rows, depth), BF),
             jax.ShapeDtypeStruct((3 * width, n * rows), BF),
+            jax.ShapeDtypeStruct((n, m) + strip.shape, BF),
         ],
-        in_specs=[VM] * 6,
-        out_specs=[HBM, VM],
+        in_specs=[VM] * 7,
+        out_specs=[HBM, VM, HBM],
         scratch_shapes=[
             pltpu.VMEM((n * rows, depth), BF),
-            DMA,
+            DMA((2,)),
             DMA((n,)),
             DMA((2, n - 1)),
             DMA((2, n - 1)),
+            DMA((2, n - 1)),
+            DMA((2, n - 1)),
+            DMA((2, m - 1)),
+            DMA((2, m - 1)),
         ],
         compiler_params=pltpu.CompilerParams(collective_id=0, has_side_effects=True, vmem_limit_bytes=VMEM_MAX),
+        cost_estimate=cost(90),
         name="gather_qkv",
-    )(n1, wq, wk, wv, cosine, sine)
+    )(n1, wq, wk, wv, cosine, sine, strip)
 
 
 def masked(scores, seg_col, seg_row, start):
@@ -322,6 +431,7 @@
             jax.ShapeDtypeStruct((heads, 1, length), F32),
         ],
         compiler_params=pltpu.CompilerParams(vmem_limit_bytes=48 << 20),
+        cost_estimate=cost(13),
         name="attend",
     )(qkv, qkv, qkv, seg_row, seg_col)
 
@@ -381,6 +491,7 @@
         out_shape=[jax.ShapeDtypeStruct((heads * HEAD_DIM, length), BF)] * 3,
         scratch_shapes=[pltpu.VMEM((HEAD_DIM, length), F32)] * 2,
         compiler_params=pltpu.CompilerParams(vmem_limit_bytes=48 << 20),
+        cost_estimate=cost(22),
         name="attend_back",
     )(qkv, qkv, qkv, grads, lse, seg_row, seg_col, cosine, sine)
 
@@ -430,6 +541,7 @@
         compiler_params=pltpu.CompilerParams(
             collective_id=1 if forward else 2, has_side_effects=True, vmem_limit_bytes=32 << 20
         ),
+        cost_estimate=cost(25),
         name="swap_out" if forward else "swap_back",
     )(x)
 
@@ -445,6 +557,8 @@
     out_ref,
     dn2_ref,
     grads_ref,
+    got_ref,
+    give_ref,
     n2,
     cot,
     wg,
@@ -467,18 +581,22 @@
     rs_recv,
     core_send,
     core_recv,
+    chip_send,
+    chip_recv,
     sum_sem,
     ready,
 ):
     t = lax.axis_index(ZAXIS)
     index = lax.axis_index("dp")
     core = index % 2
-    partner = index + 1 - 2 * core
+    partner = flip(index, 0)
+    top_bit = m.bit_length() - 2
+    peers = [flip(index, 1), flip(index, top_bit)]
     rows, depth = n2_ref.shape
     units = wg.shape[1]
     strip = depth // m
     wide = min(512, units)
-    line = LineGather(t, n, rows, n2, ag_send, ag_recv)
+    line = LineGather(t, n, rows_of(n2, rows), ag_send, ag_recv)
     ring = LineScatter(t, n, part, recv, rs_send, rs_recv)
     loads = [
         pltpu.make_async_copy(n2_ref, line.slot(t), load_sem.at[0]),
@@ -489,7 +607,7 @@
     ]
     for load in loads:
         load.start()
-    greet_line(t, n, partner)
+    greet_line(t, n, [partner] + peers)
     loads[0].wait()
     line.start(0, 0)
     line.start(0, 1)
@@ -596,12 +714,49 @@
             device_id_type=MESH,
         )
 
-    def put(which, store, k, part_half):
+    def chip_bit(part_index, side):
+        return part_index % 2 if side == 0 else part_index // (pairs // 2)
+
+    def short(k, side):
+        return k // 2 if side == 0 else k % (pairs // 2)
+
+    def source(store, k, side):
         size = strip // 2
-        source = pl.ds(pl.multiple_of((pairs + k) * strip + part_half * size, size), size)
+        return store.at[pl.ds(pl.multiple_of((pairs + k) * strip + side * size, size), size)]
+
+    def put(which, store, k, side):
+        at = short(k, side)
         return pltpu.make_async_copy(
-            store.at[source], grads_ref.at[k, part_half, which], grad_sem.at[which, k, part_half]
+            source(store, k, side), grads_ref.at[side, at, which], grad_sem.at[which, at, side]
         )
+
+    def give(which, store, k, side):
+        at = short(k, side)
+        return pltpu.make_async_remote_copy(
+            src_ref=source(store, k, side),
+            dst_ref=got_ref.at[side, at, which],
+            send_sem=chip_send.at[which, at, side],
+            recv_sem=chip_recv.at[which, at, side],
+            device_id={"dp": peers[side]},
+            device_id_type=MESH,
+        )
+
+    def leave(store, k, side):
+        at = short(k, side)
+        return pltpu.make_async_copy(source(store, k, side), give_ref.at[side, at], chip_send.at[2, at, side])
+
+    def moves(which, store, k):
+        for side in range(2):
+            mine = chip_bit(k, side) == chip_bit(index // 2, side)
+            yield mine, put(which, store, k, side)
+            yield jnp.logical_not(mine), leave(store, k, side) if which == 2 else give(which, store, k, side)
+
+    def pass_on(which, store, k):
+        for here, copy in moves(which, store, k):
+
+            @pl.when(here)
+            def _():
+                copy.start()
 
     def weight_grad(left, rights, mine):
         def outer(k, carry):
@@ -625,8 +780,7 @@
             lax.fori_loop(0, units // wide, inner, 0)
             for which, right, store in rights:
                 if mine:
-                    put(which, store, k, 0).start()
-                    put(which, store, k, 1).start()
+                    pass_on(which, store, k)
                 else:
                     cross(which, store, k).start()
             return carry
@@ -650,8 +804,12 @@
     def settle(k, carry):
         for which, store in ((0, wg), (1, wu), (2, down_store)):
             cross(which, store, k).wait_send()
-            put(which, store, k, 0).wait()
-            put(which, store, k, 1).wait()
+            for here, copy in moves(which, store, k):
+
+                @pl.when(here)
+                def _():
+                    copy.wait()
+
         return carry
 
     lax.fori_loop(0, pairs, settle, 0)
@@ -666,10 +824,12 @@
         out_shape=[
             jax.ShapeDtypeStruct((n * rows, depth), BF),
             jax.ShapeDtypeStruct((3, rows, depth), BF),
-            jax.ShapeDtypeStruct((m // 2, 2, 3, depth // m // 2, units), BF),
+            jax.ShapeDtypeStruct((2, m // 4, 3, depth // m // 2, units), BF),
+            jax.ShapeDtypeStruct((2, m // 4, 2, depth // m // 2, units), BF),
+            jax.ShapeDtypeStruct((2, m // 4, depth // m // 2, units), BF),
         ],
         in_specs=[HBM] * 5,
-        out_specs=[HBM, HBM, HBM],
+        out_specs=[HBM] * 5,
         scratch_shapes=[
             pltpu.VMEM((n * rows, depth), BF),
             pltpu.VMEM((n * rows, depth), BF),
@@ -686,26 +846,144 @@
             pltpu.VMEM(spare, BF),
             DMA((5,)),
             DMA,
-            DMA((3, m // 2, 2)),
+            DMA((3, m // 4, 2)),
             DMA((2, n - 1)),
             DMA((2, n - 1)),
             DMA((2, n - 1)),
             DMA((2, n - 1)),
             DMA((3, m // 2)),
             DMA((3, m // 2)),
+            DMA((3, m // 4, 2)),
+            DMA((2, m // 4, 2)),
             DMA((3,)),
             pltpu.SemaphoreType.REGULAR,
         ],
         compiler_params=pltpu.CompilerParams(collective_id=3, has_side_effects=True, vmem_limit_bytes=VMEM_MAX),
+        cost_estimate=cost(155),
         name="mlp",
     )(n2, cot, wg, wu, wd)
 
 
-def input_kernel(n, dq_ref, dk_ref, dv_ref, wq, wk, wv, dn1_ref, part, recv, send_sem, recv_sem, sum_sem):
+class ChipSum:
+    def __init__(self, m, index, block, inbox, send_sem, recv_sem, begin=0):
+        bits = list(range(1, m.bit_length() - 1))
+        self.m, self.index, self.block, self.inbox = m, index, block, inbox
+        self.send_sem, self.recv_sem, self.begin = send_sem, recv_sem, begin
+        self.orders = [bits, bits[::-1]]
+        self.stages = len(bits)
+
+    def slot(self, i, j):
+        return sum((self.m // 2) >> (p + 1) for p in range(self.begin, i)) + j
+
+    def kept(self, side, i, j):
+        k = 0
+        for bit in self.orders[side][: i + 1]:
+            k = k + (self.index // (1 << bit)) % 2 * (1 << (bit - 1))
+        for place, bit in enumerate(self.orders[side][i + 1 :]):
+            k = k + (j >> place & 1) * (1 << (bit - 1))
+        return k
+
+    def copies(self, i):
+        for side in range(2):
+            bit = self.orders[side][i]
+            for j in range((self.m // 2) >> (i + 1)):
+                at = self.slot(i, j)
+                kept = self.kept(side, i, j)
+                copy = pltpu.make_async_remote_copy(
+                    src_ref=self.block(side, flip(kept, bit - 1)),
+                    dst_ref=self.inbox.at[side, at],
+                    send_sem=self.send_sem.at[side, at],
+                    recv_sem=self.recv_sem.at[side, at],
+                    device_id={"dp": flip(self.index, bit)},
+                    device_id_type=MESH,
+                )
+                yield side, kept, at, copy
+
+    def start(self, i):
+        for _, _, _, copy in self.copies(i):
+            copy.start()
+
+    def take(self, i, last):
+        for side, kept, at, copy in self.copies(i):
+            copy.wait_recv()
+            mine = self.block(side, kept)
+            both = mine[...].astype(F32) + self.inbox[side, at].astype(F32)
+            if i == self.stages - 1:
+                last(side, both)
+            else:
+                mine[...] = both.astype(BF)
+
+    def finish(self):
+        for i in range(self.begin, self.stages):
+            for _, _, _, copy in self.copies(i):
+                copy.wait_send()
+
+
+def input_kernel(
+    m,
+    n,
+    dq_ref,
+    dk_ref,
+    dv_ref,
+    wq,
+    wk,
+    wv,
+    full_ref,
+    half_ref,
+    dn1_ref,
+    qs_ref,
+    ks_ref,
+    vs_ref,
+    og_ref,
+    part,
+    recv,
+    full,
+    turned,
+    strips,
+    inbox,
+    out_half,
+    out_inbox,
+    out_part,
+    out_recv,
+    out_total,
+    load_sem,
+    send_sem,
+    recv_sem,
+    core_send,
+    core_recv,
+    chip_send,
+    chip_recv,
+    oc_send,
+    oc_recv,
+    oz_send,
+    oz_recv,
+    sum_sem,
+):
     t = lax.axis_index(ZAXIS)
+    index = lax.axis_index("dp")
+    core = index % 2
+    pairs = m // 2
     rows = dn1_ref.shape[1]
+    strip, width = qs_ref.shape
+    half = strip // 2
     ring = LineScatter(t, n, part, recv, send_sem, recv_sem)
-    greet_line(t, n)
+    out_ring = LineScatter(t, n, out_part, out_recv, oz_send, oz_recv)
+
+    def strip_half(side, k):
+        return strips.at[pairs + k, side * half : (side + 1) * half]
+
+    def out_block(side, k):
+        return out_half.at[side, k // 2 if side == 0 else k % (pairs // 2)]
+
+    chips = ChipSum(m, index, strip_half, inbox, chip_send, chip_recv)
+    out_chips = ChipSum(m, index, out_block, out_inbox, oc_send, oc_recv, begin=1)
+    load = pltpu.make_async_copy(full_ref, full, load_sem.at[0])
+    load_half = pltpu.make_async_copy(half_ref, out_half, load_sem.at[1])
+    load.start()
+    load_half.start()
+    greet_line(t, n, [flip(index, bit) for bit in range(m.bit_length() - 1)])
+    load_half.wait()
+    out_chips.start(1)
 
     def body(k, carry):
         owner = jnp.where(t == n - 1, k, n - 1 - k)
@@ -715,41 +993,146 @@
         total = total + dot_nt(dv_ref[:, cols].T, wv[...])
         part[owner] = total.astype(BF)
 
-        @pl.when((t == 0) & (k < n - 1))
+        @pl.when((t == 0) & (k < n - 2))
         def _():
             ring.first(k, 0)
 
-        @pl.when((t == n - 1) & (k < n - 1))
+        @pl.when((t == n - 1) & (k < n - 2))
         def _():
             ring.first(k, 1)
 
         return carry
 
     lax.fori_loop(0, n, body, 0)
-    for tau in range(1, n):
+    load.wait()
+
+    def cross(k):
+        return pltpu.make_async_remote_copy(
+            src_ref=strips.at[k],
+            dst_ref=strips.at[pairs + k],
+            send_sem=core_send.at[k],
+            recv_sem=core_recv.at[k],
+            device_id={"dp": flip(index, 0)},
+            device_id_type=MESH,
+        )
+
+    def weight_grad(mine):
+        def outer(k, carry):
+            q = 2 * k + (core if mine else 1 - core)
+            turned[...] = full[:, pl.ds(pl.multiple_of(q * strip, strip), strip)].T
+            slot = pairs + k if mine else k
+            if mine:
+                cross(k).wait_recv()
+            for i, grad in enumerate((dq_ref, dk_ref, dv_ref)):
+                at = slice(i * width, (i + 1) * width)
+                value = dot_nt(turned[...], grad[...])
+                if mine:
+                    value = value + strips[slot, :, at].astype(F32)
+                strips[slot, :, at] = value.astype(BF)
+            if not mine:
+                cross(k).start()
+            return carry
+
+        return outer
+
+    lax.fori_loop(0, pairs, weight_grad(False), 0)
+    lax.fori_loop(0, pairs, weight_grad(True), 0)
+    chips.start(0)
+    ring.step(1)
+
+    def hand_out(side, both):
+        for z in range(n):
+            out_part[z, side * half : (side + 1) * half, :] = both[:, z * width : (z + 1) * width].astype(BF)
+
+    def hand_qkv(side, both):
+        for i, ref in enumerate((qs_ref, ks_ref, vs_ref)):
+            ref[side * half : (side + 1) * half, :] = both[:, i * width : (i + 1) * width]
+
+    for i in range(1, out_chips.stages):
+        out_chips.take(i, hand_out)
+        if i + 1 < out_chips.stages:
+            out_chips.start(i + 1)
+    for d, end in ((0, 0), (1, n - 1)):
+
+        @pl.when(t == end)
+        def _():
+            for s in range(n - 1):
+                out_ring.first(s, d)
+            ring.first(n - 2, d)
+
+    for tau in range(2, n):
         ring.step(tau)
+        out_ring.step(tau - 1)
+        i = tau - 2
+        if i < chips.stages:
+            chips.take(i, hand_qkv)
+            if i + 1 < chips.stages:
+                chips.start(i + 1)
+    for i in range(max(n - 2, 0), chips.stages):
+        chips.take(i, hand_qkv)
+        if i + 1 < chips.stages:
+            chips.start(i + 1)
+    out_ring.step(n - 1)
+    out_total[...] = out_part[t].astype(F32)
+
+    @pl.when(t > 0)
+    def _():
+        out_total[...] += out_recv[out_ring.slot(n - 1 - t, 0)].astype(F32)
+
+    @pl.when(t < n - 1)
+    def _():
+        out_total[...] += out_recv[out_ring.slot(t, 1)].astype(F32)
+
+    og_ref[...] = out_total[...].T
     ring.emit(dn1_ref, sum_sem)
     ring.finish()
-
-
-def input_back(n, dq, dk, dv, wq, wk, wv):
-    depth = wq.shape[0]
+    out_ring.finish()
+    chips.finish()
+    out_chips.finish()
+    for k in range(pairs):
+        cross(k).wait_send()
+
+
+def input_back(m, n, dq, dk, dv, wq, wk, wv, full, out_halves):
+    depth, width = wq.shape
     rows = dq.shape[1] // n
+    strip = depth // m
     return pl.pallas_call(
-        functools.partial(input_kernel, n),
-        out_shape=jax.ShapeDtypeStruct((3, rows, depth), BF),
-        in_specs=[VM] * 6,
-        out_specs=HBM,
+        functools.partial(input_kernel, m, n),
+        out_shape=[jax.ShapeDtypeStruct((3, rows, depth), BF)]
+        + [jax.ShapeDtypeStruct((strip, width), F32)] * 3
+        + [jax.ShapeDtypeStruct((width, strip), F32)],
+        in_specs=[VM] * 6 + [HBM] * 2,
+        out_specs=[HBM] + [VM] * 4,
         scratch_shapes=[
             pltpu.VMEM((n, rows, depth), BF),
             pltpu.VMEM((n + 1, rows, depth), BF),
+            pltpu.VMEM(full.shape, BF),
+            pltpu.VMEM((strip, n * rows), BF),
+            pltpu.VMEM((m, strip, 3 * width), BF),
+            pltpu.VMEM((2, m // 2 - 1, strip // 2, 3 * width), BF),
+            pltpu.VMEM(out_halves.shape, BF),
+            pltpu.VMEM((2, m // 4 - 1, strip // 2, n * width), BF),
+            pltpu.VMEM((n, strip, width), BF),
+            pltpu.VMEM((n + 1, strip, width), BF),
+            pltpu.VMEM((strip, width), F32),
+            DMA((2,)),
+            DMA((2, n - 1)),
+            DMA((2, n - 1)),
+            DMA((m // 2,)),
+            DMA((m // 2,)),
+            DMA((2, m // 2 - 1)),
+            DMA((2, m // 2 - 1)),
+            DMA((2, m // 4 - 1)),
+            DMA((2, m // 4 - 1)),
             DMA((2, n - 1)),
             DMA((2, n - 1)),
             DMA((3,)),
         ],
         compiler_params=pltpu.CompilerParams(collective_id=4, has_side_effects=True, vmem_limit_bytes=VMEM_MAX),
+        cost_estimate=cost(95),
         name="input_back",
-    )(dq, dk, dv, wq, wk, wv)
+    )(dq, dk, dv, wq, wk, wv, full, out_halves)
 
 
 def halve(values, axis_name, size, axis, bit):
@@ -761,6 +1144,10 @@
     return keep, got
 
 
+def swap_bit(values, m, bit):
+    return lax.ppermute(values, "dp", [(i, i ^ (1 << bit)) for i in range(m)])
+
+
 def add_to(dtype, pair):
     keep, got = pair
     return (keep.astype(F32) + got.astype(F32)).astype(dtype)
@@ -777,12 +1164,12 @@
 
 
 class ChipReduce:
-    def __init__(self, halves, m, last=F32):
+    def __init__(self, halves, m, last=F32, done=0):
         bits = list(range(m.bit_length() - 2, 0, -1))
         self.m, self.last = m, last
-        self.orders = [bits[::-1], bits]
-        self.left = [bits, bits]
-        self.halves = [h.reshape((2,) * len(bits) + h.shape[1:]) for h in halves]
+        self.orders = [bits[::-1][done:], bits[done:]]
+        self.left = [[b for b in bits if b in order] for order in self.orders]
+        self.halves = [h.reshape((2,) * (len(bits) - done) + h.shape[1:]) for h in halves]
 
     def step(self):
         for side in range(2):
@@ -848,12 +1235,13 @@
 
     piece = output_weight.shape[0] // m
     strip = lax.dynamic_slice_in_dim(output_weight, lax.axis_index("dp") * piece, piece, 0)
-    out_full = lax.all_gather(strip, (ZAXIS, "dp"), axis=0, tiled=True)
-
     resid = hidden_in.astype(F32)
     scaled_one, inverse_one = norm_stats(resid)
     normed_one = (scaled_one * attn_gain).astype(BF)
-    full_one, qkv = gather_qkv(n, normed_one, query_weight, key_weight, value_weight, cosine, sine)
+    full_one, qkv, out_full = gather_qkv(
+        m, n, normed_one, query_weight, key_weight, value_weight, cosine, sine, strip
+    )
+    out_full = out_full.reshape(n * m * piece, depth)
     full_grad = lax.all_gather(after(out_cotangent, qkv), ZAXIS, axis=0, tiled=True)
     context, lse = attend(qkv, seg_row, seg_col)
     context_all = swap(n, context, True)
@@ -861,12 +1249,14 @@
     scaled_two, inverse_two = norm_stats(mid)
     normed_two = (scaled_two * mlp_gain).astype(BF)
 
-    out_part, grad_two_parts, mlp_grads = mlp(m, n, normed_two, full_grad, gate_weight, up_weight, down_weight)
-    mlp_reduce = ChipReduce([mlp_grads[:, 0], mlp_grads[:, 1]], m)
-    mlp_first = mlp_reduce.step()
-    block_out = (
-        mid + lax.psum_scatter(out_part, ZAXIS, scatter_dimension=0, tiled=True).astype(F32)
-    ).astype(BF)
+    out_part, grad_two_parts, mlp_kept, mlp_got, down_give = mlp(
+        m, n, normed_two, full_grad, gate_weight, up_weight, down_weight
+    )
+    bits = [1, m.bit_length() - 2]
+    down_got = [swap_bit(down_give[side], m, bits[side]) for side in range(2)]
+    up_half = [add_to(BF, (mlp_kept[side, :, :2], mlp_got[side])) for side in range(2)]
+    up_reduce = ChipReduce(up_half, m, done=1)
+    out_sum = lax.psum_scatter(out_part, ZAXIS, scatter_dimension=0, tiled=True)
     grad_normed_two = line_total(grad_two_parts, n)
     grad_mid_norm, gain_two_part = norm_back(grad_normed_two, scaled_two, inverse_two, mlp_gain)
     grad_mid = out_cotangent.astype(F32) + grad_mid_norm
@@ -876,35 +1266,34 @@
 
     grad_context = swap(n, dot_nt(out_full, branch).astype(BF), False)
     output_part = lax.dot_general(branch, context_all, (((0,), (1,)), ((), ())), preferred_element_type=F32)
-    output_reduce = ChipReduce(core_reduce(output_part.astype(BF), m), m, BF)
+    output_first = ChipReduce(core_reduce(output_part.astype(BF), m), m).step()
+    output_halves = jnp.stack([h.reshape((m // 4,) + h.shape[-2:]) for h in output_first])
+    down_half = [add_to(BF, (mlp_kept[side, :, 2], down_got[side])) for side in range(2)]
+    down_reduce = ChipReduce(down_half, m, done=1)
+    up_sum = jnp.stack(up_reduce.rest(), axis=1).reshape(2, depth // m, units)
+    down_sum = jnp.concatenate(down_reduce.rest(), axis=0)
 
     dq, dk, dv = attend_back(qkv, grad_context, lse, seg_row, seg_col, cosine, sine)
-    merged = jnp.concatenate([dq, dk, dv], axis=0)
-    qkv_part = lax.dot_general(full_one, merged, (((0,), (1,)), ((), ())), preferred_element_type=F32).astype(BF)
-    qkv_reduce = ChipReduce(core_reduce(qkv_part, m), m)
-    dq, *firsts = lax.optimization_barrier([dq] + mlp_first + qkv_reduce.halves + output_reduce.halves)
-    mlp_reduce.halves, qkv_reduce.halves, output_reduce.halves = firsts[:2], firsts[2:4], firsts[4:]
-    mlp_sum = jnp.stack(mlp_reduce.rest(), axis=1).reshape(3, depth // m, units)
-    grad_normed_one = line_total(input_back(n, dq, dk, dv, query_weight, key_weight, value_weight), n)
-    output_rows = jnp.concatenate(output_reduce.rest(), axis=0)
-    output_sum = lax.psum_scatter(output_rows, ZAXIS, scatter_dimension=1, tiled=True).astype(F32).T
-    qkv_sum = jnp.concatenate(qkv_reduce.rest(), axis=0)
+    grad_one_parts, query_sum, key_sum, value_sum, output_sum = input_back(
+        m, n, dq, dk, dv, query_weight, key_weight, value_weight, full_one, output_halves
+    )
+    grad_normed_one = line_total(grad_one_parts, n)
+    block_out = (mid + after(out_sum, grad_normed_one).astype(F32)).astype(BF)
     grad_in_norm, gain_one_part = norm_back(grad_normed_one, scaled_one, inverse_one, attn_gain)
     input_grad = (grad_mid + grad_in_norm).astype(BF)
     gain_one_sum = reduce_vector(gain_one_part, m, n)
-    width = query_weight.shape[1]
     return (
         block_out,
         input_grad,
         gain_one_sum,
-        qkv_sum[:, :width],
-        qkv_sum[:, width : 2 * width],
-        qkv_sum[:, 2 * width :],
+        query_sum,
+        key_sum,
+        value_sum,
         output_sum,
         gain_two_sum,
-        mlp_sum[0],
-        mlp_sum[1],
-        mlp_sum[2].T,
+        up_sum[0],
+        up_sum[1],
+        down_sum.T,
     )
 
 

time: 839 us -> 709 us (0.85)
  waiting for transfers between devices: 212 us -> 101 us
  Pallas kernels: 448 us -> 486 us
  matrix products: 28.6 us -> 10.6 us
  local copies, waits for them, and re-layouts: 45.4 us -> 29.5 us
  other arithmetic: 52.7 us -> 43.1 us
  starting transfers between devices: 28.7 us -> 19.2 us
    reduce_scatter x2 -> x1, waiting for transfers between devices: 75.8 us -> 0.01 us  [local(): out_sum = lax.psum_scatter(out_part, ZAXIS, scatter_dimension=0, tiled=True)]
    ppermute x24 -> x17, waiting for transfers between devices: 93.9 us -> 54.6 us  [halve(): lax.ppermute(give, axis_name, [(i, i ^ 1 << bit) for i in range(size)])]
    pallas_call x2, Pallas kernels: 198 us -> 218 us  [the longest x1 118 us: input_back(): pl.pallas_call(functools.partial(input_kernel, m, n), out_shape=[jax.Shap...]
    ppermute x24 -> x17, starting transfers between devices: 28.5 us -> 15 us  [halve(): lax.ppermute(give, axis_name, [(i, i ^ 1 << bit) for i in range(size)])]
    dot_general x1 -> x0, matrix products: 13.3 us -> none  [local(): lax.dot_general(full_one, merged, (((0,), (1,)), ((), ())), preferred_ele...]
    pallas_call x2, Pallas kernels: 58.6 us -> 68.4 us  [swap(): pl.pallas_call(functools.partial(swap_kernel, n, forward), out_shape=jax....]
    convert_element_type x10 -> x3, other arithmetic: 19.5 us -> 10.3 us  [add_to(): return (keep.astype(F32) + got.astype(F32)).astype(dtype)]
    pallas_call x1, Pallas kernels: 22.2 us -> 31 us  [attend_back(): pl.pallas_call(functools.partial(attend_back_kernel, 256), grid=(heads,),...]
  transfers between devices with their start and end apart: 28 -> 21, of which waited for: 15 -> 10; matrix products, arithmetic and copies ran while one was open for 12% -> 7% of each run, Pallas kernels for 26% -> 33%
where the time goes in v2:
time: 709 us; the launch traced here: 704 us
  Pallas kernels  486 us (69%)
  waiting for transfers between devices  101 us (14%)
  other arithmetic  43.1 us (6%)
  local copies, waits for them, and re-layouts  29.5 us (4%)
  starting transfers between devices  19.2 us (3%)
  between operations  15 us (2%)
  matrix products  10.6 us (1%)
    pallas_call x1, Pallas kernels, mlp(): pl.pallas_call(functools.partial(mlp_kernel, m, n), out_shape=[jax.ShapeD...  156 us
    pallas_call x1, Pallas kernels, input_back(): pl.pallas_call(functools.partial(input_kernel, m, n), out_shape=[jax.Shap...  118 us
    pallas_call x1, Pallas kernels, gather_qkv(): pl.pallas_call(functools.partial(qkv_kernel, m, n), out_shape=[jax.ShapeD...  99.8 us
    pallas_call x2, Pallas kernels, swap(): pl.pallas_call(functools.partial(swap_kernel, n, forward), out_shape=jax....  68.4 us
    ppermute x17, waiting for transfers between devices, halve(): lax.ppermute(give, axis_name, [(i, i ^ 1 << bit) for i in range(size)])  54.6 us
    all_gather x1, waiting for transfers between devices, local(): lax.all_gather(after(out_cotangent, qkv), ZAXIS, axis=0, tiled=True)  46.2 us
    pallas_call x1, Pallas kernels, attend_back(): pl.pallas_call(functools.partial(attend_back_kernel, 256), grid=(heads,),...  31 us
    ppermute x17, starting transfers between devices, halve(): lax.ppermute(give, axis_name, [(i, i ^ 1 << bit) for i in range(size)])  15 us
  transfers between devices with their start and end apart: 21, of which 10 were waited for; matrix products, arithmetic and copies ran while one was open for 7% of the time, Pallas kernels for 33%

profile of v2, /device:TPU:0, one launch (start us, length us, event | category | flops | bytes accessed | tf_op | source)
XLA Modules:
  0.0 704.2 jit_solution(12727766774586517454)
XLA Ops:
  12.5 2.0 fusion.5.n1_ref
  14.4 99.8 %gather_qkv.1 = (bf16[1024,2048]{1,0:T(8,128)(2,1)}, bf16[1536,1024]{1,0:T(8,128)(2,1)}, bf16[4,8,64,2048]{3,2,1,0:T(8,128)(2,1)}) custom-call(bf16[256,2048]{1,0:T(8,128)(2,1)} %fusion.5.n1_ref, bf16[2048,512]{1,0:T(8,128)(2,1)} %wq.3, bf16[2048,512]{1,0:T(8,128)(2,1)} %wk.3, bf16[2048,512]{1,0:T(8,128)(2,1)} %wv.3, f32[32,1024]{1,0:T(8,128)} %get-tuple-element.102.cos_ref, ...), custom_call_target="tpu_custom_call" | custom-call | flops 89999998976 | bytes 1048576 | tf_op jit(solution)/shard_map/gather_qkv/pallas_call | solution.py:371
  114.6 2.1 copy-done.7
  116.7 13.2 %attend.1 = (bf16[512,1024]{1,0:T(8,128)(2,1)S(1)}, f32[8,1,1024]{2,1,0:T(1,128)S(1)}) custom-call(bf16[1536,1024]{1,0:T(8,128)(2,1)S(1)} %copy-done.7, bf16[1536,1024]{1,0:T(8,128)(2,1)S(1)} %copy-done.7, bf16[1536,1024]{1,0:T(8,128)(2,1)S(1)} %copy-done.7, s32[1,1024]{1,0:T(1,128)S(1)} %bitcast.151, s32[1024,1]{1,0:T(8,128)S(1)} %copy.37.seg_col), custom_call_target="tpu_custom_call" | custom-call | flops 12999999488 | bytes 1048576 | tf_op jit(solution)/shard_map/attend/pallas_call | solution.py:424
  129.9 34.3 %swap_out.1 = bf16[2048,256]{1,0:T(8,128)(2,1)S(1)} custom-call(bf16[512,1024]{1,0:T(8,128)(2,1)S(1)} %get-tuple-element.32.x_ref), custom_call_target="tpu_custom_call" | custom-call | flops 24999999488 | bytes 1048576 | tf_op jit(solution)/shard_map/swap_out/pallas_call | solution.py:535
  164.3 2.4 multiply_reduce_fusion.1
  169.3 46.2 %all-gather.2.cloned.1.call-done.cot_ref = bf16[1024,2048]{1,0:T(8,128)(2,1)} async-done(((bf16[256,2048]{1,0:T(8,128)(2,1)}), bf16[1024,2048]{1,0:T(8,128)(2,1)}) %all-gather.2.cloned.1.call-update) | async-done | bytes 4194320 | tf_op jit(solution)/shard_map/all_gather | solution.py:1245
  215.5 155.8 %mlp.1 = (bf16[1024,2048]{1,0:T(8,128)(2,1)}, bf16[3,256,2048]{2,1,0:T(8,128)(2,1)}, bf16[2,2,3,128,2048]{4,3,2,1,0:T(8,128)(2,1)}, bf16[2,2,2,128,2048]{4,3,2,1,0:T(8,128)(2,1)}, bf16[2,2,128,2048]{3,2,1,0:T(8,128)(2,1)}) custom-call(bf16[256,2048]{1,0:T(8,128)(2,1)} %multiply_convert_fusion.n2_ref, ...), custom_call_target="tpu_custom_call" | custom-call | flops 154999996416 | bytes 1048576 | tf_op jit(solution)/shard_map/mlp/pallas_call | solution.py:822
  371.3 3.6 fusion.20
  375.4 2.5 multiply_add_fusion
  379.1 2.4 convolution_convert_fusion.1.x_ref
  381.5 5.7 convolution_convert_fusion
  387.2 34.1 %swap_back.1.g_ref = bf16[512,1024]{1,0:T(8,128)(2,1)S(1)} custom-call(bf16[2048,256]{1,0:T(8,128)(2,1)S(1)} %convolution_convert_fusion.1.x_ref), custom_call_target="tpu_custom_call" | custom-call | flops 24999999488 | bytes 1048576 | tf_op jit(solution)/shard_map/swap_back/pallas_call | solution.py:535
  421.5 3.3 slice_bitcast_fusion.3
  426.3 2.6 collective-permute-start.17
  428.9 3.2 add_convert_fusion
  434.9 4.2 constant_dynamic-slice_fusion.21
  439.1 4.9 copy.53
  444.1 6.6 collective-permute-done.9
  450.7 2.6 collective-permute-start.10
  453.3 31.0 %attend_back.1 = (bf16[512,1024]{1,0:T(8,128)(2,1)S(1)}, bf16[512,1024]{1,0:T(8,128)(2,1)S(1)}, bf16[512,1024]{1,0:T(8,128)(2,1)S(1)}) custom-call(bf16[1536,1024]{1,0:T(8,128)(2,1)} %get-tuple-element.31.q_ref.k_ref.v_ref, bf16[1536,1024]{1,0:T(8,128)(2,1)} %get-tuple-element.31.q_ref.k_ref.v_ref, bf16[1536,1024]{1,0:T(8,128)(2,1)} %get-tuple-element.31.q_ref.k_ref.v_ref, ...), custom_call_target="tpu_custom_call" | custom-call | flops 22000001024 | bytes 1048576 | tf_op jit(solution)/shard_map/attend_back/pallas_call | solution.py:476
  486.0 3.0 fusion.15
  492.6 17.9 %collective-permute-done.14 = bf16[2,128,2048]{2,1,0:T(8,128)(2,1)S(1)} collective-permute-done((bf16[2,128,2048]{2,1,0:T(8,128)(2,1)S(1)}, bf16[2,128,2048]{2,1,0:T(8,128)(2,1)S(1)}, u32[]{:S(2)}, u32[]{:S(2)}) %collective-permute-start.14) | collective-permute-done | bytes 1048608 | tf_op jit(solution)/shard_map/ppermute | solution.py:1143
  510.9 4.1 fusion
  517.3 2.5 pad_maximum_fusion
  522.9 19.8 %collective-permute-done.1 = bf16[2,128,2048]{2,1,0:T(8,128)(2,1)S(1)} collective-permute-done((bf16[2,128,2048]{2,1,0:T(8,128)(2,1)S(1)}, bf16[2,128,2048]{2,1,0:T(8,128)(2,1)S(1)}, u32[]{:S(2)}, u32[]{:S(2)}) %collective-permute-start.1) | collective-permute-done | bytes 1048608 | tf_op jit(solution)/shard_map/ppermute | solution.py:1143
  545.0 118.0 %input_back.1 = (bf16[3,256,2048]{2,1,0:T(8,128)(2,1)}, f32[256,512]{1,0:T(8,128)}, f32[256,512]{1,0:T(8,128)}, f32[256,512]{1,0:T(8,128)}, f32[512,256]{1,0:T(8,128)}) custom-call(bf16[512,1024]{1,0:T(8,128)(2,1)} %copy-done.8, bf16[512,1024]{1,0:T(8,128)(2,1)} %copy-done.9, bf16[512,1024]{1,0:T(8,128)(2,1)} %copy-done.10, bf16[2048,512]{1,0:T(8,128)(2,1)} %wq.3, ...), custom_call_target="tpu_custom_call" | custom-call | flops 95000002560 | bytes 1048576 | tf_op jit(solution)/shard_map/input_back/pallas_call | solution.py:1100
  663.0 4.5 fusion.11
  671.7 3.0 copy.44
  675.5 3.0 collective-permute-done.5
  678.5 2.0 collective-permute-start.6
  689.0 5.0 fusion.10
  (174 shorter events, 44.1 us)
Async XLA Ops:
  7.2 208.3 %all-gather.2.cloned.1.call-start = ((), (), s32[]{:S(2)}) async-start(), calls=%async_computation.1 | async-start | bytes 5242880 | tf_op jit(solution)/shard_map/all_gather | solution.py:1245
  14.4 99.9 %copy-start.6 = (s32[1024]{0:T(1024)S(1)}, s32[1024]{0:T(1024)}, u32[]{:S(2)}) copy-start(s32[1024]{0:T(1024)} %param.23) | copy-start | bytes 12292
  114.3 574.7 %reduce-scatter.2.cloned.1.call-start = ((), (), s32[]{:S(2)}) async-start(), calls=%async_computation.2 | async-start | bytes 5242880 | tf_op jit(solution)/shard_map/reduce_scatter | solution.py:1259
  129.9 34.3 %slice-start.2 = ((s8[8388608]{0:T(1024)(128)(4,1)}), s8[4194304]{0:T(1024)(128)(4,1)S(1)}, s32[]{:S(2)}) async-start(s8[8388608]{0:T(1024)(128)(4,1)} %bitcast.156), calls=%async_computation.5 | async-start | bytes 8388608
  129.9 34.3 %copy-start.15 = (bf16[256,2048]{1,0:T(8,128)(2,1)S(1)}, bf16[256,2048]{1,0:T(8,128)(2,1)}, u32[]{:S(2)}) copy-start(bf16[256,2048]{1,0:T(8,128)(2,1)} %param.13) | copy-start | bytes 3145732
  129.9 34.3 %slice-start.3 = ((s8[8388608]{0:T(1024)(128)(4,1)}), s8[4194304]{0:T(1024)(128)(4,1)S(1)}, s32[]{:S(2)}) async-start(s8[8388608]{0:T(1024)(128)(4,1)} %bitcast.156), calls=%async_computation.6 | async-start | bytes 8388608
  215.5 155.8 %copy-start.34 = (f32[2048]{0:T(1024)S(1)}, f32[2048]{0:T(1024)}, u32[]{:S(2)}) copy-start(f32[2048]{0:T(1024)} %param.19) | copy-start | bytes 24580
  215.5 155.8 %copy-start.38 = (f32[256]{0:T(256)S(1)}, f32[256]{0:T(256)}, u32[]{:S(2)}) copy-start(f32[256]{0:T(256)} %copy-done.37) | copy-start | bytes 3076
  421.4 12.8 %collective-permute-start.8 = (f32[2,2,1,4,64]{4,3,1,0,2:T(4,128)S(1)}, f32[2,2,1,4,64]{4,3,1,0,2:T(4,128)S(1)}, u32[]{:S(2)}, u32[]{:S(2)}) collective-permute-start(f32[2,2,1,4,64]{4,3,1,0,2:T(4,128)S(1)} %fusion.30), channel_id=1, source_target_pairs={{0,4},{4,0},{8,12},{12,8},{16,20},{20,16},{24,28},{28,24},{1,5},{5... | collective-permute-start | bytes 12296 | tf_op jit(solution)/shard_map/ppermute | solution.py:1143
  424.8 61.2 %collective-permute-start.15 = (bf16[2,128,2048]{2,1,0:T(8,128)(2,1)}, bf16[2,128,2048]{2,1,0:T(8,128)(2,1)}, u32[]{:S(2)}, u32[]{:S(2)}) collective-permute-start(bf16[2,128,2048]{2,1,0:T(8,128)(2,1)} %get-tuple-element.99), channel_id=1, source_target_pairs={{0,8},{4,12},{8,0},{12,4},{16,24},{20,28},{24,16},{28,20},{1,9},{5... | collective-permute-start | bytes 3145736 | tf_op jit(solution)/shard_map/ppermute | solution.py:1148
  426.3 59.7 %collective-permute-start.17 = (bf16[2,128,2048]{2,1,0:T(8,128)(2,1)}, bf16[2,128,2048]{2,1,0:T(8,128)(2,1)}, u32[]{:S(2)}, u32[]{:S(2)}) collective-permute-start(bf16[2,128,2048]{2,1,0:T(8,128)(2,1)} %get-tuple-element.100), channel_id=1, source_target_pairs={{0,16},{4,20},{8,24},{12,28},{16,0},{20,4},{24,8},{28,12},{1,17},{... | collective-permute-start | bytes 3145736 | tf_op jit(solution)/shard_map/ppermute | solution.py:1148
  433.2 57.8 %collective-permute-start.13 = (bf16[2,128,2048]{2,1,0:T(8,128)(2,1)}, bf16[2,128,2048]{2,1,0:T(8,128)(2,1)}, u32[]{:S(2)}, u32[]{:S(2)}) collective-permute-start(bf16[2,128,2048]{2,1,0:T(8,128)(2,1)} %dynamic-slice_bitcast_fusion.1), channel_id=1, source_target_pairs={{0,16},{4,20},{8,24},{12,28},{16,0},{20,4},{24,8},{28,12},{1,17},{... | collective-permute-start | bytes 3145736 | tf_op jit(solution)/shard_map/ppermute | solution.py:1143
  434.3 16.4 %collective-permute-start.9 = (f32[2,1,4,64]{3,2,1,0:T(4,128)S(1)}, f32[2,1,4,64]{3,2,1,0:T(4,128)S(1)}, u32[]{:S(2)}, u32[]{:S(2)}) collective-permute-start(f32[2,1,4,64]{3,2,1,0:T(4,128)S(1)} %fusion.36), channel_id=1, source_target_pairs={{0,8},{4,12},{8,0},{12,4},{16,24},{20,28},{24,16},{28,20},{1,9},{5... | collective-permute-start | bytes 6152 | tf_op jit(solution)/shard_map/ppermute | solution.py:1143
  444.0 66.8 %collective-permute-start = (bf16[4,2,128,2048]{3,2,0,1:T(8,128)(2,1)}, bf16[4,2,128,2048]{3,2,0,1:T(8,128)(2,1)}, u32[]{:S(2)}, u32[]{:S(2)}) collective-permute-start(bf16[4,2,128,2048]{3,2,0,1:T(8,128)(2,1)} %bitcast.149), channel_id=1, source_target_pairs={{0,4},{4,0},{8,12},{12,8},{16,20},{20,16},{24,28},{28,24},{1,5},{5... | collective-permute-start | bytes 12582920 | tf_op jit(solution)/shard_map/ppermute | solution.py:1143
  450.7 33.7 %collective-permute-start.10 = (f32[1,4,64]{2,1,0:T(4,128)S(1)}, f32[1,4,64]{2,1,0:T(4,128)S(1)}, u32[]{:S(2)}, u32[]{:S(2)}) collective-permute-start(f32[1,4,64]{2,1,0:T(4,128)S(1)} %fusion.42), channel_id=1, source_target_pairs={{0,16},{4,20},{8,24},{12,28},{16,0},{20,4},{24,8},{28,12},{1,17},{... | collective-permute-start | bytes 3080 | tf_op jit(solution)/shard_map/ppermute | solution.py:1143
  453.3 31.1 %copy-start.27 = (bf16[2,128,2048]{2,1,0:T(8,128)(2,1)S(1)}, bf16[2,128,2048]{2,1,0:T(8,128)(2,1)}, u32[]{:S(2)}) copy-start(bf16[2,128,2048]{2,1,0:T(8,128)(2,1)} %dynamic-slice_bitcast_fusion) | copy-start | bytes 3145732
  484.4 26.1 %collective-permute-start.14 = (bf16[2,128,2048]{2,1,0:T(8,128)(2,1)S(1)}, bf16[2,128,2048]{2,1,0:T(8,128)(2,1)S(1)}, u32[]{:S(2)}, u32[]{:S(2)}) collective-permute-start(bf16[2,128,2048]{2,1,0:T(8,128)(2,1)S(1)} %copy-done.27), channel_id=1, source_target_pairs={{0,8},{4,12},{8,0},{12,4},{16,24},{20,28},{24,16},{28,20},{1,9},{5... | collective-permute-start | bytes 3145736 | tf_op jit(solution)/shard_map/ppermute | solution.py:1143
  489.1 32.6 %collective-permute-start.18 = (bf16[128,2048]{1,0:T(8,128)(2,1)S(1)}, bf16[128,2048]{1,0:T(8,128)(2,1)S(1)}, u32[]{:S(2)}, u32[]{:S(2)}) collective-permute-start(bf16[128,2048]{1,0:T(8,128)(2,1)S(1)} %dynamic-slice_bitcast_fusion.4), channel_id=1, source_target_pairs={{0,8},{4,12},{8,0},{12,4},{16,24},{20,28},{24,16},{28,20},{1,9},{5... | collective-permute-start | bytes 1572872 | tf_op jit(solution)/shard_map/ppermute | solution.py:1143
  491.0 176.6 %collective-permute-start.16 = (bf16[128,2048]{1,0:T(8,128)(2,1)}, bf16[128,2048]{1,0:T(8,128)(2,1)S(1)}, u32[]{:S(2)}, u32[]{:S(2)}) collective-permute-start(bf16[128,2048]{1,0:T(8,128)(2,1)} %dynamic-slice_bitcast_fusion.5), channel_id=1, source_target_pairs={{0,16},{4,20},{8,24},{12,28},{16,0},{20,4},{24,8},{28,12},{1,17},{... | collective-permute-start | bytes 1572872 | tf_op jit(solution)/shard_map/ppermute | solution.py:1143
  492.6 18.3 %copy-start.18 = (bf16[4,1,2,128,2048]{4,3,2,1,0:T(8,128)(2,1)S(1)}, bf16[4,1,2,128,2048]{4,3,2,1,0:T(8,128)(2,1)}, u32[]{:S(2)}) copy-start(bf16[4,1,2,128,2048]{4,3,2,1,0:T(8,128)(2,1)} %get-tuple-element.91) | copy-start | bytes 12582916
  515.5 27.1 %collective-permute-start.1 = (bf16[2,128,2048]{2,1,0:T(8,128)(2,1)S(1)}, bf16[2,128,2048]{2,1,0:T(8,128)(2,1)S(1)}, u32[]{:S(2)}, u32[]{:S(2)}) collective-permute-start(bf16[2,128,2048]{2,1,0:T(8,128)(2,1)S(1)} %dynamic-slice_bitcast_fusion.3), channel_id=1, source_target_pairs={{0,8},{4,12},{8,0},{12,4},{16,24},{20,28},{24,16},{28,20},{1,9},{5... | collective-permute-start | bytes 3145736 | tf_op jit(solution)/shard_map/ppermute | solution.py:1143
  517.2 25.9 %collective-permute-start.2 = (bf16[2,128,2048]{2,1,0:T(8,128)(2,1)S(1)}, bf16[2,128,2048]{2,1,0:T(8,128)(2,1)S(1)}, u32[]{:S(2)}, u32[]{:S(2)}) collective-permute-start(bf16[2,128,2048]{2,1,0:T(8,128)(2,1)S(1)} %dynamic-slice_bitcast_fusion.2), channel_id=1, source_target_pairs={{0,16},{4,20},{8,24},{12,28},{16,0},{20,4},{24,8},{28,12},{1,17},{... | collective-permute-start | bytes 3145736 | tf_op jit(solution)/shard_map/ppermute | solution.py:1143
  545.0 118.0 %copy-start.32 = (f32[2048]{0:T(1024)S(1)}, f32[2048]{0:T(1024)}, u32[]{:S(2)}) copy-start(f32[2048]{0:T(1024)} %param.14) | copy-start | bytes 24580
  545.0 118.0 %copy-start.36 = (f32[256]{0:T(256)S(1)}, f32[256]{0:T(256)}, u32[]{:S(2)}) copy-start(f32[256]{0:T(256)} %copy-done.35) | copy-start | bytes 3076
  667.5 1.2 collective-permute-start.3
  668.7 6.0 collective-permute-start.4
  671.7 17.3 %copy-start.16 = (bf16[256,2048]{1,0:T(8,128)(2,1)S(1)}, bf16[256,2048]{1,0:T(8,128)(2,1)}, u32[]{:S(2)}) copy-start(bf16[256,2048]{1,0:T(8,128)(2,1)} %param.13) | copy-start | bytes 3145732
  674.8 3.7 collective-permute-start.5
  678.5 3.6 collective-permute-start.11
  678.5 5.4 collective-permute-start.6
  682.1 4.5 collective-permute-start.12
  683.9 4.5 collective-permute-start.7
  (32 other events, 174.9 us)
Sparse Core Ops, SparseCore 0:
  114.4 101.0 all-gather.1
  387.3 87.3 reduce-scatter.1

commit v3 on v2

--- a/solution.py
+++ b/solution.py
@@ -442,22 +442,24 @@
     return jnp.concatenate([first * cosine + second * sine, second * cosine - first * sine], axis=0)
 
 
-def attend_back_kernel(
-    block, q_ref, k_ref, v_ref, g_ref, lse_ref, seg_row, seg_col, cos_ref, sin_ref, dq_ref, dk_ref, dv_ref, dk_sum, dv_sum
-):
-    keys, values = k_ref[...], v_ref[...]
+def attend_back_head(block, head, qkv_ref, g_ref, lse_ref, seg_row, seg_col, cos_ref, sin_ref, outs, dk_sum, dv_sum):
+    dq_ref, dk_ref, dv_ref = outs
+    width, length = g_ref.shape
+    at = lambda base: pl.ds(pl.multiple_of(base + head * HEAD_DIM, HEAD_DIM), HEAD_DIM)
+    keys, values = qkv_ref[at(width), :], qkv_ref[at(2 * width), :]
+    rows = at(0)
     column = seg_col[...]
-    for start in range(0, q_ref.shape[1], block):
+    for start in range(0, length, block):
         end = start + block
         here = slice(start, end)
-        queries, grads = q_ref[:, here], g_ref[:, here]
+        queries, grads = qkv_ref[rows, here], g_ref[rows, here]
         scores = masked(dot_tn(keys[:, :end], queries), column[:end], seg_row[:, here], start)
-        probs = jnp.exp(scores - lse_ref[0, :, here])
+        probs = jnp.exp(scores - lse_ref[head, :, here])
         prob_grad = dot_tn(values[:, :end], grads)
         inner = jnp.sum(probs * prob_grad, axis=0, keepdims=True)
         score_grad = (probs * (prob_grad - inner)).astype(BF)
         dq = dot_nn(keys[:, :end], score_grad) * HEAD_DIM ** (-0.5)
-        dq_ref[:, here] = turn_back(dq, cos_ref[:, here], sin_ref[:, here]).astype(BF)
+        dq_ref[rows, here] = turn_back(dq, cos_ref[:, here], sin_ref[:, here]).astype(BF)
         dv = dot_nt(grads, probs.astype(BF))
         dk = dot_nt(queries, score_grad)
         if start:
@@ -465,45 +467,15 @@
             dk_sum[:, :start] += dk[:, :start]
         dv_sum[:, here] = dv[:, start:]
         dk_sum[:, here] = dk[:, start:]
-    dk_ref[...] = turn_back(dk_sum[...], cos_ref[...], sin_ref[...]).astype(BF)
-    dv_ref[...] = dv_sum[...].astype(BF)
-
-
-def attend_back(qkv, grads, lse, seg_row, seg_col, cosine, sine):
-    heads, length = qkv.shape[0] // (3 * HEAD_DIM), qkv.shape[1]
-    part = lambda o: pl.BlockSpec((HEAD_DIM, length), lambda h: (h + o * heads, 0))
-    whole = lambda *shape: pl.BlockSpec(shape, lambda h: (0,) * len(shape))
-    return pl.pallas_call(
-        functools.partial(attend_back_kernel, 256),
-        grid=(heads,),
-        in_specs=[
-            part(0),
-            part(1),
-            part(2),
-            part(0),
-            pl.BlockSpec((1, 1, length), lambda h: (h, 0, 0)),
-            whole(1, length),
-            whole(length, 1),
-            whole(HEAD_DIM // 2, length),
-            whole(HEAD_DIM // 2, length),
-        ],
-        out_specs=[part(0)] * 3,
-        out_shape=[jax.ShapeDtypeStruct((heads * HEAD_DIM, length), BF)] * 3,
-        scratch_shapes=[pltpu.VMEM((HEAD_DIM, length), F32)] * 2,
-        compiler_params=pltpu.CompilerParams(vmem_limit_bytes=48 << 20),
-        cost_estimate=cost(22),
-        name="attend_back",
-    )(qkv, qkv, qkv, grads, lse, seg_row, seg_col, cosine, sine)
-
-
-def swap_kernel(n, forward, x_ref, o_ref, own_sem, send_sem, recv_sem):
+    dk_ref[rows, :] = turn_back(dk_sum[...], cos_ref[...], sin_ref[...]).astype(BF)
+    dv_ref[rows, :] = dv_sum[...].astype(BF)
+
+
+def swap_kernel(n, x_ref, o_ref, own_sem, send_sem, recv_sem):
     t = lax.axis_index(ZAXIS)
-    rows = x_ref.shape[0] if forward else x_ref.shape[0] // n
-    cols = x_ref.shape[1] // n if forward else x_ref.shape[1]
-    row = lambda i: pl.ds(pl.multiple_of(i * rows, rows), rows)
-    col = lambda i: pl.ds(pl.multiple_of(i * cols, cols), cols)
-    source = lambda i: x_ref.at[:, col(i)] if forward else x_ref.at[row(i), :]
-    target = o_ref.at[row(t), :] if forward else o_ref.at[:, col(t)]
+    rows, cols = x_ref.shape[0], x_ref.shape[1] // n
+    source = lambda i: x_ref.at[:, pl.ds(pl.multiple_of(i * cols, cols), cols)]
+    target = o_ref.at[pl.ds(pl.multiple_of(t * rows, rows), rows), :]
     barrier = pltpu.get_barrier_semaphore()
     for s in range(1, n):
         pl.semaphore_signal(barrier, inc=1, device_id={ZAXIS: lax.rem(t + s, n)}, device_id_type=MESH)
@@ -529,20 +501,17 @@
     own.wait()
 
 
-def swap(n, x, forward):
+def swap(n, x):
     rows, cols = x.shape
-    shape = (rows * n, cols // n) if forward else (rows // n, cols * n)
     return pl.pallas_call(
-        functools.partial(swap_kernel, n, forward),
-        out_shape=jax.ShapeDtypeStruct(shape, x.dtype),
+        functools.partial(swap_kernel, n),
+        out_shape=jax.ShapeDtypeStruct((rows * n, cols // n), x.dtype),
         in_specs=[VM],
         out_specs=VM,
         scratch_shapes=[DMA, DMA((n - 1,)), DMA((n - 1,))],
-        compiler_params=pltpu.CompilerParams(
-            collective_id=1 if forward else 2, has_side_effects=True, vmem_limit_bytes=32 << 20
-        ),
+        compiler_params=pltpu.CompilerParams(collective_id=1, has_side_effects=True, vmem_limit_bytes=32 << 20),
         cost_estimate=cost(25),
-        name="swap_out" if forward else "swap_back",
+        name="swap_out",
     )(x)
 
 
@@ -919,6 +888,257 @@
                 copy.wait_send()
 
 
+def back_kernel(
+    m,
+    n,
+    branch_ref,
+    wo_ref,
+    ctx_ref,
+    qkv_ref,
+    lse_ref,
+    seg_row,
+    seg_col,
+    cos_ref,
+    sin_ref,
+    kept_ref,
+    got_ref,
+    give_ref,
+    dq_ref,
+    dk_ref,
+    dv_ref,
+    out_ref,
+    mlp_ref,
+    wo,
+    outgoing,
+    grads,
+    turned,
+    strips,
+    inbox,
+    kept,
+    got,
+    dk_sum,
+    dv_sum,
+    wo_sem,
+    load_sem,
+    z_send,
+    z_recv,
+    core_send,
+    core_recv,
+    chip_send,
+    chip_recv,
+    down_send,
+    down_recv,
+    put_sem,
+):
+    t = lax.axis_index(ZAXIS)
+    index = lax.axis_index("dp")
+    core = index % 2
+    pairs = m // 2
+    rows, depth = branch_ref.shape
+    width = grads.shape[0]
+    strip = depth // m
+    half = strip // 2
+    peers = [flip(index, 1), flip(index, m.bit_length() - 2)]
+
+    def wo_rows(z):
+        return pl.ds(pl.multiple_of(z * width, width), width)
+
+    def load_wo(s):
+        z = lax.rem(t + s, n)
+        return pltpu.make_async_copy(wo_ref.at[wo_rows(z)], wo.at[wo_rows(z)], wo_sem.at[s - 1])
+
+    for s in range(1, n + 1):
+        load_wo(s).start()
+    loads = [pltpu.make_async_copy(kept_ref, kept, load_sem.at[0])]
+    for side in range(2):
+        for j in range(m // 4):
+            loads.append(
+                pltpu.make_async_copy(got_ref.at[side, j], got.at[side, j, 0:2], load_sem.at[1 + side * (m // 4) + j])
+            )
+    for load in loads:
+        load.start()
+    barrier = pltpu.get_barrier_semaphore()
+    for s in range(1, n):
+        pl.semaphore_signal(barrier, inc=1, device_id={ZAXIS: lax.rem(t + s, n)}, device_id_type=MESH)
+    partners = [flip(index, bit) for bit in range(m.bit_length() - 1)]
+    for partner in partners:
+        pl.semaphore_signal(barrier, inc=1, device_id={"dp": partner}, device_id_type=MESH)
+    pl.semaphore_wait(barrier, n - 1 + len(partners))
+
+    def down(side, j):
+        return pltpu.make_async_remote_copy(
+            src_ref=give_ref.at[side, j],
+            dst_ref=got.at[side, j, 2],
+            send_sem=down_send.at[side, j],
+            recv_sem=down_recv.at[side, j],
+            device_id={"dp": peers[side]},
+            device_id_type=MESH,
+        )
+
+    for side in range(2):
+        for j in range(m // 4):
+            down(side, j).start()
+
+    def token_cols(z):
+        return pl.ds(pl.multiple_of(z * rows, rows), rows)
+
+    def z_copy(s):
+        peer = lax.rem(t + s, n)
+        return pltpu.make_async_remote_copy(
+            src_ref=outgoing.at[peer],
+            dst_ref=grads.at[:, token_cols(t)],
+            send_sem=z_send.at[s - 1],
+            recv_sem=z_recv.at[s - 1],
+            device_id={ZAXIS: peer},
+            device_id_type=MESH,
+        )
+
+    def z_arrive(s):
+        source = lax.rem(t + n - s, n)
+        return pltpu.make_async_remote_copy(
+            src_ref=outgoing.at[source],
+            dst_ref=grads.at[:, token_cols(source)],
+            send_sem=z_send.at[s - 1],
+            recv_sem=z_recv.at[s - 1],
+            device_id={ZAXIS: source},
+            device_id_type=MESH,
+        )
+
+    for s in range(1, n + 1):
+        load_wo(s).wait()
+        z = lax.rem(t + s, n)
+        block = dot_nt(wo[wo_rows(z), :], branch_ref[...]).astype(BF)
+        if s < n:
+            outgoing[z] = block
+            z_copy(s).start()
+        else:
+            grads[:, token_cols(t)] = block
+
+    def cross(k):
+        return pltpu.make_async_remote_copy(
+            src_ref=strips.at[k],
+            dst_ref=strips.at[pairs + k],
+            send_sem=core_send.at[k],
+            recv_sem=core_recv.at[k],
+            device_id={"dp": flip(index, 0)},
+            device_id_type=MESH,
+        )
+
+    def weight_grad(mine):
+        def outer(k, carry):
+            q = 2 * k + (core if mine else 1 - core)
+            turned[...] = branch_ref[:, pl.ds(pl.multiple_of(q * strip, strip), strip)].T
+            slot = pairs + k if mine else k
+            if mine:
+                cross(k).wait_recv()
+            for low in range(0, depth, 512):
+                value = dot_nt(turned[...], ctx_ref[low : low + 512, :])
+                if mine:
+                    value = value + strips[slot, :, low : low + 512].astype(F32)
+                strips[slot, :, low : low + 512] = value.astype(BF)
+            if not mine:
+                cross(k).start()
+            return carry
+
+        return outer
+
+    chips = ChipSum(
+        m, index, lambda side, k: strips.at[pairs + k, side * half : (side + 1) * half], inbox, chip_send, chip_recv
+    )
+    lax.fori_loop(0, pairs, weight_grad(False), 0)
+    lax.fori_loop(0, pairs, weight_grad(True), 0)
+    chips.start(0)
+    for load in loads:
+        load.wait()
+
+    def put_mlp(side, j, which):
+        return pltpu.make_async_copy(
+            kept.at[side, j, which], mlp_ref.at[side, j, which], put_sem.at[which, side, j]
+        )
+
+    def settle(which):
+        for side in range(2):
+            for j in range(m // 4):
+                if which == 2:
+                    down(side, j).wait_recv()
+                both = kept[side, j, which].astype(F32) + got[side, j, which].astype(F32)
+                kept[side, j, which] = both.astype(BF)
+                put_mlp(side, j, which).start()
+
+    settle(0)
+    settle(1)
+    for s in range(1, n):
+        z_arrive(s).wait_recv()
+
+    def head(h, carry):
+        attend_back_head(
+            256, h, qkv_ref, grads, lse_ref, seg_row, seg_col, cos_ref, sin_ref, (dq_ref, dk_ref, dv_ref), dk_sum, dv_sum
+        )
+        return carry
+
+    lax.fori_loop(0, width // HEAD_DIM, head, 0)
+    settle(2)
+
+    def put_out(side, kept_k, j):
+        place = kept_k // 2 if side == 0 else kept_k % (pairs // 2)
+        return pltpu.make_async_copy(chips.block(side, kept_k), out_ref.at[side, place], put_sem.at[3, side, j])
+
+    chips.take(0, None)
+    for side, k, j, _ in chips.copies(0):
+        put_out(side, k, j).start()
+    for side, k, j, copy in chips.copies(0):
+        put_out(side, k, j).wait()
+        copy.wait_send()
+    for s in range(1, n):
+        z_copy(s).wait_send()
+    for k in range(pairs):
+        cross(k).wait_send()
+    for side in range(2):
+        for j in range(m // 4):
+            down(side, j).wait_send()
+            for which in range(3):
+                put_mlp(side, j, which).wait()
+
+
+def back(m, n, branch, wo, ctx, qkv, lse, seg_row, seg_col, cosine, sine, kept, got, give):
+    rows, depth = branch.shape
+    width, length = qkv.shape[0] // 3, qkv.shape[1]
+    strip = depth // m
+    return pl.pallas_call(
+        functools.partial(back_kernel, m, n),
+        out_shape=[jax.ShapeDtypeStruct((width, length), BF)] * 3
+        + [jax.ShapeDtypeStruct((2, m // 4, strip // 2, depth), BF), jax.ShapeDtypeStruct(kept.shape, BF)],
+        in_specs=[VM, HBM] + [VM] * 7 + [HBM] * 3,
+        out_specs=[VM] * 3 + [HBM] * 2,
+        scratch_shapes=[
+            pltpu.VMEM(wo.shape, BF),
+            pltpu.VMEM((n, width, rows), BF),
+            pltpu.VMEM((width, length), BF),
+            pltpu.VMEM((strip, rows), BF),
+            pltpu.VMEM((m, strip, depth), BF),
+            pltpu.VMEM((2, m // 4, strip // 2, depth), BF),
+            pltpu.VMEM(kept.shape, BF),
+            pltpu.VMEM(kept.shape, BF),
+            pltpu.VMEM((HEAD_DIM, length), F32),
+            pltpu.VMEM((HEAD_DIM, length), F32),
+            DMA((n,)),
+            DMA((1 + m // 2,)),
+            DMA((n - 1,)),
+            DMA((n - 1,)),
+            DMA((m // 2,)),
+            DMA((m // 2,)),
+            DMA((2, m // 4)),
+            DMA((2, m // 4)),
+            DMA((2, m // 4)),
+            DMA((2, m // 4)),
+            DMA((4, 2, m // 4)),
+        ],
+        compiler_params=pltpu.CompilerParams(collective_id=2, has_side_effects=True, vmem_limit_bytes=VMEM_MAX),
+        cost_estimate=cost(55),
+        name="back",
+    )(branch, wo, ctx, qkv, lse, seg_row, seg_col, cosine, sine, kept, got, give)
+
+
 def input_kernel(
     m,
     n,
@@ -930,11 +1150,15 @@
     wv,
     full_ref,
     half_ref,
+    mlp_ref,
     dn1_ref,
     qs_ref,
     ks_ref,
     vs_ref,
     og_ref,
+    gate_ref,
+    up_ref,
+    down_ref,
     part,
     recv,
     full,
@@ -946,6 +1170,8 @@
     out_part,
     out_recv,
     out_total,
+    mlp_half,
+    mlp_inbox,
     load_sem,
     send_sem,
     recv_sem,
@@ -957,6 +1183,8 @@
     oc_recv,
     oz_send,
     oz_recv,
+    mc_send,
+    mc_recv,
     sum_sem,
 ):
     t = lax.axis_index(ZAXIS)
@@ -977,13 +1205,31 @@
 
     chips = ChipSum(m, index, strip_half, inbox, chip_send, chip_recv)
     out_chips = ChipSum(m, index, out_block, out_inbox, oc_send, oc_recv, begin=1)
+
+    def mlp_chips(which):
+        def block(side, k):
+            return mlp_half.at[which, side, k // 2 if side == 0 else k % (pairs // 2)]
+
+        return ChipSum(
+            m, index, block, mlp_inbox.at[which], mc_send.at[which], mc_recv.at[which], begin=1
+        )
+
+    matrices = [mlp_chips(which) for which in range(3)]
+    load_mlp = [
+        pltpu.make_async_copy(mlp_ref.at[:, :, which], mlp_half.at[which], load_sem.at[2 + which]) for which in range(3)
+    ]
     load = pltpu.make_async_copy(full_ref, full, load_sem.at[0])
     load_half = pltpu.make_async_copy(half_ref, out_half, load_sem.at[1])
+    load_half.start()
+    for load_one in load_mlp:
+        load_one.start()
     load.start()
-    load_half.start()
     greet_line(t, n, [flip(index, bit) for bit in range(m.bit_length() - 1)])
     load_half.wait()
     out_chips.start(1)
+    for load_one in load_mlp:
+        load_one.wait()
+    matrices[0].start(1)
 
     def body(k, carry):
         owner = jnp.where(t == n - 1, k, n - 1 - k)
@@ -1038,7 +1284,24 @@
     lax.fori_loop(0, pairs, weight_grad(False), 0)
     lax.fori_loop(0, pairs, weight_grad(True), 0)
     chips.start(0)
+    matrices[1].start(1)
+    matrices[2].start(1)
     ring.step(1)
+
+    def hand_matrix(which):
+        def hand(side, both):
+            at = slice(side * half, (side + 1) * half)
+            if which == 2:
+                down_ref[:, at] = both.T
+            else:
+                (gate_ref, up_ref)[which][at, :] = both
+
+        return hand
+
+    def take_matrix(which, i):
+        matrices[which].take(i, hand_matrix(which))
+        if i + 1 < matrices[which].stages:
+            matrices[which].start(i + 1)
 
     def hand_out(side, both):
         for z in range(n):
@@ -1073,6 +1336,9 @@
         if i + 1 < chips.stages:
             chips.start(i + 1)
     out_ring.step(n - 1)
+    for i in range(1, chips.stages):
+        for which in range(3):
+            take_matrix(which, i)
     out_total[...] = out_part[t].astype(F32)
 
     @pl.when(t > 0)
@@ -1089,21 +1355,26 @@
     out_ring.finish()
     chips.finish()
     out_chips.finish()
+    for matrix in matrices:
+        matrix.finish()
     for k in range(pairs):
         cross(k).wait_send()
 
 
-def input_back(m, n, dq, dk, dv, wq, wk, wv, full, out_halves):
+def input_back(m, n, dq, dk, dv, wq, wk, wv, full, out_halves, mlp_halves):
     depth, width = wq.shape
+    units = mlp_halves.shape[-1]
     rows = dq.shape[1] // n
     strip = depth // m
     return pl.pallas_call(
         functools.partial(input_kernel, m, n),
         out_shape=[jax.ShapeDtypeStruct((3, rows, depth), BF)]
         + [jax.ShapeDtypeStruct((strip, width), F32)] * 3
-        + [jax.ShapeDtypeStruct((width, strip), F32)],
-        in_specs=[VM] * 6 + [HBM] * 2,
-        out_specs=[HBM] + [VM] * 4,
+        + [jax.ShapeDtypeStruct((width, strip), F32)]
+        + [jax.ShapeDtypeStruct((strip, units), F32)] * 2
+        + [jax.ShapeDtypeStruct((units, strip), F32)],
+        in_specs=[VM] * 6 + [HBM] * 3,
+        out_specs=[HBM] + [VM] * 7,
         scratch_shapes=[
             pltpu.VMEM((n, rows, depth), BF),
             pltpu.VMEM((n + 1, rows, depth), BF),
@@ -1116,7 +1387,9 @@
             pltpu.VMEM((n, strip, width), BF),
             pltpu.VMEM((n + 1, strip, width), BF),
             pltpu.VMEM((strip, width), F32),
-            DMA((2,)),
+            pltpu.VMEM((3, 2, m // 4, strip // 2, units), BF),
+            pltpu.VMEM((3, 2, m // 4 - 1, strip // 2, units), BF),
+            DMA((5,)),
             DMA((2, n - 1)),
             DMA((2, n - 1)),
             DMA((m // 2,)),
@@ -1127,81 +1400,93 @@
             DMA((2, m // 4 - 1)),
             DMA((2, n - 1)),
             DMA((2, n - 1)),
+            DMA((3, 2, m // 4 - 1)),
+            DMA((3, 2, m // 4 - 1)),
             DMA((3,)),
         ],
         compiler_params=pltpu.CompilerParams(collective_id=4, has_side_effects=True, vmem_limit_bytes=VMEM_MAX),
         cost_estimate=cost(95),
         name="input_back",
-    )(dq, dk, dv, wq, wk, wv, full, out_halves)
-
-
-def halve(values, axis_name, size, axis, bit):
-    me = lax.axis_index(axis_name)
-    mine = (me >> bit) & 1
-    keep = lax.dynamic_index_in_dim(values, mine, axis, keepdims=False)
-    give = lax.dynamic_index_in_dim(values, 1 - mine, axis, keepdims=False)
-    got = lax.ppermute(give, axis_name, [(i, i ^ (1 << bit)) for i in range(size)])
-    return keep, got
-
-
-def swap_bit(values, m, bit):
-    return lax.ppermute(values, "dp", [(i, i ^ (1 << bit)) for i in range(m)])
-
-
-def add_to(dtype, pair):
-    keep, got = pair
-    return (keep.astype(F32) + got.astype(F32)).astype(dtype)
-
-
-def split_bits(values, size):
-    bits = size.bit_length() - 1
-    return values.reshape((2,) * bits + (values.shape[0] // size,) + values.shape[1:])
-
-
-def fold(values, m, left, bit, kind):
-    axis = left.index(bit)
-    return add_to(kind, halve(values, "dp", m, axis, bit)), [b for b in left if b != bit]
-
-
-class ChipReduce:
-    def __init__(self, halves, m, last=F32, done=0):
-        bits = list(range(m.bit_length() - 2, 0, -1))
-        self.m, self.last = m, last
-        self.orders = [bits[::-1][done:], bits[done:]]
-        self.left = [[b for b in bits if b in order] for order in self.orders]
-        self.halves = [h.reshape((2,) * (len(bits) - done) + h.shape[1:]) for h in halves]
-
-    def step(self):
-        for side in range(2):
-            bit = self.orders[side][0]
-            self.orders[side] = self.orders[side][1:]
-            kind = BF if self.orders[side] else self.last
-            self.halves[side], self.left[side] = fold(self.halves[side], self.m, self.left[side], bit, kind)
-        return self.halves
-
-    def rest(self):
-        while self.orders[0]:
-            self.step()
-        return self.halves
-
-
-def core_reduce(values, m):
-    rows, cols = values.shape
-    parts = values.reshape(m // 2, 2, 2, rows // m // 2, cols)
-    core_sum = add_to(BF, halve(parts, "dp", m, 1, 0))
-    return [core_sum[:, 0], core_sum[:, 1]]
-
-
-def reduce_vector(values, m, n):
-    parts = split_bits(values.reshape(m, n, -1), m)
-    for bit in range(m.bit_length() - 1):
-        left = m.bit_length() - 1 - bit
-        parts = add_to(F32, halve(parts, "dp", m, left - 1, bit))
-    parts = split_bits(parts[0], n)
-    for bit in range(n.bit_length() - 1):
-        left = n.bit_length() - 1 - bit
-        parts = add_to(F32, halve(parts, ZAXIS, n, left - 1, bit))
-    return parts[0]
+    )(dq, dk, dv, wq, wk, wv, full, out_halves, mlp_halves)
+
+
+def gains_kernel(m, n, x_ref, o_ref, z_in, total, dp_in, z_send, z_recv, dp_send, dp_recv):
+    t = lax.axis_index(ZAXIS)
+    index = lax.axis_index("dp")
+    barrier = pltpu.get_barrier_semaphore()
+    for s in range(1, n):
+        pl.semaphore_signal(barrier, inc=1, device_id={ZAXIS: lax.rem(t + s, n)}, device_id_type=MESH)
+    for s in range(1, m):
+        pl.semaphore_signal(barrier, inc=1, device_id={"dp": lax.rem(index + s, m)}, device_id_type=MESH)
+    pl.semaphore_wait(barrier, n + m - 2)
+
+    def z_copy(s):
+        peer = lax.rem(t + s, n)
+        return pltpu.make_async_remote_copy(
+            src_ref=x_ref.at[peer],
+            dst_ref=z_in.at[s - 1],
+            send_sem=z_send.at[s - 1],
+            recv_sem=z_recv.at[s - 1],
+            device_id={ZAXIS: peer},
+            device_id_type=MESH,
+        )
+
+    def dp_copy(s):
+        peer = lax.rem(index + s, m)
+        return pltpu.make_async_remote_copy(
+            src_ref=total.at[peer],
+            dst_ref=dp_in.at[s - 1],
+            send_sem=dp_send.at[s - 1],
+            recv_sem=dp_recv.at[s - 1],
+            device_id={"dp": peer},
+            device_id_type=MESH,
+        )
+
+    for s in range(1, n):
+        z_copy(s).start()
+    for s in range(1, n):
+        z_copy(s).wait_recv()
+    value = x_ref[t]
+    for s in range(1, n):
+        value = value + z_in[s - 1]
+    total[...] = value
+    for s in range(1, m):
+        dp_copy(s).start()
+    for s in range(1, m):
+        dp_copy(s).wait_recv()
+    value = total[index]
+    for s in range(1, m):
+        value = value + dp_in[s - 1]
+    o_ref[...] = value
+    for s in range(1, n):
+        z_copy(s).wait_send()
+    for s in range(1, m):
+        dp_copy(s).wait_send()
+
+
+def reduce_gains(m, n, first, second):
+    size = first.shape[0] // (m * n)
+    parts = jnp.stack([first, second]).reshape(2, m, n, size).transpose(2, 1, 0, 3)
+    parts = jnp.pad(parts, ((0, 0), (0, 0), (0, 6), (0, 128 - size)))
+    total = pl.pallas_call(
+        functools.partial(gains_kernel, m, n),
+        out_shape=jax.ShapeDtypeStruct((8, 128), F32),
+        in_specs=[VM],
+        out_specs=VM,
+        scratch_shapes=[
+            pltpu.VMEM((n - 1, m, 8, 128), F32),
+            pltpu.VMEM((m, 8, 128), F32),
+            pltpu.VMEM((m - 1, 8, 128), F32),
+            DMA((n - 1,)),
+            DMA((n - 1,)),
+            DMA((m - 1,)),
+            DMA((m - 1,)),
+        ],
+        compiler_params=pltpu.CompilerParams(collective_id=5, has_side_effects=True),
+        cost_estimate=cost(6),
+        name="gains",
+    )(parts)
+    return total[0, :size], total[1, :size]
 
 
 def after(value, *others):
@@ -1244,7 +1529,7 @@
     out_full = out_full.reshape(n * m * piece, depth)
     full_grad = lax.all_gather(after(out_cotangent, qkv), ZAXIS, axis=0, tiled=True)
     context, lse = attend(qkv, seg_row, seg_col)
-    context_all = swap(n, context, True)
+    context_all = swap(n, context)
     mid = resid + dot_tn(context_all, out_full)
     scaled_two, inverse_two = norm_stats(mid)
     normed_two = (scaled_two * mlp_gain).astype(BF)
@@ -1252,36 +1537,22 @@
     out_part, grad_two_parts, mlp_kept, mlp_got, down_give = mlp(
         m, n, normed_two, full_grad, gate_weight, up_weight, down_weight
     )
-    bits = [1, m.bit_length() - 2]
-    down_got = [swap_bit(down_give[side], m, bits[side]) for side in range(2)]
-    up_half = [add_to(BF, (mlp_kept[side, :, :2], mlp_got[side])) for side in range(2)]
-    up_reduce = ChipReduce(up_half, m, done=1)
     out_sum = lax.psum_scatter(out_part, ZAXIS, scatter_dimension=0, tiled=True)
     grad_normed_two = line_total(grad_two_parts, n)
     grad_mid_norm, gain_two_part = norm_back(grad_normed_two, scaled_two, inverse_two, mlp_gain)
     grad_mid = out_cotangent.astype(F32) + grad_mid_norm
     branch = grad_mid.astype(BF)
-    units = gate_weight.shape[1]
-    gain_two_sum = reduce_vector(gain_two_part, m, n)
-
-    grad_context = swap(n, dot_nt(out_full, branch).astype(BF), False)
-    output_part = lax.dot_general(branch, context_all, (((0,), (1,)), ((), ())), preferred_element_type=F32)
-    output_first = ChipReduce(core_reduce(output_part.astype(BF), m), m).step()
-    output_halves = jnp.stack([h.reshape((m // 4,) + h.shape[-2:]) for h in output_first])
-    down_half = [add_to(BF, (mlp_kept[side, :, 2], down_got[side])) for side in range(2)]
-    down_reduce = ChipReduce(down_half, m, done=1)
-    up_sum = jnp.stack(up_reduce.rest(), axis=1).reshape(2, depth // m, units)
-    down_sum = jnp.concatenate(down_reduce.rest(), axis=0)
-
-    dq, dk, dv = attend_back(qkv, grad_context, lse, seg_row, seg_col, cosine, sine)
-    grad_one_parts, query_sum, key_sum, value_sum, output_sum = input_back(
-        m, n, dq, dk, dv, query_weight, key_weight, value_weight, full_one, output_halves
+    dq, dk, dv, out_halves, mlp_halves = back(
+        m, n, branch, out_full, context_all, qkv, lse, seg_row, seg_col, cosine, sine, mlp_kept, mlp_got, down_give
+    )
+    grad_one_parts, query_sum, key_sum, value_sum, output_sum, gate_sum, up_sum, down_sum = input_back(
+        m, n, dq, dk, dv, query_weight, key_weight, value_weight, full_one, out_halves, mlp_halves
     )
     grad_normed_one = line_total(grad_one_parts, n)
-    block_out = (mid + after(out_sum, grad_normed_one).astype(F32)).astype(BF)
     grad_in_norm, gain_one_part = norm_back(grad_normed_one, scaled_one, inverse_one, attn_gain)
     input_grad = (grad_mid + grad_in_norm).astype(BF)
-    gain_one_sum = reduce_vector(gain_one_part, m, n)
+    gain_one_sum, gain_two_sum = reduce_gains(m, n, gain_one_part, gain_two_part)
+    block_out = (mid + after(out_sum, grad_normed_one).astype(F32)).astype(BF)
     return (
         block_out,
         input_grad,
@@ -1291,9 +1562,9 @@
         value_sum,
         output_sum,
         gain_two_sum,
-        up_sum[0],
-        up_sum[1],
-        down_sum.T,
+        gate_sum,
+        up_sum,
+        down_sum,
     )
 
 

time: 709 us -> 612 us (0.86)
  waiting for transfers between devices: 101 us -> 46.3 us
  Pallas kernels: 486 us -> 507 us
  other arithmetic: 43.1 us -> 22.6 us
  starting transfers between devices: 19.2 us -> 0.08 us
  local copies, waits for them, and re-layouts: 29.5 us -> 18.2 us
  matrix products: 10.6 us -> 2.45 us
    ppermute x19 -> x0, waiting for transfers between devices: 54.6 us -> none  [the longest x17 54.6 us: halve(): lax.ppermute(give, axis_name, [(i, i ^ 1 << bit) for i in range(size)])]
    ppermute x19 -> x0, starting transfers between devices: 19.1 us -> none  [the longest x17 15 us: halve(): lax.ppermute(give, axis_name, [(i, i ^ 1 << bit) for i in range(size)])]
    pallas_call x3, Pallas kernels: 99.4 us -> 116 us  [the longest x1 65.6 us: back(): pl.pallas_call(functools.partial(back_kernel, m, n), out_shape=[jax.Shape...]
    dynamic_slice x3 -> x0, local copies, waits for them, and re-layouts: 9.13 us -> none  [the longest x2 4.91 us: halve(): give = lax.dynamic_index_in_dim(values, 1 - mine, axis, keepdims=False)]
    dot_general x2 -> x0, matrix products: 8.1 us -> none  [the longest x1 5.72 us: local(): lax.dot_general(branch, context_all, (((0,), (1,)), ((), ())), preferred_...]
    convert_element_type x3 -> x1, other arithmetic: 10.3 us -> 2.93 us  [local(): branch = grad_mid.astype(BF)]
    unnamed x91 -> x67, local copies, waits for them, and re-layouts: 11.4 us -> 14.2 us
  transfers between devices with their start and end apart: 21 -> 2, of which waited for: 10 -> 1; matrix products, arithmetic and copies ran while one was open for 7% -> 3% of each run, Pallas kernels for 33% -> 41%
where the time goes in v3:
time: 612 us; the launch traced here: 611 us
  Pallas kernels  507 us (83%)
  waiting for transfers between devices  46.3 us (8%)
  other arithmetic  22.6 us (4%)
  local copies, waits for them, and re-layouts  18.2 us (3%)
  between operations  14.4 us (2%)
    pallas_call x1, Pallas kernels, mlp(): pl.pallas_call(functools.partial(mlp_kernel, m, n), out_shape=[jax.ShapeD...  156 us
    pallas_call x1, Pallas kernels, input_back(): pl.pallas_call(functools.partial(input_kernel, m, n), out_shape=[jax.Shap...  122 us
    pallas_call x1, Pallas kernels, gather_qkv(): pl.pallas_call(functools.partial(qkv_kernel, m, n), out_shape=[jax.ShapeD...  99.8 us
    pallas_call x1, Pallas kernels, back(): pl.pallas_call(functools.partial(back_kernel, m, n), out_shape=[jax.Shape...  65.6 us
    all_gather x1, waiting for transfers between devices, local(): lax.all_gather(after(out_cotangent, qkv), ZAXIS, axis=0, tiled=True)  46.3 us
    pallas_call x1, Pallas kernels, swap(): pl.pallas_call(functools.partial(swap_kernel, n), out_shape=jax.ShapeDtyp...  34.3 us
    pallas_call x1, Pallas kernels, reduce_gains(): pl.pallas_call(functools.partial(gains_kernel, m, n), out_shape=jax.Shape...  16.5 us
    unnamed x67, local copies, waits for them, and re-layouts  14.2 us
  transfers between devices with their start and end apart: 2, of which 1 were waited for; matrix products, arithmetic and copies ran while one was open for 3% of the time, Pallas kernels for 41%

profile of v3, /device:TPU:0, one launch (start us, length us, event | category | flops | bytes accessed | tf_op | source)
XLA Modules:
  0.0 611.2 jit_solution(2220630202357157960)
XLA Ops:
  7.3 1.6 fusion.11
  8.9 0.7 convert_element_type.55
  9.6 1.2 multiply_sine_fusion
  10.8 1.7 constant_dynamic-slice_fusion.strip_ref
  12.5 2.0 fusion.4.n1_ref
  14.4 99.8 %gather_qkv.1 = (bf16[1024,2048]{1,0:T(8,128)(2,1)}, bf16[1536,1024]{1,0:T(8,128)(2,1)}, bf16[4,8,64,2048]{3,2,1,0:T(8,128)(2,1)}) custom-call(bf16[256,2048]{1,0:T(8,128)(2,1)} %fusion.4.n1_ref, bf16[2048,512]{1,0:T(8,128)(2,1)} %wq.3, bf16[2048,512]{1,0:T(8,128)(2,1)} %wk.3, bf16[2048,512]{1,0:T(8,128)(2,1)} %wv.3, f32[32,1024]{1,0:T(8,128)} %get-tuple-element.69.cos_ref, ...), custom_call_target="tpu_custom_call" | custom-call | flops 89999998976 | bytes 1048576 | tf_op jit(solution)/shard_map/gather_qkv/pallas_call | solution.py:371
  114.6 2.1 copy-done.3
  116.7 13.2 %attend.1 = (bf16[512,1024]{1,0:T(8,128)(2,1)S(1)}, f32[8,1,1024]{2,1,0:T(1,128)S(1)}) custom-call(bf16[1536,1024]{1,0:T(8,128)(2,1)S(1)} %copy-done.3, bf16[1536,1024]{1,0:T(8,128)(2,1)S(1)} %copy-done.3, bf16[1536,1024]{1,0:T(8,128)(2,1)S(1)} %copy-done.3, s32[1,1024]{1,0:T(1,128)S(1)} %bitcast.26, s32[1024,1]{1,0:T(8,128)S(1)} %copy.24.seg_col), custom_call_target="tpu_custom_call" | custom-call | flops 12999999488 | bytes 1048576 | tf_op jit(solution)/shard_map/attend/pallas_call | solution.py:424
  129.9 34.3 %swap_out.1.ctx_ref = bf16[2048,256]{1,0:T(8,128)(2,1)S(1)} custom-call(bf16[512,1024]{1,0:T(8,128)(2,1)S(1)} %get-tuple-element.37.x_ref), custom_call_target="tpu_custom_call" | custom-call | flops 24999999488 | bytes 1048576 | tf_op jit(solution)/shard_map/swap_out/pallas_call | solution.py:506
  164.3 2.4 multiply_reduce_fusion.1
  166.8 1.3 copy-done.5
  168.1 1.2 multiply_convert_fusion.n2_ref
  169.3 46.3 %all-gather.2.cloned.1.call-done.cot_ref = bf16[1024,2048]{1,0:T(8,128)(2,1)} async-done(((bf16[256,2048]{1,0:T(8,128)(2,1)}), bf16[1024,2048]{1,0:T(8,128)(2,1)}) %all-gather.2.cloned.1.call-update) | async-done | bytes 4194320 | tf_op jit(solution)/shard_map/all_gather | solution.py:1530
  215.5 155.6 %mlp.1 = (bf16[1024,2048]{1,0:T(8,128)(2,1)}, bf16[3,256,2048]{2,1,0:T(8,128)(2,1)}, bf16[2,2,3,128,2048]{4,3,2,1,0:T(8,128)(2,1)}, bf16[2,2,2,128,2048]{4,3,2,1,0:T(8,128)(2,1)}, bf16[2,2,128,2048]{3,2,1,0:T(8,128)(2,1)}) custom-call(bf16[256,2048]{1,0:T(8,128)(2,1)} %multiply_convert_fusion.n2_ref, ...), custom_call_target="tpu_custom_call" | custom-call | flops 154999996416 | bytes 1048576 | tf_op jit(solution)/shard_map/mlp/pallas_call | solution.py:791
  371.2 1.5 copy-done.6
  372.8 3.6 fusion.12
  376.4 2.9 fusion.13
  379.3 65.6 %back.1 = (bf16[512,1024]{1,0:T(8,128)(2,1)}, bf16[512,1024]{1,0:T(8,128)(2,1)}, bf16[512,1024]{1,0:T(8,128)(2,1)}, bf16[2,2,128,2048]{3,2,1,0:T(8,128)(2,1)}, bf16[2,2,3,128,2048]{4,3,2,1,0:T(8,128)(2,1)}) custom-call(bf16[256,2048]{1,0:T(8,128)(2,1)} %get-tuple-element.66.branch_ref, bf16[2048,2048]{1,0:T(8,128)(2,1)} %bitcast.27, ...), custom_call_target="tpu_custom_call" | custom-call | flops 54999998464 | bytes 1048576 | tf_op jit(solution)/shard_map/back/pallas_call | solution.py:1107
  445.0 122.0 %input_back.1 = (bf16[3,256,2048]{2,1,0:T(8,128)(2,1)}, f32[256,512]{1,0:T(8,128)}, f32[256,512]{1,0:T(8,128)}, f32[256,512]{1,0:T(8,128)}, f32[512,256]{1,0:T(8...) custom-call(bf16[512,1024]{1,0:T(8,128)(2,1)} %get-tuple-element.46.dq_ref, ...), custom_call_target="tpu_custom_call" | custom-call | flops 95000002560 | bytes 1048576 | tf_op jit(solution)/shard_map/input_back/pallas_call | solution.py:1369
  567.1 4.4 fusion.10
  572.4 16.5 %gains.1 = f32[8,128]{1,0:T(8,128)} custom-call(f32[4,8,8,128]{3,2,1,0:T(8,128)} %pad.4.x_ref), custom_call_target="tpu_custom_call" | custom-call | flops 6000000000 | bytes 1048576 | tf_op jit(solution)/shard_map/gains/pallas_call | solution.py:1471
  588.9 1.3 slice_bitcast_fusion
  590.2 5.0 fusion.9
  595.1 0.8 copy.35
  595.9 0.8 copy.36
  596.7 0.8 copy.37
  597.5 0.8 copy.38
  598.3 1.3 copy.39
  599.6 1.0 copy-done.14
  600.7 1.3 copy.40
  602.0 1.0 copy-done.13
  603.0 1.3 copy.41
  (73 shorter events, 1.4 us)
Async XLA Ops:
  7.2 5.3 copy-start.8
  7.2 208.4 %all-gather.2.cloned.1.call-start = ((), (), s32[]{:S(2)}) async-start(), calls=%async_computation.1 | async-start | bytes 5242880 | tf_op jit(solution)/shard_map/all_gather | solution.py:1530
  8.9 5.6 copy-start.24
  14.4 99.9 %copy-start.2 = (s32[1024]{0:T(1024)S(1)}, s32[1024]{0:T(1024)}, u32[]{:S(2)}) copy-start(s32[1024]{0:T(1024)} %param.23) | copy-start | bytes 12292
  114.3 475.9 %reduce-scatter.2.cloned.1.call-start = ((), (), s32[]{:S(2)}) async-start(), calls=%async_computation.2 | async-start | bytes 5242880 | tf_op jit(solution)/shard_map/reduce_scatter | solution.py:1540
  114.6 15.3 %copy-start.1 = (s32[1024,1]{1,0:T(8,128)}, s32[1024,1]{1,0:T(8,128)S(1)}, u32[]{:S(2)}) copy-start(s32[1024,1]{1,0:T(8,128)S(1)} %copy.24.seg_col) | copy-start | bytes 12292
  114.6 2.1 copy-start.3
  129.9 34.3 %copy-start.4 = (f32[8,1,1024]{2,1,0:T(1,128)}, f32[8,1,1024]{2,1,0:T(1,128)S(1)}, u32[]{:S(2)}) copy-start(f32[8,1,1024]{2,1,0:T(1,128)S(1)} %get-tuple-element.42.lse_ref) | copy-start | bytes 98308
  129.9 34.3 %slice-start = ((s8[8388608]{0:T(1024)(128)(4,1)}), s8[4194304]{0:T(1024)(128)(4,1)S(1)}, s32[]{:S(2)}) async-start(s8[8388608]{0:T(1024)(128)(4,1)} %bitcast.28), calls=%async_computation.3 | async-start | bytes 8388608
  129.9 34.3 %copy-start.9 = (bf16[256,2048]{1,0:T(8,128)(2,1)S(1)}, bf16[256,2048]{1,0:T(8,128)(2,1)}, u32[]{:S(2)}) copy-start(bf16[256,2048]{1,0:T(8,128)(2,1)} %param.13) | copy-start | bytes 3145732
  129.9 34.3 %slice-start.1 = ((s8[8388608]{0:T(1024)(128)(4,1)}), s8[4194304]{0:T(1024)(128)(4,1)S(1)}, s32[]{:S(2)}) async-start(s8[8388608]{0:T(1024)(128)(4,1)} %bitcast.28), calls=%async_computation.4 | async-start | bytes 8388608
  164.2 2.5 copy-start
  164.3 3.8 copy-start.20
  166.7 1.3 copy-start.5
  166.8 1.3 copy-start.26
  371.2 1.6 copy-start.6
  371.2 1.6 copy-start.21
  371.2 1.6 copy-start.27
  372.8 3.6 copy-start.11
  372.8 3.6 copy-start.12
  444.9 122.1 %copy-start.22 = (f32[2048]{0:T(1024)S(1)}, f32[2048]{0:T(1024)}, u32[]{:S(2)}) copy-start(f32[2048]{0:T(1024)} %param.14) | copy-start | bytes 24580
  445.0 122.1 %copy-start.25 = (f32[256]{0:T(256)S(1)}, f32[256]{0:T(256)}, u32[]{:S(2)}) copy-start(f32[256]{0:T(256)} %copy-done.24) | copy-start | bytes 3076
  567.0 4.5 copy-start.23
  572.3 17.8 %copy-start.7 = (f32[256,2048]{1,0:T(8,128)S(1)}, f32[256,2048]{1,0:T(8,128)}, u32[]{:S(2)}) copy-start(f32[256,2048]{1,0:T(8,128)} %copy-done.5) | copy-start | bytes 6291460
  572.4 17.8 %copy-start.10 = (bf16[256,2048]{1,0:T(8,128)(2,1)S(1)}, bf16[256,2048]{1,0:T(8,128)(2,1)}, u32[]{:S(2)}) copy-start(bf16[256,2048]{1,0:T(8,128)(2,1)} %param.13) | copy-start | bytes 3145732
  590.1 5.0 copy-start.19
  590.2 5.8 copy-start.18
  595.1 1.6 copy-start.17
  595.1 2.4 copy-start.16
  595.1 3.2 copy-start.15
  598.3 2.3 copy-start.14
  600.7 2.3 copy-start.13
Sparse Core Ops, SparseCore 0:
  114.4 101.0 all-gather.1
  371.4 93.5 reduce-scatter.1

commit v4 on v3

--- a/solution.py
+++ b/solution.py
@@ -19,7 +19,8 @@
 VM = pl.BlockSpec(memory_space=pltpu.VMEM)
 DMA = pltpu.SemaphoreType.DMA
 ZAXIS = "tensor"
-VMEM_MAX = 66_000_000
+VMEM_MAX = 67_000_000
+CHUNKS = 4
 
 
 def dot_nn(left, right):
@@ -205,6 +206,130 @@
                 @pl.when(sends)
                 def _():
                     self._copy(self.recv.at[self.slot(s, d)], s, d).wait_send()
+
+
+class ArrivalScatter:
+    def __init__(self, t, n, part, recv, send_sem, recv_sem, chunks, low=1, high=None):
+        self.t, self.n, self.part, self.recv, self.chunks = t, n, part, recv, chunks
+        self.send_sem, self.recv_sem = send_sem, recv_sem
+        self.rows = part.shape[1] // chunks
+        self.messages = range(low, n if high is None else high)
+
+    def owner(self, a, d):
+        return a + d * (self.n - 1 - 2 * a)
+
+    def slot(self, a, d):
+        s = jnp.clip(self.n - 1 - a, 0, self.n - 1)
+        return s + d * (self.n - 2 * s)
+
+    def piece(self, ref, at, c):
+        return ref.at[at, c * self.rows : (c + 1) * self.rows]
+
+    def _copy(self, src, a, d, c):
+        s = jnp.clip(self.n - 1 - a, 0, self.n - 2)
+        return pltpu.make_async_remote_copy(
+            src_ref=src,
+            dst_ref=self.piece(self.recv, self.slot(a, d), c),
+            send_sem=self.send_sem.at[d, s, c],
+            recv_sem=self.recv_sem.at[d, s, c],
+            device_id={ZAXIS: jnp.clip(self.t + 1 - 2 * d, 0, self.n - 1)},
+            device_id_type=MESH,
+        )
+
+    def first(self, a, d):
+        for c in range(self.chunks):
+            self._copy(self.piece(self.part, self.owner(a, d), c), a, d, c).start()
+
+    def relay(self, p, a, c):
+        t, n = self.t, self.n
+        d = (t != p).astype(jnp.int32)
+
+        @pl.when((t == p) | (t == n - 1 - p))
+        def _():
+            at = self.slot(a, d)
+            self._copy(self.piece(self.recv, at, c), a, d, c).wait_recv()
+            rows = slice(c * self.rows, (c + 1) * self.rows)
+            both = self.recv[at, rows].astype(F32) + self.part[self.owner(a, d), rows].astype(F32)
+            self.recv[at, rows] = both.astype(BF)
+            self._copy(self.piece(self.recv, at, c), a, d, c).start()
+
+    def groups(self):
+        for a in self.messages:
+            for slot in range(self.chunks + a - 2 if a > 1 else 0):
+                yield [(p, a, slot - p + 1) for p in range(1, a) if 0 <= slot - p + 1 < self.chunks]
+
+    def own(self):
+        t, n = self.t, self.n
+        for d, has in ((0, t > 0), (1, t < n - 1)):
+            a = t if d == 0 else n - 1 - t
+
+            @pl.when(has & (a >= self.messages.start) & (a < self.messages.stop))
+            def _():
+                for c in range(self.chunks):
+                    self._copy(self.piece(self.recv, self.slot(a, d), c), a, d, c).wait_recv()
+
+    def finish(self):
+        t, n = self.t, self.n
+        for a in self.messages:
+            for d in range(2):
+
+                @pl.when((t < a) if d == 0 else (n - 1 - t < a))
+                def _():
+                    for c in range(self.chunks):
+                        self._copy(self.piece(self.recv, self.slot(a, d), c), a, d, c).wait_send()
+
+
+class FarScatter(ArrivalScatter):
+    def stage(self, buf, sem):
+        self.buf, self.sem = buf, sem
+
+    def relay(self, p, a, c):
+        t, n = self.t, self.n
+        d = (t != p).astype(jnp.int32)
+
+        @pl.when((t == p) | (t == n - 1 - p))
+        def _():
+            arrived = self.piece(self.recv, self.slot(a, d), c)
+            self._copy(arrived, a, d, c).wait_recv()
+            pulls = [
+                pltpu.make_async_copy(arrived, self.buf.at[0], self.sem.at[0]),
+                pltpu.make_async_copy(self.piece(self.part, self.owner(a, d), c), self.buf.at[1], self.sem.at[1]),
+            ]
+            for pull in pulls:
+                pull.start()
+            for pull in pulls:
+                pull.wait()
+            self.buf[0] = (self.buf[0].astype(F32) + self.buf[1].astype(F32)).astype(BF)
+            back = pltpu.make_async_copy(self.buf.at[0], arrived, self.sem.at[0])
+            back.start()
+            back.wait()
+            self._copy(arrived, a, d, c).start()
+
+
+def emit_parts(t, n, part, recv, out, sem):
+    left_slot, right_slot = jnp.clip(n - 1 - t, 0, n - 1), n - t
+    own = pltpu.make_async_copy(part.at[t], out.at[0], sem.at[0])
+    left = pltpu.make_async_copy(recv.at[left_slot], out.at[1], sem.at[1])
+    right = pltpu.make_async_copy(recv.at[jnp.clip(right_slot, 0, n)], out.at[2], sem.at[2])
+    own.start()
+
+    @pl.when(t > 0)
+    def _():
+        left.start()
+
+    @pl.when(t < n - 1)
+    def _():
+        right.start()
+
+    own.wait()
+
+    @pl.when(t > 0)
+    def _():
+        left.wait()
+
+    @pl.when(t < n - 1)
+    def _():
+        right.wait()
 
 
 def line_total(parts, n):
@@ -525,9 +650,10 @@
     wd_ref,
     out_ref,
     dn2_ref,
-    grads_ref,
+    kept_ref,
     got_ref,
-    give_ref,
+    sums_ref,
+    far_ref,
     n2,
     cot,
     wg,
@@ -541,11 +667,17 @@
     recv,
     turned,
     spare,
+    far_buf,
     load_sem,
     out_sem,
-    grad_sem,
+    put_sem,
     ag_send,
     ag_recv,
+    cot_send,
+    cot_recv,
+    far_send,
+    far_recv,
+    far_sem,
     rs_send,
     rs_recv,
     core_send,
@@ -566,28 +698,34 @@
     strip = depth // m
     wide = min(512, units)
     line = LineGather(t, n, rows_of(n2, rows), ag_send, ag_recv)
-    ring = LineScatter(t, n, part, recv, rs_send, rs_recv)
+    cots = LineGather(t, n, rows_of(cot, rows), cot_send, cot_recv)
+    ring = ArrivalScatter(t, n, part, recv, rs_send, rs_recv, CHUNKS)
+    far = FarScatter(t, n, out_ref, far_ref, far_send, far_recv, CHUNKS, 1, n - 1)
+    far.stage(far_buf, far_sem)
     loads = [
         pltpu.make_async_copy(n2_ref, line.slot(t), load_sem.at[0]),
-        pltpu.make_async_copy(wg_ref, wg, load_sem.at[1]),
-        pltpu.make_async_copy(wu_ref, wu, load_sem.at[2]),
-        pltpu.make_async_copy(cot_ref, cot, load_sem.at[3]),
+        pltpu.make_async_copy(cot_ref, cots.slot(t), load_sem.at[1]),
+        pltpu.make_async_copy(wg_ref, wg, load_sem.at[2]),
+        pltpu.make_async_copy(wu_ref, wu, load_sem.at[3]),
         pltpu.make_async_copy(wd_ref, wd, load_sem.at[4]),
     ]
     for load in loads:
         load.start()
     greet_line(t, n, [partner] + peers)
-    loads[0].wait()
-    line.start(0, 0)
-    line.start(0, 1)
-    for load in loads[1:]:
+    for load, lines in zip(loads, (line, cots)):
         load.wait()
+        lines.start(0, 0)
+        lines.start(0, 1)
+    for load in loads[2:]:
+        load.wait()
+
+    def take(s):
+        for lines in (line, cots):
+            for d in range(2):
+                lines.take(s, d)
 
     def place(shard):
         return pl.ds(pl.multiple_of(shard * rows, rows), rows)
-
-    def flush(shard):
-        return pltpu.make_async_copy(obuf, out_ref.at[place(shard)], out_sem)
 
     def up_half(shard):
         at = place(shard)
@@ -606,12 +744,8 @@
 
         lax.fori_loop(0, units // wide, body, 0)
 
-    def down_half(shard, first):
+    def down_half(shard):
         at = place(shard)
-
-        @pl.when(jnp.logical_not(first))
-        def _():
-            flush(shard).wait()
 
         def body(i, carry):
             cols = pl.ds(pl.multiple_of(i * 512, 512), 512)
@@ -620,7 +754,9 @@
             return carry
 
         lax.fori_loop(0, depth // 512, body, 0)
-        flush(shard).start()
+        flush = pltpu.make_async_copy(obuf, out_ref.at[shard], out_sem)
+        flush.start()
+        flush.wait()
 
     def event(e, carry):
         es = jnp.maximum(e - 1, 0)
@@ -635,36 +771,33 @@
 
         @pl.when((e > 0) & (d == 1) & two)
         def _():
-            line.take(s + 1, 0)
-            line.take(s + 1, 1)
+            take(s + 1)
 
         @pl.when(valid)
         def _():
-            down_half(shard, e == 0)
+            down_half(shard)
+
+        for end, d_end in ((0, 0), (n - 1, 1)):
+
+            @pl.when(valid & (e > 0) & (t == end))
+            def _():
+                ring.first(s + 1, d_end)
+
+            @pl.when(valid & (e > 0) & (t == end) & (s < n - 2))
+            def _():
+                far.first(s + 1, d_end)
 
         @pl.when(e == 0)
         def _():
-            line.take(0, 0)
-            line.take(0, 1)
+            take(0)
 
         @pl.when((e > 0) & (d == 1) & jnp.logical_not(two))
         def _():
-            line.take(s + 1, 0)
-            line.take(s + 1, 1)
+            take(s + 1)
 
         return carry
 
     lax.fori_loop(0, 2 * n - 1, event, 0)
-
-    for s in range(n - 1):
-
-        @pl.when(t == 0)
-        def _():
-            ring.first(s, 0)
-
-        @pl.when(t == n - 1)
-        def _():
-            ring.first(s, 1)
 
     pl.semaphore_signal(ready, inc=1, device_id={"dp": partner}, device_id_type=MESH)
     pl.semaphore_wait(ready, 1)
@@ -693,32 +826,32 @@
         size = strip // 2
         return store.at[pl.ds(pl.multiple_of((pairs + k) * strip + side * size, size), size)]
 
-    def put(which, store, k, side):
+    def keep(store, k, side):
         at = short(k, side)
-        return pltpu.make_async_copy(
-            source(store, k, side), grads_ref.at[side, at, which], grad_sem.at[which, at, side]
-        )
-
-    def give(which, store, k, side):
+        return pltpu.make_async_copy(source(store, k, side), kept_ref.at[side, at], put_sem.at[0, k, side])
+
+    def give(store, k, side):
         at = short(k, side)
         return pltpu.make_async_remote_copy(
             src_ref=source(store, k, side),
-            dst_ref=got_ref.at[side, at, which],
-            send_sem=chip_send.at[which, at, side],
-            recv_sem=chip_recv.at[which, at, side],
+            dst_ref=got_ref.at[side, at],
+            send_sem=chip_send.at[at, side],
+            recv_sem=chip_recv.at[at, side],
             device_id={"dp": peers[side]},
             device_id_type=MESH,
         )
 
-    def leave(store, k, side):
-        at = short(k, side)
-        return pltpu.make_async_copy(source(store, k, side), give_ref.at[side, at], chip_send.at[2, at, side])
-
     def moves(which, store, k):
         for side in range(2):
+            if which:
+                copy = pltpu.make_async_copy(
+                    source(store, k, side), sums_ref.at[which - 1, side, k], put_sem.at[which, k, side]
+                )
+                yield k >= 0, copy
+                continue
             mine = chip_bit(k, side) == chip_bit(index // 2, side)
-            yield mine, put(which, store, k, side)
-            yield jnp.logical_not(mine), leave(store, k, side) if which == 2 else give(which, store, k, side)
+            yield mine, keep(store, k, side)
+            yield jnp.logical_not(mine), give(store, k, side)
 
     def pass_on(which, store, k):
         for here, copy in moves(which, store, k):
@@ -727,51 +860,95 @@
             def _():
                 copy.start()
 
+    down_store = wd if wd.shape == (depth, units) else spare
+    stores = (wg, wu, down_store)
+    sides = ((n2, ((0, dgate), (1, dup))), (cot, ((2, hid),)))
+
     def weight_grad(left, rights, mine):
-        def outer(k, carry):
-            q = 2 * k + (core if mine else 1 - core)
-            turned[...] = left[:, pl.ds(pl.multiple_of(q * strip, strip), strip)].T
+        steps = units // wide
+        tall = n * rows // steps
+
+        def turn(place, q, j):
+            tokens = pl.ds(pl.multiple_of(j * tall, tall), tall)
+            columns = pl.ds(pl.multiple_of(q * strip, strip), strip)
+            turned[place, :, tokens] = left[tokens, columns].T
+
+        def begin():
+            if not mine:
+                for j in range(steps):
+                    turn(0, 1 - core, j)
+
+        def strip_of(k, carry):
+            now, later = k % 2, (k + 1) % 2
+            if mine:
+                upcoming = 2 * jnp.minimum(k + 1, pairs - 1) + core
+            else:
+                upcoming = jnp.where(k < pairs - 1, 2 * (k + 1) + 1 - core, core)
             slot = pairs + k if mine else k
             at = pl.ds(pl.multiple_of(slot * strip, strip), strip)
-            if mine:
-                for which, right, store in rights:
+            for number, (which, right) in enumerate(rights):
+                store = stores[which]
+                if mine:
                     cross(which, store, k).wait_recv()
 
-            def inner(j, c):
-                cols = pl.ds(pl.multiple_of(j * wide, wide), wide)
-                for which, right, store in rights:
-                    value = dot_nn(turned[...], right[:, cols])
+                def inner(j, c):
+                    cols = pl.ds(pl.multiple_of(j * wide, wide), wide)
+                    value = dot_nn(turned[now], right[:, cols])
                     if mine:
                         value = value + store[at, cols].astype(F32)
                     store[at, cols] = value.astype(BF)
-                return c
-
-            lax.fori_loop(0, units // wide, inner, 0)
-            for which, right, store in rights:
+                    if number == 0:
+                        turn(later, upcoming, j)
+                    return c
+
+                lax.fori_loop(0, steps, inner, 0)
                 if mine:
                     pass_on(which, store, k)
                 else:
                     cross(which, store, k).start()
             return carry
 
-        return outer
-
-    down_store = wd if wd.shape == (depth, units) else spare
-    both = ((0, dgate, wg), (1, dup, wu))
-    down = ((2, hid, down_store),)
-    lax.fori_loop(0, pairs, weight_grad(n2, both, False), 0)
-    lax.fori_loop(0, pairs, weight_grad(n2, both, True), 0)
-    for tau in range(1, n):
-        ring.step(tau)
-        if tau < 3:
-            lax.fori_loop(0, pairs, weight_grad(cot, down, tau == 2), 0)
-    ring.emit(dn2_ref, sum_sem)
+        return begin, strip_of
+
+    work = [weight_grad(left, rights, mine) for left, rights in sides for mine in (False, True)]
+    total = len(work) * pairs
+
+    def run(lo, hi):
+        for i, (begin, unit) in enumerate(work):
+            first, last = max(lo - i * pairs, 0), min(hi - i * pairs, pairs)
+            if first < last:
+                if first == 0:
+                    begin()
+                lax.fori_loop(first, last, unit, 0)
+
+    batches = []
+    upto = {}
+    for a in range(2, n):
+        near = [[(ring, relay) for relay in group] for group in ring.groups() if group[0][1] == a]
+        wide_ring = [[(far, relay) for relay in group] for group in far.groups() if group[0][1] == a]
+        if a == 2:
+            near, wide_ring = [sum(near, [])], [sum(wide_ring, [])]
+            upto = {0: 2 * pairs, 1: 3 * pairs}
+        batches += near + wide_ring
+    done = pairs
+    run(0, done)
+    for i, batch in enumerate(batches):
+        for which, (p, a, c) in batch:
+            which.relay(p, a, c)
+        if i in upto:
+            run(done, upto[i])
+            done = upto[i]
+    run(done, total)
+    ring.own()
+    emit_parts(t, n, part, recv, dn2_ref, sum_sem)
+    far.own()
     line.finish()
+    cots.finish()
     ring.finish()
-    flush(0).wait()
+    far.finish()
 
     def settle(k, carry):
-        for which, store in ((0, wg), (1, wu), (2, down_store)):
+        for which, store in enumerate(stores):
             cross(which, store, k).wait_send()
             for here, copy in moves(which, store, k):
 
@@ -791,14 +968,15 @@
     return pl.pallas_call(
         functools.partial(mlp_kernel, m, n),
         out_shape=[
-            jax.ShapeDtypeStruct((n * rows, depth), BF),
+            jax.ShapeDtypeStruct((n, rows, depth), BF),
             jax.ShapeDtypeStruct((3, rows, depth), BF),
-            jax.ShapeDtypeStruct((2, m // 4, 3, depth // m // 2, units), BF),
-            jax.ShapeDtypeStruct((2, m // 4, 2, depth // m // 2, units), BF),
             jax.ShapeDtypeStruct((2, m // 4, depth // m // 2, units), BF),
+            jax.ShapeDtypeStruct((2, m // 4, depth // m // 2, units), BF),
+            jax.ShapeDtypeStruct((2, 2, m // 2, depth // m // 2, units), BF),
+            jax.ShapeDtypeStruct((n + 1, rows, depth), BF),
         ],
         in_specs=[HBM] * 5,
-        out_specs=[HBM] * 5,
+        out_specs=[HBM] * 6,
         scratch_shapes=[
             pltpu.VMEM((n * rows, depth), BF),
             pltpu.VMEM((n * rows, depth), BF),
@@ -811,19 +989,25 @@
             pltpu.VMEM((rows, depth), BF),
             pltpu.VMEM((n, rows, depth), BF),
             pltpu.VMEM((n + 1, rows, depth), BF),
-            pltpu.VMEM((depth // m, n * rows), BF),
+            pltpu.VMEM((2, depth // m, n * rows), BF),
             pltpu.VMEM(spare, BF),
+            pltpu.VMEM((2, rows // CHUNKS, depth), BF),
             DMA((5,)),
             DMA,
-            DMA((3, m // 4, 2)),
+            DMA((3, m // 2, 2)),
             DMA((2, n - 1)),
             DMA((2, n - 1)),
             DMA((2, n - 1)),
             DMA((2, n - 1)),
+            DMA((2, n - 1, CHUNKS)),
+            DMA((2, n - 1, CHUNKS)),
+            DMA((2,)),
+            DMA((2, n - 1, CHUNKS)),
+            DMA((2, n - 1, CHUNKS)),
             DMA((3, m // 2)),
             DMA((3, m // 2)),
-            DMA((3, m // 4, 2)),
-            DMA((2, m // 4, 2)),
+            DMA((m // 4, 2)),
+            DMA((m // 4, 2)),
             DMA((3,)),
             pltpu.SemaphoreType.REGULAR,
         ],
@@ -902,12 +1086,14 @@
     sin_ref,
     kept_ref,
     got_ref,
-    give_ref,
+    sums_ref,
+    part_ref,
     dq_ref,
     dk_ref,
     dv_ref,
     out_ref,
     mlp_ref,
+    far_ref,
     wo,
     outgoing,
     grads,
@@ -916,6 +1102,10 @@
     inbox,
     kept,
     got,
+    ups,
+    up_inbox,
+    part,
+    far_in,
     dk_sum,
     dv_sum,
     wo_sem,
@@ -926,8 +1116,11 @@
     core_recv,
     chip_send,
     chip_recv,
-    down_send,
-    down_recv,
+    up_send,
+    up_recv,
+    far_send,
+    far_recv,
+    far_sem,
     put_sem,
 ):
     t = lax.axis_index(ZAXIS)
@@ -938,7 +1131,6 @@
     width = grads.shape[0]
     strip = depth // m
     half = strip // 2
-    peers = [flip(index, 1), flip(index, m.bit_length() - 2)]
 
     def wo_rows(z):
         return pl.ds(pl.multiple_of(z * width, width), width)
@@ -949,12 +1141,11 @@
 
     for s in range(1, n + 1):
         load_wo(s).start()
-    loads = [pltpu.make_async_copy(kept_ref, kept, load_sem.at[0])]
-    for side in range(2):
-        for j in range(m // 4):
-            loads.append(
-                pltpu.make_async_copy(got_ref.at[side, j], got.at[side, j, 0:2], load_sem.at[1 + side * (m // 4) + j])
-            )
+    loads = [
+        pltpu.make_async_copy(sums_ref.at[0], ups, load_sem.at[0]),
+        pltpu.make_async_copy(kept_ref, kept, load_sem.at[1]),
+        pltpu.make_async_copy(got_ref, got, load_sem.at[2]),
+    ]
     for load in loads:
         load.start()
     barrier = pltpu.get_barrier_semaphore()
@@ -964,20 +1155,13 @@
     for partner in partners:
         pl.semaphore_signal(barrier, inc=1, device_id={"dp": partner}, device_id_type=MESH)
     pl.semaphore_wait(barrier, n - 1 + len(partners))
-
-    def down(side, j):
-        return pltpu.make_async_remote_copy(
-            src_ref=give_ref.at[side, j],
-            dst_ref=got.at[side, j, 2],
-            send_sem=down_send.at[side, j],
-            recv_sem=down_recv.at[side, j],
-            device_id={"dp": peers[side]},
-            device_id_type=MESH,
-        )
-
-    for side in range(2):
-        for j in range(m // 4):
-            down(side, j).start()
+    far = ArrivalScatter(t, n, part, far_in, far_send, far_recv, CHUNKS, n - 1)
+    load_part = pltpu.make_async_copy(part_ref, part, far_sem)
+    load_part.start()
+
+    up_chips = ChipSum(m, index, lambda side, k: ups.at[side, k], up_inbox, up_send, up_recv)
+    loads[0].wait()
+    up_chips.start(0)
 
     def token_cols(z):
         return pl.ds(pl.multiple_of(z * rows, rows), rows)
@@ -1013,6 +1197,13 @@
             z_copy(s).start()
         else:
             grads[:, token_cols(t)] = block
+
+    load_part.wait()
+    for d, end in ((0, 0), (1, n - 1)):
+
+        @pl.when(t == end)
+        def _():
+            far.first(n - 1, d)
 
     def cross(k):
         return pltpu.make_async_remote_copy(
@@ -1048,25 +1239,23 @@
     lax.fori_loop(0, pairs, weight_grad(False), 0)
     lax.fori_loop(0, pairs, weight_grad(True), 0)
     chips.start(0)
-    for load in loads:
+    for load in loads[1:]:
         load.wait()
 
-    def put_mlp(side, j, which):
-        return pltpu.make_async_copy(
-            kept.at[side, j, which], mlp_ref.at[side, j, which], put_sem.at[which, side, j]
-        )
-
-    def settle(which):
-        for side in range(2):
-            for j in range(m // 4):
-                if which == 2:
-                    down(side, j).wait_recv()
-                both = kept[side, j, which].astype(F32) + got[side, j, which].astype(F32)
-                kept[side, j, which] = both.astype(BF)
-                put_mlp(side, j, which).start()
-
-    settle(0)
-    settle(1)
+    def put_mlp(which, source, side, place, j):
+        return pltpu.make_async_copy(source, mlp_ref.at[which, side, place], put_sem.at[which, side, j])
+
+    def put_gate(side, j):
+        return put_mlp(0, kept.at[side, j], side, j, j)
+
+    def put_up(side, k, j):
+        return put_mlp(1, ups.at[side, k], side, k // 2 if side == 0 else k % (pairs // 2), j)
+
+    for side in range(2):
+        for j in range(m // 4):
+            both = kept[side, j].astype(F32) + got[side, j].astype(F32)
+            kept[side, j] = both.astype(BF)
+            put_gate(side, j).start()
     for s in range(1, n):
         z_arrive(s).wait_recv()
 
@@ -1076,12 +1265,19 @@
         )
         return carry
 
-    lax.fori_loop(0, width // HEAD_DIM, head, 0)
-    settle(2)
+    heads = width // HEAD_DIM
+    groups = list(far.groups())
+    for i, group in enumerate(groups):
+        lax.fori_loop(heads * i // (len(groups) - 1), min(heads * (i + 1) // (len(groups) - 1), heads), head, 0)
+        for relay in group:
+            far.relay(*relay)
+    up_chips.take(0, None)
+    for side, k, j, _ in up_chips.copies(0):
+        put_up(side, k, j).start()
 
     def put_out(side, kept_k, j):
         place = kept_k // 2 if side == 0 else kept_k % (pairs // 2)
-        return pltpu.make_async_copy(chips.block(side, kept_k), out_ref.at[side, place], put_sem.at[3, side, j])
+        return pltpu.make_async_copy(chips.block(side, kept_k), out_ref.at[side, place], put_sem.at[2, side, j])
 
     chips.take(0, None)
     for side, k, j, _ in chips.copies(0):
@@ -1093,23 +1289,32 @@
         z_copy(s).wait_send()
     for k in range(pairs):
         cross(k).wait_send()
-    for side in range(2):
-        for j in range(m // 4):
-            down(side, j).wait_send()
-            for which in range(3):
-                put_mlp(side, j, which).wait()
-
-
-def back(m, n, branch, wo, ctx, qkv, lse, seg_row, seg_col, cosine, sine, kept, got, give):
+    for side, k, j, copy in up_chips.copies(0):
+        put_up(side, k, j).wait()
+        put_gate(side, j).wait()
+        copy.wait_send()
+    far.own()
+    far.finish()
+    for place, (end, slot) in enumerate(((n - 1, 0), (0, n))):
+
+        @pl.when(t == end)
+        def _():
+            last = pltpu.make_async_copy(far_in.at[slot], far_ref.at[place], far_sem)
+            last.start()
+            last.wait()
+
+
+def back(m, n, branch, wo, ctx, qkv, lse, seg_row, seg_col, cosine, sine, kept, got, sums, part):
     rows, depth = branch.shape
     width, length = qkv.shape[0] // 3, qkv.shape[1]
     strip = depth // m
     return pl.pallas_call(
         functools.partial(back_kernel, m, n),
         out_shape=[jax.ShapeDtypeStruct((width, length), BF)] * 3
-        + [jax.ShapeDtypeStruct((2, m // 4, strip // 2, depth), BF), jax.ShapeDtypeStruct(kept.shape, BF)],
-        in_specs=[VM, HBM] + [VM] * 7 + [HBM] * 3,
-        out_specs=[VM] * 3 + [HBM] * 2,
+        + [jax.ShapeDtypeStruct((2, m // 4, strip // 2, depth), BF), jax.ShapeDtypeStruct((2,) + kept.shape, BF)]
+        + [jax.ShapeDtypeStruct((2, rows, depth), BF)],
+        in_specs=[VM, HBM] + [VM] * 7 + [HBM] * 4,
+        out_specs=[VM] * 3 + [HBM] * 3,
         scratch_shapes=[
             pltpu.VMEM(wo.shape, BF),
             pltpu.VMEM((n, width, rows), BF),
@@ -1119,10 +1324,14 @@
             pltpu.VMEM((2, m // 4, strip // 2, depth), BF),
             pltpu.VMEM(kept.shape, BF),
             pltpu.VMEM(kept.shape, BF),
+            pltpu.VMEM(sums.shape[1:], BF),
+            pltpu.VMEM(kept.shape, BF),
+            pltpu.VMEM(part.shape, BF),
+            pltpu.VMEM((n + 1, rows, depth), BF),
             pltpu.VMEM((HEAD_DIM, length), F32),
             pltpu.VMEM((HEAD_DIM, length), F32),
             DMA((n,)),
-            DMA((1 + m // 2,)),
+            DMA((3,)),
             DMA((n - 1,)),
             DMA((n - 1,)),
             DMA((m // 2,)),
@@ -1131,12 +1340,15 @@
             DMA((2, m // 4)),
             DMA((2, m // 4)),
             DMA((2, m // 4)),
-            DMA((4, 2, m // 4)),
+            DMA((2, n - 1, CHUNKS)),
+            DMA((2, n - 1, CHUNKS)),
+            DMA,
+            DMA((3, 2, m // 4)),
         ],
         compiler_params=pltpu.CompilerParams(collective_id=2, has_side_effects=True, vmem_limit_bytes=VMEM_MAX),
         cost_estimate=cost(55),
         name="back",
-    )(branch, wo, ctx, qkv, lse, seg_row, seg_col, cosine, sine, kept, got, give)
+    )(branch, wo, ctx, qkv, lse, seg_row, seg_col, cosine, sine, kept, got, sums, part)
 
 
 def input_kernel(
@@ -1151,6 +1363,7 @@
     full_ref,
     half_ref,
     mlp_ref,
+    sums_ref,
     dn1_ref,
     qs_ref,
     ks_ref,
@@ -1172,6 +1385,8 @@
     out_total,
     mlp_half,
     mlp_inbox,
+    downs,
+    down_inbox,
     load_sem,
     send_sem,
     recv_sem,
@@ -1185,6 +1400,8 @@
     oz_recv,
     mc_send,
     mc_recv,
+    dc_send,
+    dc_recv,
     sum_sem,
 ):
     t = lax.axis_index(ZAXIS)
@@ -1214,22 +1431,22 @@
             m, index, block, mlp_inbox.at[which], mc_send.at[which], mc_recv.at[which], begin=1
         )
 
-    matrices = [mlp_chips(which) for which in range(3)]
-    load_mlp = [
-        pltpu.make_async_copy(mlp_ref.at[:, :, which], mlp_half.at[which], load_sem.at[2 + which]) for which in range(3)
-    ]
+    down_chips = ChipSum(m, index, lambda side, k: downs.at[side, k], down_inbox, dc_send, dc_recv)
+    matrices = [mlp_chips(0), mlp_chips(1), down_chips]
+    load_mlp = pltpu.make_async_copy(mlp_ref, mlp_half, load_sem.at[2])
+    load_down = pltpu.make_async_copy(sums_ref.at[1], downs, load_sem.at[3])
     load = pltpu.make_async_copy(full_ref, full, load_sem.at[0])
     load_half = pltpu.make_async_copy(half_ref, out_half, load_sem.at[1])
     load_half.start()
-    for load_one in load_mlp:
-        load_one.start()
+    load_down.start()
+    load_mlp.start()
     load.start()
     greet_line(t, n, [flip(index, bit) for bit in range(m.bit_length() - 1)])
     load_half.wait()
     out_chips.start(1)
-    for load_one in load_mlp:
-        load_one.wait()
-    matrices[0].start(1)
+    load_down.wait()
+    down_chips.start(0)
+    load_mlp.wait()
 
     def body(k, carry):
         owner = jnp.where(t == n - 1, k, n - 1 - k)
@@ -1284,8 +1501,8 @@
     lax.fori_loop(0, pairs, weight_grad(False), 0)
     lax.fori_loop(0, pairs, weight_grad(True), 0)
     chips.start(0)
+    matrices[0].start(1)
     matrices[1].start(1)
-    matrices[2].start(1)
     ring.step(1)
 
     def hand_matrix(which):
@@ -1327,6 +1544,8 @@
         ring.step(tau)
         out_ring.step(tau - 1)
         i = tau - 2
+        if i == 0:
+            take_matrix(2, 0)
         if i < chips.stages:
             chips.take(i, hand_qkv)
             if i + 1 < chips.stages:
@@ -1361,7 +1580,7 @@
         cross(k).wait_send()
 
 
-def input_back(m, n, dq, dk, dv, wq, wk, wv, full, out_halves, mlp_halves):
+def input_back(m, n, dq, dk, dv, wq, wk, wv, full, out_halves, mlp_halves, sums):
     depth, width = wq.shape
     units = mlp_halves.shape[-1]
     rows = dq.shape[1] // n
@@ -1373,7 +1592,7 @@
         + [jax.ShapeDtypeStruct((width, strip), F32)]
         + [jax.ShapeDtypeStruct((strip, units), F32)] * 2
         + [jax.ShapeDtypeStruct((units, strip), F32)],
-        in_specs=[VM] * 6 + [HBM] * 3,
+        in_specs=[VM] * 6 + [HBM] * 4,
         out_specs=[HBM] + [VM] * 7,
         scratch_shapes=[
             pltpu.VMEM((n, rows, depth), BF),
@@ -1387,9 +1606,11 @@
             pltpu.VMEM((n, strip, width), BF),
             pltpu.VMEM((n + 1, strip, width), BF),
             pltpu.VMEM((strip, width), F32),
-            pltpu.VMEM((3, 2, m // 4, strip // 2, units), BF),
-            pltpu.VMEM((3, 2, m // 4 - 1, strip // 2, units), BF),
-            DMA((5,)),
+            pltpu.VMEM(mlp_halves.shape, BF),
+            pltpu.VMEM((2, 2, m // 4 - 1, strip // 2, units), BF),
+            pltpu.VMEM(sums.shape[1:], BF),
+            pltpu.VMEM((2, m // 2 - 1, strip // 2, units), BF),
+            DMA((4,)),
             DMA((2, n - 1)),
             DMA((2, n - 1)),
             DMA((m // 2,)),
@@ -1400,14 +1621,16 @@
             DMA((2, m // 4 - 1)),
             DMA((2, n - 1)),
             DMA((2, n - 1)),
-            DMA((3, 2, m // 4 - 1)),
-            DMA((3, 2, m // 4 - 1)),
+            DMA((2, 2, m // 4 - 1)),
+            DMA((2, 2, m // 4 - 1)),
+            DMA((2, m // 2 - 1)),
+            DMA((2, m // 2 - 1)),
             DMA((3,)),
         ],
         compiler_params=pltpu.CompilerParams(collective_id=4, has_side_effects=True, vmem_limit_bytes=VMEM_MAX),
         cost_estimate=cost(95),
         name="input_back",
-    )(dq, dk, dv, wq, wk, wv, full, out_halves, mlp_halves)
+    )(dq, dk, dv, wq, wk, wv, full, out_halves, mlp_halves, sums)
 
 
 def gains_kernel(m, n, x_ref, o_ref, z_in, total, dp_in, z_send, z_recv, dp_send, dp_recv):
@@ -1527,32 +1750,48 @@
         m, n, normed_one, query_weight, key_weight, value_weight, cosine, sine, strip
     )
     out_full = out_full.reshape(n * m * piece, depth)
-    full_grad = lax.all_gather(after(out_cotangent, qkv), ZAXIS, axis=0, tiled=True)
     context, lse = attend(qkv, seg_row, seg_col)
     context_all = swap(n, context)
     mid = resid + dot_tn(context_all, out_full)
     scaled_two, inverse_two = norm_stats(mid)
     normed_two = (scaled_two * mlp_gain).astype(BF)
 
-    out_part, grad_two_parts, mlp_kept, mlp_got, down_give = mlp(
-        m, n, normed_two, full_grad, gate_weight, up_weight, down_weight
+    out_part, grad_two_parts, gate_kept, gate_got, mlp_sums, out_got = mlp(
+        m, n, normed_two, out_cotangent, gate_weight, up_weight, down_weight
     )
-    out_sum = lax.psum_scatter(out_part, ZAXIS, scatter_dimension=0, tiled=True)
+    t = lax.axis_index(ZAXIS)
+    pick = lambda parts, i: lax.dynamic_index_in_dim(parts, i, 0, keepdims=False)
     grad_normed_two = line_total(grad_two_parts, n)
     grad_mid_norm, gain_two_part = norm_back(grad_normed_two, scaled_two, inverse_two, mlp_gain)
     grad_mid = out_cotangent.astype(F32) + grad_mid_norm
     branch = grad_mid.astype(BF)
-    dq, dk, dv, out_halves, mlp_halves = back(
-        m, n, branch, out_full, context_all, qkv, lse, seg_row, seg_col, cosine, sine, mlp_kept, mlp_got, down_give
+    dq, dk, dv, out_halves, mlp_halves, out_far = back(
+        m,
+        n,
+        branch,
+        out_full,
+        context_all,
+        qkv,
+        lse,
+        seg_row,
+        seg_col,
+        cosine,
+        sine,
+        gate_kept,
+        gate_got,
+        mlp_sums,
+        out_part,
     )
+    from_left = jnp.where(t == n - 1, out_far[0], pick(out_got, jnp.clip(n - 1 - t, 0, n)))
+    from_right = jnp.where(t == 0, out_far[1], pick(out_got, n - t))
+    block_out = (mid + line_total((pick(out_part, t), from_left, from_right), n)).astype(BF)
     grad_one_parts, query_sum, key_sum, value_sum, output_sum, gate_sum, up_sum, down_sum = input_back(
-        m, n, dq, dk, dv, query_weight, key_weight, value_weight, full_one, out_halves, mlp_halves
+        m, n, dq, dk, dv, query_weight, key_weight, value_weight, full_one, out_halves, mlp_halves, mlp_sums
     )
     grad_normed_one = line_total(grad_one_parts, n)
     grad_in_norm, gain_one_part = norm_back(grad_normed_one, scaled_one, inverse_one, attn_gain)
     input_grad = (grad_mid + grad_in_norm).astype(BF)
     gain_one_sum, gain_two_sum = reduce_gains(m, n, gain_one_part, gain_two_part)
-    block_out = (mid + after(out_sum, grad_normed_one).astype(F32)).astype(BF)
     return (
         block_out,
         input_grad,

time: 612 us -> 591 us (0.966); the launches traced: 611 us -> 583 us
  waiting for transfers between devices: 46.3 us -> 0 us
  Pallas kernels: 507 us -> 536 us
  between operations: 14.4 us -> 1.48 us
    pallas_call x1, Pallas kernels: 156 us -> 214 us  [mlp(): pl.pallas_call(functools.partial(mlp_kernel, m, n), out_shape=[jax.ShapeD...]
    all_gather x1 -> x0, waiting for transfers between devices: 46.3 us -> none  [local(): lax.all_gather(after(out_cotangent, qkv), ZAXIS, axis=0, tiled=True)]
    pallas_call x1, Pallas kernels: 34.3 us -> 18.1 us  [swap(): pl.pallas_call(functools.partial(swap_kernel, n), out_shape=jax.ShapeDtyp...]
    pallas_call x1, Pallas kernels: 122 us -> 106 us  [input_back(): pl.pallas_call(functools.partial(input_kernel, m, n), out_shape=[jax.Shap...]
  transfers between devices with their start and end apart: 2 -> 0, of which waited for: 1 -> 0; matrix products, arithmetic and copies ran while one was open for 3% -> 0% of each run, Pallas kernels for 41% -> 0%
where the time goes in v4:
time: 591 us; the launch traced here: 583 us
  Pallas kernels  536 us (91%)
  other arithmetic  24.7 us (4%)
  local copies, waits for them, and re-layouts  17.4 us (3%)
    pallas_call x1, Pallas kernels, mlp(): pl.pallas_call(functools.partial(mlp_kernel, m, n), out_shape=[jax.ShapeD...  214 us
    pallas_call x1, Pallas kernels, input_back(): pl.pallas_call(functools.partial(input_kernel, m, n), out_shape=[jax.Shap...  106 us
    pallas_call x1, Pallas kernels, gather_qkv(): pl.pallas_call(functools.partial(qkv_kernel, m, n), out_shape=[jax.ShapeD...  99.9 us
    pallas_call x1, Pallas kernels, back(): pl.pallas_call(functools.partial(back_kernel, m, n), out_shape=[jax.Shape...  71.3 us
    pallas_call x1, Pallas kernels, swap(): pl.pallas_call(functools.partial(swap_kernel, n), out_shape=jax.ShapeDtyp...  18.1 us
    pallas_call x1, Pallas kernels, reduce_gains(): pl.pallas_call(functools.partial(gains_kernel, m, n), out_shape=jax.Shape...  13.5 us
    unnamed x67, local copies, waits for them, and re-layouts  13.2 us
    pallas_call x1, Pallas kernels, attend(): pl.pallas_call(functools.partial(attend_kernel, 512), grid=(heads,), in_s...  13.2 us

profile of v4, /device:TPU:0, one launch (start us, length us, event | category | flops | bytes accessed | tf_op | source)
XLA Modules:
  0.0 582.5 jit_solution(485605629871845833)
XLA Ops:
  0.7 1.8 constant_dynamic-slice_fusion.strip_ref
  2.4 1.5 fusion.11
  4.0 2.0 fusion.4.n1_ref
  6.0 1.2 multiply_sine_fusion
  7.2 99.9 %gather_qkv.1 = (bf16[1024,2048]{1,0:T(8,128)(2,1)}, bf16[1536,1024]{1,0:T(8,128)(2,1)}, bf16[4,8,64,2048]{3,2,1,0:T(8,128)(2,1)}) custom-call(bf16[256,2048]{1,0:T(8,128)(2,1)} %fusion.4.n1_ref, bf16[2048,512]{1,0:T(8,128)(2,1)} %wq.3, bf16[2048,512]{1,0:T(8,128)(2,1)} %wk.3, bf16[2048,512]{1,0:T(8,128)(2,1)} %wv.3, f32[32,1024]{1,0:T(8,128)} %get-tuple-element.68.cos_ref, ...), custom_call_target="tpu_custom_call" | custom-call | flops 89999998976 | bytes 1048576 | tf_op jit(solution)/shard_map/gather_qkv/pallas_call | solution.py:496
  107.1 0.2 copy.24.seg_col
  107.4 2.1 copy-done.3
  109.4 13.2 %attend.1 = (bf16[512,1024]{1,0:T(8,128)(2,1)S(1)}, f32[8,1,1024]{2,1,0:T(1,128)S(1)}) custom-call(bf16[1536,1024]{1,0:T(8,128)(2,1)S(1)} %copy-done.3, bf16[1536,1024]{1,0:T(8,128)(2,1)S(1)} %copy-done.3, bf16[1536,1024]{1,0:T(8,128)(2,1)S(1)} %copy-done.3, s32[1,1024]{1,0:T(1,128)S(1)} %bitcast.34, s32[1024,1]{1,0:T(8,128)S(1)} %copy.24.seg_col), custom_call_target="tpu_custom_call" | custom-call | flops 12999999488 | bytes 1048576 | tf_op jit(solution)/shard_map/attend/pallas_call | solution.py:549
  122.7 18.1 %swap_out.1.ctx_ref = bf16[2048,256]{1,0:T(8,128)(2,1)S(1)} custom-call(bf16[512,1024]{1,0:T(8,128)(2,1)S(1)} %get-tuple-element.37.x_ref), custom_call_target="tpu_custom_call" | custom-call | flops 24999999488 | bytes 1048576 | tf_op jit(solution)/shard_map/swap_out/pallas_call | solution.py:631
  140.9 2.4 multiply_reduce_fusion.1
  143.4 1.3 copy-done.5
  144.7 0.6 copy-done.25
  145.3 1.2 multiply_convert_fusion.n2_ref
  146.5 214.4 %mlp.1 = (bf16[4,256,2048]{2,1,0:T(8,128)(2,1)}, bf16[3,256,2048]{2,1,0:T(8,128)(2,1)}, bf16[2,2,128,2048]{3,2,1,0:T(8,128)(2,1)}, bf16[2,2,128,2048]{3,2,1,0:T(...) custom-call(bf16[256,2048]{1,0:T(8,128)(2,1)} %multiply_convert_fusion.n2_ref, ...), custom_call_target="tpu_custom_call" | custom-call | flops 154999996416 | bytes 1048576 | tf_op jit(solution)/shard_map/mlp/pallas_call | solution.py:968
  360.9 4.2 fusion.13
  365.1 4.2 fusion.14
  369.3 71.3 %back.1 = (bf16[512,1024]{1,0:T(8,128)(2,1)}, bf16[512,1024]{1,0:T(8,128)(2,1)}, bf16[512,1024]{1,0:T(8,128)(2,1)}, bf16[2,2,128,2048]{3,2,1,0:T(8,128)(2,1)}, b...) custom-call(bf16[256,2048]{1,0:T(8,128)(2,1)} %get-tuple-element.65.branch_ref, ...), custom_call_target="tpu_custom_call" | custom-call | flops 54999998464 | bytes 1048576 | tf_op jit(solution)/shard_map/back/pallas_call | solution.py:1311
  440.7 106.1 %input_back.1 = (bf16[3,256,2048]{2,1,0:T(8,128)(2,1)}, f32[256,512]{1,0:T(8,128)}, f32[256,512]{1,0:T(8,128)}, f32[256,512]{1,0:T(8,128)}, f32[512,256]{1,0:T(8...) custom-call(bf16[512,1024]{1,0:T(8,128)(2,1)} %get-tuple-element.47.dq_ref, ...), custom_call_target="tpu_custom_call" | custom-call | flops 95000002560 | bytes 1048576 | tf_op jit(solution)/shard_map/input_back/pallas_call | solution.py:1588
  546.8 6.3 %fusion.10 = (f32[2048]{0:T(1024)S(1)}, f32[256]{0:T(256)S(1)}, bf16[256,2048]{1,0:T(8,128)(2,1)}) fusion(bf16[256,2048]{1,0:T(8,128)(2,1)} %param.13, f32[256]{0:T(256)S(1)} %copy-done.24, bf16[3,256,2048]{2,1,0:T(8,128)(2,1)} %get-tuple-element.53, pred[]{:T(512)S(6)} %lt.19, pred[]{:T(512)S(6)} %gt.2, f32[2048]{0:T(1024)S(1)} %copy-done.21, ...), kind=kLoop, calls=%fused_computation.13 | loop fusion | flops 13104896 | bytes 12601360 | tf_op jit(solution)/shard_map/reduce_sum | solution.py:46
  553.3 0.7 pad.4.x_ref
  554.0 13.5 %gains.1 = f32[8,128]{1,0:T(8,128)} custom-call(f32[4,8,8,128]{3,2,1,0:T(8,128)} %pad.4.x_ref), custom_call_target="tpu_custom_call" | custom-call | flops 6000000000 | bytes 1048576 | tf_op jit(solution)/shard_map/gains/pallas_call | solution.py:1694
  567.5 1.3 slice_bitcast_fusion
  568.8 4.1 fusion.9
  572.9 0.8 copy.35
  573.7 0.8 copy.36
  574.5 0.8 copy.37
  575.3 0.8 copy.38
  576.1 1.3 copy.39
  577.4 1.0 copy-done.13
  578.4 1.3 copy.40
  579.7 1.0 copy-done.12
  580.8 1.3 copy.41
  (67 shorter events, 0.4 us)
Async XLA Ops:
  0.6 3.3 copy-start.7
  0.7 5.3 copy-start.27
  4.0 3.2 copy-start.23
  7.2 99.9 %copy-start.2 = (s32[1024]{0:T(1024)S(1)}, s32[1024]{0:T(1024)}, u32[]{:S(2)}) copy-start(s32[1024]{0:T(1024)} %param.23) | copy-start | bytes 12292
  107.3 15.3 %copy-start.1 = (s32[1024,1]{1,0:T(8,128)}, s32[1024,1]{1,0:T(8,128)S(1)}, u32[]{:S(2)}) copy-start(s32[1024,1]{1,0:T(8,128)S(1)} %copy.24.seg_col) | copy-start | bytes 12292
  107.3 2.1 copy-start.3
  122.7 18.2 %copy-start.4 = (f32[8,1,1024]{2,1,0:T(1,128)}, f32[8,1,1024]{2,1,0:T(1,128)S(1)}, u32[]{:S(2)}) copy-start(f32[8,1,1024]{2,1,0:T(1,128)S(1)} %get-tuple-element.41.lse_ref) | copy-start | bytes 98308
  122.7 18.2 %slice-start = ((s8[8388608]{0:T(1024)(128)(4,1)}), s8[4194304]{0:T(1024)(128)(4,1)S(1)}, s32[]{:S(2)}) async-start(s8[8388608]{0:T(1024)(128)(4,1)} %bitcast.36), calls=%async_computation | async-start | bytes 8388608
  122.7 18.2 %copy-start.8 = (bf16[256,2048]{1,0:T(8,128)(2,1)S(1)}, bf16[256,2048]{1,0:T(8,128)(2,1)}, u32[]{:S(2)}) copy-start(bf16[256,2048]{1,0:T(8,128)(2,1)} %param.13) | copy-start | bytes 3145732
  122.7 18.2 %slice-start.1 = ((s8[8388608]{0:T(1024)(128)(4,1)}), s8[4194304]{0:T(1024)(128)(4,1)S(1)}, s32[]{:S(2)}) async-start(s8[8388608]{0:T(1024)(128)(4,1)} %bitcast.36), calls=%async_computation.1 | async-start | bytes 8388608
  140.8 2.5 copy-start
  140.9 4.4 copy-start.19
  143.4 1.3 copy-start.5
  144.7 0.6 copy-start.25
  146.5 214.4 %copy-start.20 = (f32[2048]{0:T(1024)S(1)}, f32[2048]{0:T(1024)}, u32[]{:S(2)}) copy-start(f32[2048]{0:T(1024)} %param.19) | copy-start | bytes 24580
  146.5 214.4 %copy-start.26 = (f32[256]{0:T(256)S(1)}, f32[256]{0:T(256)}, u32[]{:S(2)}) copy-start(f32[256]{0:T(256)} %copy-done.25) | copy-start | bytes 3076
  360.9 4.3 copy-start.6
  360.9 4.3 copy-start.10
  440.6 106.1 %copy-start.21 = (f32[2048]{0:T(1024)S(1)}, f32[2048]{0:T(1024)}, u32[]{:S(2)}) copy-start(f32[2048]{0:T(1024)} %param.14) | copy-start | bytes 24580
  440.7 106.1 %copy-start.24 = (f32[256]{0:T(256)S(1)}, f32[256]{0:T(256)}, u32[]{:S(2)}) copy-start(f32[256]{0:T(256)} %copy-done.23) | copy-start | bytes 3076
  546.8 6.4 %copy-start.22 = (f32[2048]{0:T(1024)S(1)}, f32[2048]{0:T(1024)}, u32[]{:S(2)}) copy-start(f32[2048]{0:T(1024)} %get-tuple-element.61) | copy-start | bytes 24580
  554.0 14.8 %copy-start.9 = (bf16[256,2048]{1,0:T(8,128)(2,1)S(1)}, bf16[256,2048]{1,0:T(8,128)(2,1)}, u32[]{:S(2)}) copy-start(bf16[256,2048]{1,0:T(8,128)(2,1)} %param.13) | copy-start | bytes 3145732
  554.0 14.8 %copy-start.11 = (f32[256,2048]{1,0:T(8,128)S(1)}, f32[256,2048]{1,0:T(8,128)}, u32[]{:S(2)}) copy-start(f32[256,2048]{1,0:T(8,128)} %get-tuple-element.66) | copy-start | bytes 6291460
  568.8 4.1 copy-start.18
  568.8 4.9 copy-start.17
  572.9 1.6 copy-start.16
  572.9 2.4 copy-start.15
  572.9 3.2 copy-start.14
  576.1 2.3 copy-start.13
  578.4 2.3 copy-start.12

commit v5 on v4

--- a/solution.py
+++ b/solution.py
@@ -21,6 +21,7 @@
 ZAXIS = "tensor"
 VMEM_MAX = 67_000_000
 CHUNKS = 4
+GRAD_WIDE = 1024
 
 
 def dot_nn(left, right):
@@ -48,6 +49,20 @@
 
 def cost(us):
     return pl.CostEstimate(flops=int(us * 1e9), bytes_accessed=1 << 20, transcendentals=0)
+
+
+def by_rows(total, body, block=32):
+    block = min(block, total)
+
+    def one(i, carry):
+        body(pl.ds(pl.multiple_of(i * block, block), block))
+        return carry
+
+    lax.fori_loop(0, total // block, one, 0)
+
+
+def below(start, rows):
+    return pl.ds(pl.multiple_of(start + rows.start, rows.size), rows.size)
 
 
 def inside(value, size):
@@ -168,8 +183,12 @@
 
                 @pl.when(owner != t)
                 def _():
-                    both = self.recv[at].astype(F32) + self.part[owner].astype(F32)
-                    self.recv[at] = both.astype(BF)
+
+                    def add(rows):
+                        both = self.recv[at, rows].astype(F32) + self.part[owner, rows].astype(F32)
+                        self.recv[at, rows] = both.astype(BF)
+
+                    by_rows(self.part.shape[1], add)
                     self._copy(self.recv.at[at], s, d).start()
 
     def emit(self, out, sem):
@@ -248,9 +267,14 @@
         def _():
             at = self.slot(a, d)
             self._copy(self.piece(self.recv, at, c), a, d, c).wait_recv()
-            rows = slice(c * self.rows, (c + 1) * self.rows)
-            both = self.recv[at, rows].astype(F32) + self.part[self.owner(a, d), rows].astype(F32)
-            self.recv[at, rows] = both.astype(BF)
+            owner = self.owner(a, d)
+
+            def add(rows):
+                rows = below(c * self.rows, rows)
+                both = self.recv[at, rows].astype(F32) + self.part[owner, rows].astype(F32)
+                self.recv[at, rows] = both.astype(BF)
+
+            by_rows(self.rows, add)
             self._copy(self.piece(self.recv, at, c), a, d, c).start()
 
     def groups(self):
@@ -299,7 +323,11 @@
                 pull.start()
             for pull in pulls:
                 pull.wait()
-            self.buf[0] = (self.buf[0].astype(F32) + self.buf[1].astype(F32)).astype(BF)
+
+            def add(rows):
+                self.buf[0, rows] = (self.buf[0, rows].astype(F32) + self.buf[1, rows].astype(F32)).astype(BF)
+
+            by_rows(self.rows, add)
             back = pltpu.make_async_copy(self.buf.at[0], arrived, self.sem.at[0])
             back.start()
             back.wait()
@@ -528,37 +556,84 @@
     return jnp.concatenate([scores[:start], corner], axis=0) if start else corner
 
 
-def attend_kernel(block, q_ref, k_ref, v_ref, seg_row, seg_col, ctx_ref, lse_ref):
-    keys, values = k_ref[...], v_ref[...]
+def attend_kernel(n, qkv_ref, seg_row, seg_col, out_ref, lse_ref, context, own_sem, send_sem, recv_sem):
+    t = lax.axis_index(ZAXIS)
+    width, length = context.shape
+    rows = length // n
+    barrier = pltpu.get_barrier_semaphore()
+    for s in range(1, n):
+        pl.semaphore_signal(barrier, inc=1, device_id={ZAXIS: lax.rem(t + s, n)}, device_id_type=MESH)
+
+    def move(owner, source):
+        return pltpu.make_async_remote_copy(
+            src_ref=context.at[:, pl.ds(owner * rows, rows)],
+            dst_ref=out_ref.at[pl.ds(pl.multiple_of(source * width, width), width), :],
+            send_sem=send_sem.at[owner],
+            recv_sem=recv_sem.at[source],
+            device_id={ZAXIS: owner},
+            device_id_type=MESH,
+        )
+
+    def keep(owner):
+        place = out_ref.at[pl.ds(owner * width, width), :]
+        return pltpu.make_async_copy(context.at[:, pl.ds(owner * rows, rows)], place, own_sem)
+
     column = seg_col[...]
-    for start in range(0, q_ref.shape[1], block):
-        end = start + block
-        scores = masked(dot_tn(keys[:, :end], q_ref[:, start:end]), column[:end], seg_row[:, start:end], start)
-        top = jnp.max(scores, axis=0, keepdims=True)
-        expo = jnp.exp(scores - top)
-        total = jnp.sum(expo, axis=0, keepdims=True)
-        weights = (expo * (1.0 / total)).astype(BF)
-        ctx_ref[:, start:end] = dot_nn(values[:, :end], weights).astype(BF)
-        lse_ref[0, :, start:end] = top + jnp.log(total)
-
-
-def attend(qkv, seg_row, seg_col):
-    heads, length = qkv.shape[0] // (3 * HEAD_DIM), qkv.shape[1]
-    part = lambda o: pl.BlockSpec((HEAD_DIM, length), lambda h: (h + o * heads, 0))
-    whole = lambda *shape: pl.BlockSpec(shape, lambda h: (0,) * len(shape))
+    edges = [0, length // 2, length * 3 // 4, length]
+    for start, end in zip(edges[:-1], edges[1:]):
+
+        def head(h, carry):
+            at = lambda base: pl.ds(pl.multiple_of(base + h * HEAD_DIM, HEAD_DIM), HEAD_DIM)
+            keys, values = qkv_ref[at(width), :end], qkv_ref[at(2 * width), :end]
+            scores = masked(dot_tn(keys, qkv_ref[at(0), start:end]), column[:end], seg_row[:, start:end], start)
+            top = jnp.max(scores, axis=0, keepdims=True)
+            expo = jnp.exp(scores - top)
+            total = jnp.sum(expo, axis=0, keepdims=True)
+            weights = (expo * (1.0 / total)).astype(BF)
+            context[at(0), start:end] = dot_nn(values, weights).astype(BF)
+            lse_ref[h, :, start:end] = top + jnp.log(total)
+            return carry
+
+        lax.fori_loop(0, width // HEAD_DIM, head, 0)
+        if start == 0:
+            pl.semaphore_wait(barrier, n - 1)
+        for owner in range(start // rows, end // rows):
+
+            @pl.when(owner != t)
+            def _():
+                move(owner, t).start()
+
+            @pl.when(owner == t)
+            def _():
+                keep(owner).start()
+
+    for other in range(n):
+
+        @pl.when(other != t)
+        def _():
+            move(other, t).wait_send()
+            move(other, other).wait_recv()
+
+        @pl.when(other == t)
+        def _():
+            keep(other).wait()
+
+
+def attend(n, qkv, seg_row, seg_col):
+    width, length = qkv.shape[0] // 3, qkv.shape[1]
     return pl.pallas_call(
-        functools.partial(attend_kernel, 512),
-        grid=(heads,),
-        in_specs=[part(0), part(1), part(2), whole(1, length), whole(length, 1)],
-        out_specs=[part(0), pl.BlockSpec((1, 1, length), lambda h: (h, 0, 0))],
+        functools.partial(attend_kernel, n),
+        in_specs=[VM] * 3,
+        out_specs=[VM] * 2,
         out_shape=[
-            jax.ShapeDtypeStruct((heads * HEAD_DIM, length), BF),
-            jax.ShapeDtypeStruct((heads, 1, length), F32),
+            jax.ShapeDtypeStruct((n * width, length // n), BF),
+            jax.ShapeDtypeStruct((width // HEAD_DIM, 1, length), F32),
         ],
-        compiler_params=pltpu.CompilerParams(vmem_limit_bytes=48 << 20),
-        cost_estimate=cost(13),
+        scratch_shapes=[pltpu.VMEM((width, length), BF), DMA, DMA((n,)), DMA((n,))],
+        compiler_params=pltpu.CompilerParams(collective_id=1, has_side_effects=True, vmem_limit_bytes=48 << 20),
+        cost_estimate=cost(25),
         name="attend",
-    )(qkv, qkv, qkv, seg_row, seg_col)
+    )(qkv, seg_row, seg_col)
 
 
 def turn_back(values, cosine, sine):
@@ -594,50 +669,6 @@
         dk_sum[:, here] = dk[:, start:]
     dk_ref[rows, :] = turn_back(dk_sum[...], cos_ref[...], sin_ref[...]).astype(BF)
     dv_ref[rows, :] = dv_sum[...].astype(BF)
-
-
-def swap_kernel(n, x_ref, o_ref, own_sem, send_sem, recv_sem):
-    t = lax.axis_index(ZAXIS)
-    rows, cols = x_ref.shape[0], x_ref.shape[1] // n
-    source = lambda i: x_ref.at[:, pl.ds(pl.multiple_of(i * cols, cols), cols)]
-    target = o_ref.at[pl.ds(pl.multiple_of(t * rows, rows), rows), :]
-    barrier = pltpu.get_barrier_semaphore()
-    for s in range(1, n):
-        pl.semaphore_signal(barrier, inc=1, device_id={ZAXIS: lax.rem(t + s, n)}, device_id_type=MESH)
-    pl.semaphore_wait(barrier, n - 1)
-    copies = []
-    for s in range(1, n):
-        peer = lax.rem(t + s, n)
-        copies.append(
-            pltpu.make_async_remote_copy(
-                src_ref=source(peer),
-                dst_ref=target,
-                send_sem=send_sem.at[s - 1],
-                recv_sem=recv_sem.at[s - 1],
-                device_id={ZAXIS: peer},
-                device_id_type=MESH,
-            )
-        )
-        copies[-1].start()
-    own = pltpu.make_async_copy(source(t), target, own_sem)
-    own.start()
-    for copy in copies:
-        copy.wait()
-    own.wait()
-
-
-def swap(n, x):
-    rows, cols = x.shape
-    return pl.pallas_call(
-        functools.partial(swap_kernel, n),
-        out_shape=jax.ShapeDtypeStruct((rows * n, cols // n), x.dtype),
-        in_specs=[VM],
-        out_specs=VM,
-        scratch_shapes=[DMA, DMA((n - 1,)), DMA((n - 1,))],
-        compiler_params=pltpu.CompilerParams(collective_id=1, has_side_effects=True, vmem_limit_bytes=32 << 20),
-        cost_estimate=cost(25),
-        name="swap_out",
-    )(x)
 
 
 def mlp_kernel(
@@ -865,7 +896,8 @@
     sides = ((n2, ((0, dgate), (1, dup))), (cot, ((2, hid),)))
 
     def weight_grad(left, rights, mine):
-        steps = units // wide
+        broad = min(GRAD_WIDE, units)
+        steps = units // broad
         tall = n * rows // steps
 
         def turn(place, q, j):
@@ -892,7 +924,7 @@
                     cross(which, store, k).wait_recv()
 
                 def inner(j, c):
-                    cols = pl.ds(pl.multiple_of(j * wide, wide), wide)
+                    cols = pl.ds(pl.multiple_of(j * broad, broad), broad)
                     value = dot_nn(turned[now], right[:, cols])
                     if mine:
                         value = value + store[at, cols].astype(F32)
@@ -1060,11 +1092,15 @@
         for side, kept, at, copy in self.copies(i):
             copy.wait_recv()
             mine = self.block(side, kept)
-            both = mine[...].astype(F32) + self.inbox[side, at].astype(F32)
-            if i == self.stages - 1:
-                last(side, both)
+            sent = self.inbox.at[side, at]
+            if i < self.stages - 1 or last is None:
+
+                def add(rows):
+                    mine[rows] = (mine[rows].astype(F32) + sent[rows].astype(F32)).astype(BF)
+
+                by_rows(mine.shape[0], add)
             else:
-                mine[...] = both.astype(BF)
+                last(side, mine, sent)
 
     def finish(self):
         for i in range(self.begin, self.stages):
@@ -1188,15 +1224,19 @@
             device_id_type=MESH,
         )
 
-    for s in range(1, n + 1):
+    def project(s, carry):
         load_wo(s).wait()
         z = lax.rem(t + s, n)
-        block = dot_nt(wo[wo_rows(z), :], branch_ref[...]).astype(BF)
-        if s < n:
-            outgoing[z] = block
-            z_copy(s).start()
-        else:
-            grads[:, token_cols(t)] = block
+        outgoing[z] = dot_nt(wo[wo_rows(z), :], branch_ref[...]).astype(BF)
+
+        @pl.when(s < n)
+        def _():
+            z_copy(jnp.minimum(s, n - 1)).start()
+
+        return carry
+
+    lax.fori_loop(1, n + 1, project, 0)
+    grads[:, token_cols(t)] = outgoing[t]
 
     load_part.wait()
     for d, end in ((0, 0), (1, n - 1)):
@@ -1222,11 +1262,14 @@
             slot = pairs + k if mine else k
             if mine:
                 cross(k).wait_recv()
-            for low in range(0, depth, 512):
-                value = dot_nt(turned[...], ctx_ref[low : low + 512, :])
+
+            def columns(cols):
+                value = dot_nt(turned[...], ctx_ref[cols, :])
                 if mine:
-                    value = value + strips[slot, :, low : low + 512].astype(F32)
-                strips[slot, :, low : low + 512] = value.astype(BF)
+                    value = value + strips[slot, :, cols].astype(F32)
+                strips[slot, :, cols] = value.astype(BF)
+
+            by_rows(depth, columns, 512)
             if not mine:
                 cross(k).start()
             return carry
@@ -1253,8 +1296,12 @@
 
     for side in range(2):
         for j in range(m // 4):
-            both = kept[side, j].astype(F32) + got[side, j].astype(F32)
-            kept[side, j] = both.astype(BF)
+            mine, sent = kept.at[side, j], got.at[side, j]
+
+            def add(rows, mine=mine, sent=sent):
+                mine[rows] = (mine[rows].astype(F32) + sent[rows].astype(F32)).astype(BF)
+
+            by_rows(half, add)
             put_gate(side, j).start()
     for s in range(1, n):
         z_arrive(s).wait_recv()
@@ -1263,14 +1310,20 @@
         attend_back_head(
             256, h, qkv_ref, grads, lse_ref, seg_row, seg_col, cos_ref, sin_ref, (dq_ref, dk_ref, dv_ref), dk_sum, dv_sum
         )
+        for i, group in enumerate(groups[:-1]):
+
+            @pl.when(h == max((i + 1) * heads // (len(groups) - 1) - 1, 0))
+            def _():
+                for relay in group:
+                    far.relay(*relay)
+
         return carry
 
     heads = width // HEAD_DIM
     groups = list(far.groups())
-    for i, group in enumerate(groups):
-        lax.fori_loop(heads * i // (len(groups) - 1), min(heads * (i + 1) // (len(groups) - 1), heads), head, 0)
-        for relay in group:
-            far.relay(*relay)
+    lax.fori_loop(0, heads, head, 0)
+    for relay in groups[-1]:
+        far.relay(*relay)
     up_chips.take(0, None)
     for side, k, j, _ in up_chips.copies(0):
         put_up(side, k, j).start()
@@ -1506,12 +1559,21 @@
     ring.step(1)
 
     def hand_matrix(which):
-        def hand(side, both):
-            at = slice(side * half, (side + 1) * half)
-            if which == 2:
-                down_ref[:, at] = both.T
-            else:
-                (gate_ref, up_ref)[which][at, :] = both
+        def hand(side, mine, sent):
+            if which < 2:
+                ref = (gate_ref, up_ref)[which]
+
+                def add(rows):
+                    ref[below(side * half, rows), :] = mine[rows].astype(F32) + sent[rows].astype(F32)
+
+                by_rows(half, add)
+                return
+
+            def turn(cols):
+                both = mine[:, cols].astype(F32) + sent[:, cols].astype(F32)
+                down_ref[cols, side * half : (side + 1) * half] = both.T
+
+            by_rows(down_ref.shape[0], turn, 256)
 
         return hand
 
@@ -1520,13 +1582,21 @@
         if i + 1 < matrices[which].stages:
             matrices[which].start(i + 1)
 
-    def hand_out(side, both):
-        for z in range(n):
-            out_part[z, side * half : (side + 1) * half, :] = both[:, z * width : (z + 1) * width].astype(BF)
-
-    def hand_qkv(side, both):
-        for i, ref in enumerate((qs_ref, ks_ref, vs_ref)):
-            ref[side * half : (side + 1) * half, :] = both[:, i * width : (i + 1) * width]
+    def hand_out(side, mine, sent):
+        def add(rows):
+            both = mine[rows].astype(F32) + sent[rows].astype(F32)
+            for z in range(n):
+                out_part[z, below(side * half, rows), :] = both[:, z * width : (z + 1) * width].astype(BF)
+
+        by_rows(half, add)
+
+    def hand_qkv(side, mine, sent):
+        def add(rows):
+            both = mine[rows].astype(F32) + sent[rows].astype(F32)
+            for i, ref in enumerate((qs_ref, ks_ref, vs_ref)):
+                ref[below(side * half, rows), :] = both[:, i * width : (i + 1) * width]
+
+        by_rows(half, add)
 
     for i in range(1, out_chips.stages):
         out_chips.take(i, hand_out)
@@ -1750,8 +1820,7 @@
         m, n, normed_one, query_weight, key_weight, value_weight, cosine, sine, strip
     )
     out_full = out_full.reshape(n * m * piece, depth)
-    context, lse = attend(qkv, seg_row, seg_col)
-    context_all = swap(n, context)
+    context_all, lse = attend(n, qkv, seg_row, seg_col)
     mid = resid + dot_tn(context_all, out_full)
     scaled_two, inverse_two = norm_stats(mid)
     normed_two = (scaled_two * mlp_gain).astype(BF)

time: 591 us -> 575 us (0.973); the launches traced: 583 us -> 574 us
  Pallas kernels: 536 us -> 529 us
    pallas_call x2 -> x1, Pallas kernels: 31.3 us -> 22.5 us  [attend(): pl.pallas_call(functools.partial(attend_kernel, n), in_specs=[VM] * 3, ou...]
    unnamed x67 -> x65, local copies, waits for them, and re-layouts: 13.2 us -> 13.2 us
where the time goes in v5:
time: 575 us; the launch traced here: 574 us
  Pallas kernels  529 us (92%)
  other arithmetic  24.7 us (4%)
  local copies, waits for them, and re-layouts  17.3 us (3%)
    pallas_call x1, Pallas kernels, mlp(): pl.pallas_call(functools.partial(mlp_kernel, m, n), out_shape=[jax.ShapeD...  214 us
    pallas_call x1, Pallas kernels, input_back(): pl.pallas_call(functools.partial(input_kernel, m, n), out_shape=[jax.Shap...  107 us
    pallas_call x1, Pallas kernels, gather_qkv(): pl.pallas_call(functools.partial(qkv_kernel, m, n), out_shape=[jax.ShapeD...  99.9 us
    pallas_call x1, Pallas kernels, back(): pl.pallas_call(functools.partial(back_kernel, m, n), out_shape=[jax.Shape...  72.7 us
    pallas_call x1, Pallas kernels, attend(): pl.pallas_call(functools.partial(attend_kernel, n), in_specs=[VM] * 3, ou...  22.5 us
    unnamed x65, local copies, waits for them, and re-layouts  13.2 us
    pallas_call x1, Pallas kernels, reduce_gains(): pl.pallas_call(functools.partial(gains_kernel, m, n), out_shape=jax.Shape...  12.7 us

profile of v5, /device:TPU:0, one launch (start us, length us, event | category | flops | bytes accessed | tf_op | source)
XLA Modules:
  0.0 574.1 jit_solution(15912545700729402180)
XLA Ops:
  0.7 1.8 constant_dynamic-slice_fusion.strip_ref
  2.4 1.5 fusion.11
  4.0 2.0 fusion.4.n1_ref
  6.0 1.2 multiply_sine_fusion
  7.2 99.9 %gather_qkv.1 = (bf16[1024,2048]{1,0:T(8,128)(2,1)}, bf16[1536,1024]{1,0:T(8,128)(2,1)}, bf16[4,8,64,2048]{3,2,1,0:T(8,128)(2,1)}) custom-call(bf16[256,2048]{1,0:T(8,128)(2,1)} %fusion.4.n1_ref, bf16[2048,512]{1,0:T(8,128)(2,1)} %wq.3, bf16[2048,512]{1,0:T(8,128)(2,1)} %wk.3, bf16[2048,512]{1,0:T(8,128)(2,1)} %wv.3, f32[32,1024]{1,0:T(8,128)} %get-tuple-element.68.cos_ref, ...), custom_call_target="tpu_custom_call" | custom-call | flops 89999998976 | bytes 1048576 | tf_op jit(solution)/shard_map/gather_qkv/pallas_call | solution.py:524
  107.1 0.2 copy.24.seg_col
  107.4 2.1 copy-done.3
  109.4 22.5 %attend.1 = (bf16[2048,256]{1,0:T(8,128)(2,1)S(1)}, f32[8,1,1024]{2,1,0:T(1,128)S(1)}) custom-call(bf16[1536,1024]{1,0:T(8,128)(2,1)S(1)} %copy-done.3, s32[1,1024]{1,0:T(1,128)S(1)} %bitcast.34, s32[1024,1]{1,0:T(8,128)S(1)} %copy.24.seg_col), custom_call_target="tpu_custom_call" | custom-call | flops 24999999488 | bytes 1048576 | tf_op jit(solution)/shard_map/attend/pallas_call | solution.py:624
  132.0 2.4 multiply_reduce_fusion.1
  134.5 1.3 copy-done.5
  135.8 0.6 copy-done.26
  136.4 1.2 multiply_convert_fusion.n2_ref
  137.6 213.6 %mlp.1 = (bf16[4,256,2048]{2,1,0:T(8,128)(2,1)}, bf16[3,256,2048]{2,1,0:T(8,128)(2,1)}, bf16[2,2,128,2048]{3,2,1,0:T(8,128)(2,1)}, bf16[2,2,128,2048]{3,2,1,0:T(...) custom-call(bf16[256,2048]{1,0:T(8,128)(2,1)} %multiply_convert_fusion.n2_ref, ...), custom_call_target="tpu_custom_call" | custom-call | flops 154999996416 | bytes 1048576 | tf_op jit(solution)/shard_map/mlp/pallas_call | solution.py:1000
  351.3 4.2 fusion.13
  355.6 4.2 fusion.14
  359.7 72.7 %back.1 = (bf16[512,1024]{1,0:T(8,128)(2,1)}, bf16[512,1024]{1,0:T(8,128)(2,1)}, bf16[512,1024]{1,0:T(8,128)(2,1)}, bf16[2,2,128,2048]{3,2,1,0:T(8,128)(2,1)}, b...) custom-call(bf16[256,2048]{1,0:T(8,128)(2,1)} %get-tuple-element.65.branch_ref, ...), custom_call_target="tpu_custom_call" | custom-call | flops 54999998464 | bytes 1048576 | tf_op jit(solution)/shard_map/back/pallas_call | solution.py:1364
  432.4 107.1 %input_back.1 = (bf16[3,256,2048]{2,1,0:T(8,128)(2,1)}, f32[256,512]{1,0:T(8,128)}, f32[256,512]{1,0:T(8,128)}, f32[256,512]{1,0:T(8,128)}, f32[512,256]{1,0:T(8...) custom-call(bf16[512,1024]{1,0:T(8,128)(2,1)} %get-tuple-element.47.dq_ref, ...), custom_call_target="tpu_custom_call" | custom-call | flops 95000002560 | bytes 1048576 | tf_op jit(solution)/shard_map/input_back/pallas_call | solution.py:1658
  539.6 6.3 %fusion.10 = (f32[2048]{0:T(1024)S(1)}, f32[256]{0:T(256)S(1)}, bf16[256,2048]{1,0:T(8,128)(2,1)}) fusion(bf16[256,2048]{1,0:T(8,128)(2,1)} %param.13, f32[256]{0:T(256)S(1)} %copy-done.25, bf16[3,256,2048]{2,1,0:T(8,128)(2,1)} %get-tuple-element.53, pred[]{:T(512)S(6)} %lt.19, pred[]{:T(512)S(6)} %gt.2, f32[2048]{0:T(1024)S(1)} %copy-done.22, ...), kind=kLoop, calls=%fused_computation.13 | loop fusion | flops 13104896 | bytes 12601360 | tf_op jit(solution)/shard_map/reduce_sum | solution.py:47
  545.9 0.1 stack.10
  546.1 0.7 pad.4.x_ref
  546.8 12.7 %gains.1 = f32[8,128]{1,0:T(8,128)} custom-call(f32[4,8,8,128]{3,2,1,0:T(8,128)} %pad.4.x_ref), custom_call_target="tpu_custom_call" | custom-call | flops 6000000000 | bytes 1048576 | tf_op jit(solution)/shard_map/gains/pallas_call | solution.py:1764
  559.5 1.3 slice_bitcast_fusion
  560.8 4.1 fusion.9
  564.9 0.8 copy.35
  565.6 0.8 copy.36
  566.4 0.8 copy.37
  567.2 0.8 copy.38
  568.0 1.3 copy.39
  569.4 1.0 copy-done.14
  570.4 1.3 copy.40
  571.7 1.0 copy-done.13
  572.7 1.3 copy.41
  (63 shorter events, 0.3 us)
Async XLA Ops:
  0.6 3.3 copy-start.7
  0.7 5.3 copy-start.28
  4.0 3.2 copy-start.24
  7.2 99.9 %copy-start.2 = (s32[1024]{0:T(1024)S(1)}, s32[1024]{0:T(1024)}, u32[]{:S(2)}) copy-start(s32[1024]{0:T(1024)} %param.23) | copy-start | bytes 12292
  107.3 24.6 %copy-start.1 = (s32[1024,1]{1,0:T(8,128)}, s32[1024,1]{1,0:T(8,128)S(1)}, u32[]{:S(2)}) copy-start(s32[1024,1]{1,0:T(8,128)S(1)} %copy.24.seg_col) | copy-start | bytes 12292
  107.4 2.1 copy-start.3
  109.4 22.6 %copy-start.8 = (bf16[256,2048]{1,0:T(8,128)(2,1)S(1)}, bf16[256,2048]{1,0:T(8,128)(2,1)}, u32[]{:S(2)}) copy-start(bf16[256,2048]{1,0:T(8,128)(2,1)} %param.13) | copy-start | bytes 3145732
  109.4 22.6 %copy-start.10 = (bf16[4,8,64,2048]{3,2,1,0:T(8,128)(2,1)S(1)}, bf16[4,8,64,2048]{3,2,1,0:T(8,128)(2,1)}, u32[]{:S(2)}) copy-start(bf16[4,8,64,2048]{3,2,1,0:T(8,128)(2,1)} %get-tuple-element.38) | copy-start | bytes 25165828
  132.0 2.5 copy-start
  132.0 2.5 copy-start.4
  132.0 4.4 copy-start.20
  134.5 1.3 copy-start.5
  135.8 0.6 copy-start.26
  137.6 213.7 %copy-start.21 = (f32[2048]{0:T(1024)S(1)}, f32[2048]{0:T(1024)}, u32[]{:S(2)}) copy-start(f32[2048]{0:T(1024)} %param.19) | copy-start | bytes 24580
  137.6 213.7 %copy-start.27 = (f32[256]{0:T(256)S(1)}, f32[256]{0:T(256)}, u32[]{:S(2)}) copy-start(f32[256]{0:T(256)} %copy-done.26) | copy-start | bytes 3076
  351.3 4.3 copy-start.6
  351.3 4.3 copy-start.11
  432.4 107.1 %copy-start.22 = (f32[2048]{0:T(1024)S(1)}, f32[2048]{0:T(1024)}, u32[]{:S(2)}) copy-start(f32[2048]{0:T(1024)} %param.14) | copy-start | bytes 24580
  432.4 107.1 %copy-start.25 = (f32[256]{0:T(256)S(1)}, f32[256]{0:T(256)}, u32[]{:S(2)}) copy-start(f32[256]{0:T(256)} %copy-done.24) | copy-start | bytes 3076
  539.6 6.4 %copy-start.23 = (f32[2048]{0:T(1024)S(1)}, f32[2048]{0:T(1024)}, u32[]{:S(2)}) copy-start(f32[2048]{0:T(1024)} %get-tuple-element.61) | copy-start | bytes 24580
  546.8 14.0 %copy-start.9 = (bf16[256,2048]{1,0:T(8,128)(2,1)S(1)}, bf16[256,2048]{1,0:T(8,128)(2,1)}, u32[]{:S(2)}) copy-start(bf16[256,2048]{1,0:T(8,128)(2,1)} %param.13) | copy-start | bytes 3145732
  546.8 14.0 %copy-start.12 = (f32[256,2048]{1,0:T(8,128)S(1)}, f32[256,2048]{1,0:T(8,128)}, u32[]{:S(2)}) copy-start(f32[256,2048]{1,0:T(8,128)} %get-tuple-element.66) | copy-start | bytes 6291460
  560.8 4.1 copy-start.19
  560.8 4.9 copy-start.18
  564.8 1.6 copy-start.17
  564.8 2.4 copy-start.16
  564.8 3.2 copy-start.15
  568.0 2.3 copy-start.14
  570.4 2.3 copy-start.13

commit v6 on v5

--- a/solution.py
+++ b/solution.py
@@ -21,7 +21,7 @@
 ZAXIS = "tensor"
 VMEM_MAX = 67_000_000
 CHUNKS = 4
-GRAD_WIDE = 1024
+GRAD_WIDE = 2048
 
 
 def dot_nn(left, right):
@@ -39,12 +39,6 @@
 def norm_stats(values):
     inverse = lax.rsqrt(jnp.mean(values * values, axis=-1, keepdims=True) + EPS)
     return (values * inverse, inverse)
-
-
-def norm_back(grad_normed, scaled, inverse, gain):
-    upstream = grad_normed * gain
-    grad_in = inverse * (upstream - scaled * jnp.mean(upstream * scaled, axis=-1, keepdims=True))
-    return (grad_in, jnp.sum(grad_normed * scaled, axis=0))
 
 
 def cost(us):
@@ -1703,6 +1697,50 @@
     )(dq, dk, dv, wq, wk, wv, full, out_halves, mlp_halves, sums)
 
 
+def norm_kernel(n, parts_ref, value_ref, gain_ref, base_ref, *outs):
+    share_ref, low_ref = outs[0], outs[1]
+    t = lax.axis_index(ZAXIS)
+
+    @pl.when(pl.program_id(0) == 0)
+    def _():
+        share_ref[...] = jnp.zeros_like(share_ref)
+
+    def one(rows):
+        own, left, right = (parts_ref[i, rows].astype(F32) for i in range(3))
+        grad = own + jnp.where(t > 0, left, 0.0) + jnp.where(t < n - 1, right, 0.0)
+        values = value_ref[rows].astype(F32)
+        scaled, inverse = norm_stats(values)
+        upstream = grad * gain_ref[...]
+        inner = jnp.mean(upstream * scaled, axis=-1, keepdims=True)
+        total = base_ref[rows].astype(F32) + inverse * (upstream - scaled * inner)
+        low_ref[rows] = total.astype(BF)
+        for ref in outs[2:]:
+            ref[rows] = total
+        share_ref[...] += jnp.sum(grad * scaled, axis=0, keepdims=True)
+
+    by_rows(value_ref.shape[0], one, 64)
+
+
+def norm_backward(n, parts, values, gain, base, wide):
+    rows, depth = values.shape
+    block = rows // 4
+    tokens = pl.BlockSpec((block, depth), lambda i: (i, 0))
+    row = pl.BlockSpec((1, depth), lambda i: (0, 0))
+    shapes = [jax.ShapeDtypeStruct((1, depth), F32), jax.ShapeDtypeStruct((rows, depth), BF)]
+    if wide:
+        shapes.append(jax.ShapeDtypeStruct((rows, depth), F32))
+    share, *totals = pl.pallas_call(
+        functools.partial(norm_kernel, n),
+        grid=(rows // block,),
+        in_specs=[pl.BlockSpec((3, block, depth), lambda i: (0, i, 0)), tokens, row, tokens],
+        out_specs=[row] + [tokens] * (len(shapes) - 1),
+        out_shape=shapes,
+        cost_estimate=cost(4),
+        name="norm_backward",
+    )(parts, values, gain[None, :], base)
+    return share[0], totals
+
+
 def gains_kernel(m, n, x_ref, o_ref, z_in, total, dp_in, z_send, z_recv, dp_send, dp_recv):
     t = lax.axis_index(ZAXIS)
     index = lax.axis_index("dp")
@@ -1830,10 +1868,8 @@
     )
     t = lax.axis_index(ZAXIS)
     pick = lambda parts, i: lax.dynamic_index_in_dim(parts, i, 0, keepdims=False)
-    grad_normed_two = line_total(grad_two_parts, n)
-    grad_mid_norm, gain_two_part = norm_back(grad_normed_two, scaled_two, inverse_two, mlp_gain)
-    grad_mid = out_cotangent.astype(F32) + grad_mid_norm
-    branch = grad_mid.astype(BF)
+    gain_two_part, (branch, grad_mid) = norm_backward(n, grad_two_parts, mid, mlp_gain, out_cotangent, True)
+
     dq, dk, dv, out_halves, mlp_halves, out_far = back(
         m,
         n,
@@ -1857,9 +1893,7 @@
     grad_one_parts, query_sum, key_sum, value_sum, output_sum, gate_sum, up_sum, down_sum = input_back(
         m, n, dq, dk, dv, query_weight, key_weight, value_weight, full_one, out_halves, mlp_halves, mlp_sums
     )
-    grad_normed_one = line_total(grad_one_parts, n)
-    grad_in_norm, gain_one_part = norm_back(grad_normed_one, scaled_one, inverse_one, attn_gain)
-    input_grad = (grad_mid + grad_in_norm).astype(BF)
+    gain_one_part, (input_grad,) = norm_backward(n, grad_one_parts, hidden_in, attn_gain, grad_mid, False)
     gain_one_sum, gain_two_sum = reduce_gains(m, n, gain_one_part, gain_two_part)
     return (
         block_out,

time: 575 us -> 569 us (0.990)
  other arithmetic: 24.7 us -> 12.1 us
  Pallas kernels: 529 us -> 537 us
    pallas_call x0 -> x2, Pallas kernels: none -> 10.9 us  [norm_backward(): pl.pallas_call(functools.partial(norm_kernel, n), grid=(rows // block,),...]
    reduce_sum x2 -> x0, other arithmetic: 10.5 us -> none  [norm_back(): return (grad_in, jnp.sum(grad_normed * scaled, axis=0))]
    unnamed x65 -> x45, local copies, waits for them, and re-layouts: 13.2 us -> 12.6 us
where the time goes in v6:
time: 569 us
  Pallas kernels  537 us (94%)
  local copies, waits for them, and re-layouts  16.7 us (3%)
  other arithmetic  12.1 us (2%)
    pallas_call x1, Pallas kernels, mlp(): pl.pallas_call(functools.partial(mlp_kernel, m, n), out_shape=[jax.ShapeD...  212 us
    pallas_call x1, Pallas kernels, input_back(): pl.pallas_call(functools.partial(input_kernel, m, n), out_shape=[jax.Shap...  107 us
    pallas_call x1, Pallas kernels, gather_qkv(): pl.pallas_call(functools.partial(qkv_kernel, m, n), out_shape=[jax.ShapeD...  99.9 us
    pallas_call x1, Pallas kernels, back(): pl.pallas_call(functools.partial(back_kernel, m, n), out_shape=[jax.Shape...  70.9 us
    pallas_call x1, Pallas kernels, attend(): pl.pallas_call(functools.partial(attend_kernel, n), in_specs=[VM] * 3, ou...  22.5 us
    pallas_call x1, Pallas kernels, reduce_gains(): pl.pallas_call(functools.partial(gains_kernel, m, n), out_shape=jax.Shape...  13.1 us
    unnamed x45, local copies, waits for them, and re-layouts  12.6 us

profile of v6, /device:TPU:0, one launch (start us, length us, event | category | flops | bytes accessed | tf_op | source)
XLA Modules:
  0.0 568.9 jit_solution(6196801765424181216)
XLA Ops:
  0.7 1.8 constant_dynamic-slice_fusion.strip_ref
  2.4 0.7 convert_element_type.31
  3.1 1.2 multiply_sine_fusion
  4.4 1.5 fusion
  5.9 2.0 fusion.2.n1_ref
  7.9 99.9 %gather_qkv.1 = (bf16[1024,2048]{1,0:T(8,128)(2,1)}, bf16[1536,1024]{1,0:T(8,128)(2,1)}, bf16[4,8,64,2048]{3,2,1,0:T(8,128)(2,1)}) custom-call(bf16[256,2048]{1,0:T(8,128)(2,1)} %fusion.2.n1_ref, bf16[2048,512]{1,0:T(8,128)(2,1)} %wq.3, bf16[2048,512]{1,0:T(8,128)(2,1)} %wk.3, bf16[2048,512]{1,0:T(8,128)(2,1)} %wv.3, f32[32,1024]{1,0:T(8,128)} %get-tuple-element.72.cos_ref, ...), custom_call_target="tpu_custom_call" | custom-call | flops 89999998976 | bytes 1048576 | tf_op jit(solution)/shard_map/gather_qkv/pallas_call | solution.py:518
  107.8 0.2 copy.24.seg_col
  108.0 2.1 copy-done.3
  110.1 22.5 %attend.1 = (bf16[2048,256]{1,0:T(8,128)(2,1)S(1)}, f32[8,1,1024]{2,1,0:T(1,128)S(1)}) custom-call(bf16[1536,1024]{1,0:T(8,128)(2,1)S(1)} %copy-done.3, s32[1,1024]{1,0:T(1,128)S(1)} %bitcast.20, s32[1024,1]{1,0:T(8,128)S(1)} %copy.24.seg_col), custom_call_target="tpu_custom_call" | custom-call | flops 24999999488 | bytes 1048576 | tf_op jit(solution)/shard_map/attend/pallas_call | solution.py:618
  132.7 2.5 multiply_reduce_fusion
  135.2 1.3 copy-done.5
  136.5 1.2 multiply_convert_fusion.n2_ref
  137.7 212.1 %mlp.1 = (bf16[4,256,2048]{2,1,0:T(8,128)(2,1)}, bf16[3,256,2048]{2,1,0:T(8,128)(2,1)}, bf16[2,2,128,2048]{3,2,1,0:T(8,128)(2,1)}, bf16[2,2,128,2048]{3,2,1,0:T(...) custom-call(bf16[256,2048]{1,0:T(8,128)(2,1)} %multiply_convert_fusion.n2_ref, ...), custom_call_target="tpu_custom_call" | custom-call | flops 154999996416 | bytes 1048576 | tf_op jit(solution)/shard_map/mlp/pallas_call | solution.py:994
  349.8 5.7 norm_backward.2
  355.5 70.9 %back.1 = (bf16[512,1024]{1,0:T(8,128)(2,1)}, bf16[512,1024]{1,0:T(8,128)(2,1)}, bf16[512,1024]{1,0:T(8,128)(2,1)}, bf16[2,2,128,2048]{3,2,1,0:T(8,128)(2,1)}, b...) custom-call(bf16[256,2048]{1,0:T(8,128)(2,1)} %get-tuple-element.46.branch_ref, ...), custom_call_target="tpu_custom_call" | custom-call | flops 54999998464 | bytes 1048576 | tf_op jit(solution)/shard_map/back/pallas_call | solution.py:1358
  426.4 107.4 %input_back.1 = (bf16[3,256,2048]{2,1,0:T(8,128)(2,1)}, f32[256,512]{1,0:T(8,128)}, f32[256,512]{1,0:T(8,128)}, f32[256,512]{1,0:T(8,128)}, f32[512,256]{1,0:T(8...) custom-call(bf16[512,1024]{1,0:T(8,128)(2,1)} %get-tuple-element.53.dq_ref, ...), custom_call_target="tpu_custom_call" | custom-call | flops 95000002560 | bytes 1048576 | tf_op jit(solution)/shard_map/input_back/pallas_call | solution.py:1652
  533.7 5.2 norm_backward.3
  538.9 0.7 pad_maximum_fusion
  539.7 0.1 reshape.68
  539.8 0.7 pad.4.x_ref
  540.5 13.1 %gains.1 = f32[8,128]{1,0:T(8,128)} custom-call(f32[4,8,8,128]{3,2,1,0:T(8,128)} %pad.4.x_ref), custom_call_target="tpu_custom_call" | custom-call | flops 6000000000 | bytes 1048576 | tf_op jit(solution)/shard_map/gains/pallas_call | solution.py:1802
  553.6 1.3 slice_bitcast_fusion
  554.9 4.8 fusion.3
  559.6 0.8 copy.36
  560.4 0.8 copy.37
  561.2 0.8 copy.38
  562.0 0.8 copy.39
  562.8 1.3 copy.40
  564.2 1.0 copy-done.11
  565.2 1.3 copy.41
  566.5 1.0 copy-done.10
  567.5 1.3 copy.42
  (38 shorter events, 0.1 us)
Async XLA Ops:
  0.6 5.2 copy-start.8
  7.9 99.9 %copy-start.2 = (s32[1024]{0:T(1024)S(1)}, s32[1024]{0:T(1024)}, u32[]{:S(2)}) copy-start(s32[1024]{0:T(1024)} %param.23) | copy-start | bytes 12292
  108.0 24.6 %copy-start.1 = (s32[1024,1]{1,0:T(8,128)}, s32[1024,1]{1,0:T(8,128)S(1)}, u32[]{:S(2)}) copy-start(s32[1024,1]{1,0:T(8,128)S(1)} %copy.24.seg_col) | copy-start | bytes 12292
  108.0 2.1 copy-start.3
  110.1 22.6 %copy-start.7 = (bf16[4,8,64,2048]{3,2,1,0:T(8,128)(2,1)S(1)}, bf16[4,8,64,2048]{3,2,1,0:T(8,128)(2,1)}, u32[]{:S(2)}) copy-start(bf16[4,8,64,2048]{3,2,1,0:T(8,128)(2,1)} %get-tuple-element.43) | copy-start | bytes 25165828
  110.1 22.6 %copy-start.9 = (bf16[256,2048]{1,0:T(8,128)(2,1)S(1)}, bf16[256,2048]{1,0:T(8,128)(2,1)}, u32[]{:S(2)}) copy-start(bf16[256,2048]{1,0:T(8,128)(2,1)} %value_ref.1) | copy-start | bytes 3145732
  132.6 2.5 copy-start
  132.7 2.5 copy-start.4
  132.7 3.8 copy-start.17
  135.2 1.3 copy-start.5
  533.7 5.2 copy-start.18
  540.5 14.4 %copy-start.6 = (f32[256,2048]{1,0:T(8,128)S(1)}, f32[256,2048]{1,0:T(8,128)}, u32[]{:S(2)}) copy-start(f32[256,2048]{1,0:T(8,128)} %copy-done.5) | copy-start | bytes 6291460
  554.9 4.8 copy-start.16
  554.9 5.6 copy-start.15
  554.9 6.4 %copy-start.14 = (f32[256,512]{1,0:T(8,128)S(1)}, f32[256,512]{1,0:T(8,128)}, u32[]{:S(2)}) copy-start(f32[256,512]{1,0:T(8,128)} %get-tuple-element.93) | copy-start | bytes 1572868
  559.6 2.4 copy-start.13
  559.6 3.2 copy-start.12
  562.8 2.3 copy-start.11
  565.2 2.3 copy-start.10
